TPU v7x, 8 devices: a whole 2x2x1 slice. The times are simulated.
8 devices in a mesh: dp: 1 (over z), pp: 8 (over y, x, core).
Axes of the slice: x: 2, y: 2, z: 1, core: 2. Of those that a mesh axis runs over, the one named last changes fastest.
Arguments:
- acts_in: bfloat16 [8, 2, 512, 1536], P(None, 'dp')
- cotangent: bfloat16 [8, 2, 512, 1536], P(None, 'dp')
- ln1_gain: bfloat16 [8, 1536], P('pp')
- ln1_shift: bfloat16 [8, 1536], P('pp')
- w_qkv: bfloat16 [8, 1536, 4608], P('pp')
- b_qkv: bfloat16 [8, 4608], P('pp')
- w_proj: bfloat16 [8, 16, 96, 1536], P('pp')
- b_proj: bfloat16 [8, 1536], P('pp')
- ln2_gain: bfloat16 [8, 1536], P('pp')
- ln2_shift: bfloat16 [8, 1536], P('pp')
- w_up: bfloat16 [8, 1536, 6144], P('pp')
- b_up: bfloat16 [8, 6144], P('pp')
- w_down: bfloat16 [8, 6144, 1536], P('pp')
- b_down: bfloat16 [8, 1536], P('pp')
Outputs:
- output 1: bfloat16 [8, 2, 512, 1536], P(None, 'dp')
- output 2: bfloat16 [8, 2, 512, 1536], P(None, 'dp')
- output 3: float32 [8, 1536], P(('dp', 'pp'))
- output 4: float32 [8, 1536], P(('dp', 'pp'))
- output 5: float32 [8, 1536, 4608], P(('dp', 'pp'))
- output 6: float32 [8, 4608], P(('dp', 'pp'))
- output 7: float32 [8, 16, 96, 1536], P(('dp', 'pp'))
- output 8: float32 [8, 1536], P(('dp', 'pp'))
- output 9: float32 [8, 1536], P(('dp', 'pp'))
- output 10: float32 [8, 1536], P(('dp', 'pp'))
- output 11: float32 [8, 1536, 6144], P(('dp', 'pp'))
- output 12: float32 [8, 6144], P(('dp', 'pp'))
- output 13: float32 [8, 6144, 1536], P(('dp', 'pp'))
- output 14: float32 [8, 1536], P(('dp', 'pp'))
All inputs are finite; a program needn't handle non-finite values.
Results may differ from a plain program's by a relative error of at most 0.02.
Values are sent between devices in bfloat16 or wider.
A program may use at most 1.25 GiB of HBM per device.

v0:
```python
import jax
import jax.numpy as jnp
from jax import lax
from jax.sharding import PartitionSpec as P

LN_EPS = 1e-5
PARAM_RANKS = (2, 2, 3, 2, 4, 2, 2, 2, 3, 2, 3, 2)


def layer_norm(x_wide, gain, shift):
    mean_val = jnp.mean(x_wide, axis=-1, keepdims=True)
    centered = x_wide - mean_val
    variance = jnp.mean(centered * centered, axis=-1, keepdims=True)
    return centered * lax.rsqrt(variance + LN_EPS) * gain + shift


def gelu_tanh(pre_act):
    return jax.nn.gelu(pre_act, approximate=True)


def layer_forward(weights, x_act):
    g_one, s_one, w_qkv, b_qkv, w_proj, b_proj, g_two, s_two, w_up, b_up, w_down, b_down = weights
    n_batch, n_seq = x_act.shape[0], x_act.shape[1]
    n_heads, head_dim = w_proj.shape[0], w_proj.shape[1]
    x_wide = x_act.astype(jnp.float32)
    h_one = layer_norm(x_wide, g_one.astype(jnp.float32), s_one.astype(jnp.float32)).astype(jnp.bfloat16)
    qkv_act = (jnp.einsum('bsd,de->bse', h_one, w_qkv, preferred_element_type=jnp.float32) + b_qkv.astype(jnp.float32)).astype(jnp.bfloat16)
    qkv_heads = qkv_act.reshape(n_batch, n_seq, 3, n_heads, head_dim)
    scores = jnp.einsum('bqhd,bkhd->bhqk', qkv_heads[:, :, 0], qkv_heads[:, :, 1], preferred_element_type=jnp.float32) * (head_dim ** -0.5)
    causal = jnp.arange(n_seq)[:, None] >= jnp.arange(n_seq)[None, :]
    attn_probs = jax.nn.softmax(jnp.where(causal, scores, -1e30), axis=-1).astype(jnp.bfloat16)
    attn_mix = jnp.einsum('bhqk,bkhd->bqhd', attn_probs, qkv_heads[:, :, 2], preferred_element_type=jnp.float32).astype(jnp.bfloat16)
    x_mid = (x_wide + jnp.einsum('bqhd,hde->bqe', attn_mix, w_proj, preferred_element_type=jnp.float32) + b_proj.astype(jnp.float32)).astype(jnp.bfloat16)
    mid_wide = x_mid.astype(jnp.float32)
    h_two = layer_norm(mid_wide, g_two.astype(jnp.float32), s_two.astype(jnp.float32)).astype(jnp.bfloat16)
    pre_act = jnp.einsum('bsd,df->bsf', h_two, w_up, preferred_element_type=jnp.float32) + b_up.astype(jnp.float32)
    hidden = gelu_tanh(pre_act).astype(jnp.bfloat16)
    y_act = (mid_wide + jnp.einsum('bsf,fd->bsd', hidden, w_down, preferred_element_type=jnp.float32) + b_down.astype(jnp.float32)).astype(jnp.bfloat16)
    return y_act, (x_act, qkv_act, attn_probs, attn_mix, x_mid, pre_act)


def layer_backward(weights, saved, grad_y):
    g_one, s_one, w_qkv, b_qkv, w_proj, b_proj, g_two, s_two, w_up, b_up, w_down, b_down = weights
    x_act, qkv_act, attn_probs, attn_mix, x_mid, pre_act = saved
    n_batch, n_seq = x_act.shape[0], x_act.shape[1]
    n_heads, head_dim = w_proj.shape[0], w_proj.shape[1]
    grad_wide = grad_y.astype(jnp.float32)
    hidden_f, gelu_pull = jax.vjp(gelu_tanh, pre_act)
    grad_w_down = jnp.einsum('bsf,bsd->fd', hidden_f.astype(jnp.bfloat16), grad_y, preferred_element_type=jnp.float32)
    grad_b_down = jnp.sum(grad_wide, axis=(0, 1))
    grad_hidden = jnp.einsum('bsd,fd->bsf', grad_y, w_down, preferred_element_type=jnp.float32).astype(jnp.bfloat16)
    grad_pre = gelu_pull(grad_hidden.astype(jnp.float32))[0]
    grad_b_up = jnp.sum(grad_pre, axis=(0, 1))
    grad_pre_bf = grad_pre.astype(jnp.bfloat16)
    h_two_f, ln_two_pull = jax.vjp(layer_norm, x_mid.astype(jnp.float32), g_two.astype(jnp.float32), s_two.astype(jnp.float32))
    grad_w_up = jnp.einsum('bsd,bsf->df', h_two_f.astype(jnp.bfloat16), grad_pre_bf, preferred_element_type=jnp.float32)
    grad_h_two = jnp.einsum('bsf,df->bsd', grad_pre_bf, w_up, preferred_element_type=jnp.float32).astype(jnp.bfloat16)
    grad_mid_ln, grad_g_two, grad_s_two = ln_two_pull(grad_h_two.astype(jnp.float32))
    grad_mid = (grad_wide + grad_mid_ln).astype(jnp.bfloat16)
    grad_mid_wide = grad_mid.astype(jnp.float32)
    grad_b_proj = jnp.sum(grad_mid_wide, axis=(0, 1))
    grad_w_proj = jnp.einsum('bqhd,bqe->hde', attn_mix, grad_mid, preferred_element_type=jnp.float32)
    grad_mix = jnp.einsum('bqe,hde->bqhd', grad_mid, w_proj, preferred_element_type=jnp.float32).astype(jnp.bfloat16)
    qkv_heads = qkv_act.reshape(n_batch, n_seq, 3, n_heads, head_dim)
    grad_probs = jnp.einsum('bqhd,bkhd->bhqk', grad_mix, qkv_heads[:, :, 2], preferred_element_type=jnp.float32).astype(jnp.bfloat16).astype(jnp.float32)
    grad_v = jnp.einsum('bhqk,bqhd->bkhd', attn_probs, grad_mix, preferred_element_type=jnp.float32)
    probs_wide = attn_probs.astype(jnp.float32)
    row_dot = jnp.sum(grad_probs * probs_wide, axis=-1, keepdims=True)
    grad_scores = (probs_wide * (grad_probs - row_dot) * (head_dim ** -0.5)).astype(jnp.bfloat16)
    grad_q = jnp.einsum('bhqk,bkhd->bqhd', grad_scores, qkv_heads[:, :, 1], preferred_element_type=jnp.float32)
    grad_k = jnp.einsum('bhqk,bqhd->bkhd', grad_scores, qkv_heads[:, :, 0], preferred_element_type=jnp.float32)
    grad_qkv = jnp.stack([grad_q.astype(jnp.bfloat16), grad_k.astype(jnp.bfloat16), grad_v.astype(jnp.bfloat16)], axis=2).reshape(qkv_act.shape)
    grad_b_qkv = jnp.sum(grad_qkv, axis=(0, 1), dtype=jnp.float32)
    h_one_f, ln_one_pull = jax.vjp(layer_norm, x_act.astype(jnp.float32), g_one.astype(jnp.float32), s_one.astype(jnp.float32))
    grad_w_qkv = jnp.einsum('bsd,bse->de', h_one_f.astype(jnp.bfloat16), grad_qkv, preferred_element_type=jnp.float32)
    grad_h_one = jnp.einsum('bse,de->bsd', grad_qkv, w_qkv, preferred_element_type=jnp.float32).astype(jnp.bfloat16)
    grad_x_ln, grad_g_one, grad_s_one = ln_one_pull(grad_h_one.astype(jnp.float32))
    grad_x = (grad_mid_wide + grad_x_ln).astype(jnp.bfloat16)
    return grad_x, (grad_g_one, grad_s_one, grad_w_qkv, grad_b_qkv, grad_w_proj, grad_b_proj, grad_g_two, grad_s_two, grad_w_up, grad_b_up, grad_w_down, grad_b_down)


def solution(mesh):
    n_stages = mesh.shape['pp']
    last_stage = n_stages - 1
    fwd_pairs = [(source, source + 1) for source in range(n_stages - 1)]
    bwd_pairs = [(source + 1, source) for source in range(n_stages - 1)]
    act_spec = P(None, 'dp', None, None)
    param_specs = tuple(P(*(('pp',) + (None,) * (rank_n - 1))) for rank_n in PARAM_RANKS)
    grad_specs = tuple(P(*((('dp', 'pp'),) + (None,) * (rank_n - 1))) for rank_n in PARAM_RANKS)

    def stage_body(acts_in, cotangent, *stacked_w):
        weights = tuple(tensor[0] for tensor in stacked_w)
        stage_idx = lax.axis_index('pp')
        n_micro, n_rows, n_seq, n_width = acts_in.shape
        n_heads, head_dim = stacked_w[4].shape[1], stacked_w[4].shape[2]
        n_hidden = stacked_w[8].shape[2]
        mb_shape = (n_rows, n_seq, n_width)
        n_steps = n_micro + n_stages - 1
        saved_init = (
            jnp.zeros((n_micro, n_rows, n_seq, n_width), jnp.bfloat16),
            jnp.zeros((n_micro, n_rows, n_seq, 3 * n_width), jnp.bfloat16),
            jnp.zeros((n_micro, n_rows, n_heads, n_seq, n_seq), jnp.bfloat16),
            jnp.zeros((n_micro, n_rows, n_seq, n_heads, head_dim), jnp.bfloat16),
            jnp.zeros((n_micro, n_rows, n_seq, n_width), jnp.bfloat16),
            jnp.zeros((n_micro, n_rows, n_seq, n_hidden), jnp.float32),
        )

        def fwd_step(step_idx, loop_state):
            incoming, saved_all, y_store = loop_state
            mb_index = step_idx - stage_idx
            is_valid = (mb_index >= 0) & (mb_index < n_micro)
            mb_slot = jnp.clip(mb_index, 0, n_micro - 1)
            first_in = lax.dynamic_index_in_dim(acts_in, jnp.minimum(step_idx, n_micro - 1), 0, keepdims=False)
            layer_in = jnp.where(stage_idx == 0, first_in, incoming)

            def run_layer(held_bufs):
                saved_now, y_now = held_bufs
                y_act, saved = layer_forward(weights, layer_in)
                saved_now = tuple(lax.dynamic_update_index_in_dim(buf_all, buf_new, mb_slot, 0) for buf_all, buf_new in zip(saved_now, saved))
                return y_act, saved_now, lax.dynamic_update_index_in_dim(y_now, y_act, mb_slot, 0)

            def skip_layer(held_bufs):
                return jnp.zeros(mb_shape, jnp.bfloat16), held_bufs[0], held_bufs[1]

            y_act, saved_all, y_store = lax.cond(is_valid, run_layer, skip_layer, (saved_all, y_store))
            return lax.ppermute(y_act, 'pp', fwd_pairs), saved_all, y_store

        fwd_init = (jnp.zeros(mb_shape, jnp.bfloat16), saved_init, jnp.zeros(acts_in.shape, jnp.bfloat16))
        unused_in, saved_all, y_store = lax.fori_loop(0, n_steps, fwd_step, fwd_init)

        def bwd_step(step_idx, loop_state):
            incoming, grad_acc, dx_store = loop_state
            offset = step_idx - (last_stage - stage_idx)
            is_valid = (offset >= 0) & (offset < n_micro)
            mb_slot = jnp.clip(n_micro - 1 - offset, 0, n_micro - 1)
            top_ct = lax.dynamic_index_in_dim(cotangent, jnp.clip(n_micro - 1 - step_idx, 0, n_micro - 1), 0, keepdims=False)
            layer_ct = jnp.where(stage_idx == last_stage, top_ct, incoming)

            def run_back(held_bufs):
                grad_now, dx_now = held_bufs
                saved = tuple(lax.dynamic_index_in_dim(buf_all, mb_slot, 0, keepdims=False) for buf_all in saved_all)
                grad_x, w_grads = layer_backward(weights, saved, layer_ct)
                grad_now = tuple(acc_old + acc_new for acc_old, acc_new in zip(grad_now, w_grads))
                return grad_x, grad_now, lax.dynamic_update_index_in_dim(dx_now, grad_x, mb_slot, 0)

            def skip_back(held_bufs):
                return jnp.zeros(mb_shape, jnp.bfloat16), held_bufs[0], held_bufs[1]

            grad_x, grad_acc, dx_store = lax.cond(is_valid, run_back, skip_back, (grad_acc, dx_store))
            return lax.ppermute(grad_x, 'pp', bwd_pairs), grad_acc, dx_store

        grad_zero = tuple(jnp.zeros(tensor.shape, jnp.float32) for tensor in weights)
        bwd_init = (jnp.zeros(mb_shape, jnp.bfloat16), grad_zero, jnp.zeros(acts_in.shape, jnp.bfloat16))
        unused_ct, grad_acc, dx_store = lax.fori_loop(0, n_steps, bwd_step, bwd_init)
        acts_out = lax.psum(jnp.where(stage_idx == last_stage, y_store, jnp.zeros_like(y_store)), 'pp')
        grad_in = lax.psum(jnp.where(stage_idx == 0, dx_store, jnp.zeros_like(dx_store)), 'pp')
        return (acts_out, grad_in) + tuple(acc_sum[None] for acc_sum in grad_acc)

    return jax.shard_map(stage_body, mesh=mesh, in_specs=(act_spec, act_spec) + param_specs, out_specs=(act_spec, act_spec) + grad_specs, check_vma=False)
```

profile of v0, /device:TPU:0, one launch (start us, length us, event | category | flops | bytes accessed | tf_op | source)
XLA Modules:
  0.0 9647.4 jit_solution(6717859135358898235)
XLA Ops:
  15.5 61.4 broadcast_in_dim.180
  77.0 40.9 broadcast_in_dim.178
  177.3 2526.6 %while.69 = (s32[]{:T(128)}, bf16[2,512,1536]{2,1,0:T(8,128)(2,1)}, bf16[8,2,512,1536]{3,2,1,0:T(8,128)(2,1)}, bf16[8,2,512,4608]{3,2,1,0:T(8,128)(2,1)}, bf16[8...) while((s32[]{:T(128)}, bf16[2,512,1536]{2,1,0:T(8,128)(2,1)}, ...), condition=%wide.region_9.10_spmd, body=%wide.region_0.9_spmd.sunk | while | flops 61386022912 | bytes 502186336 | solution.py:129
  177.3 169.2 %conditional.4 = (bf16[2,512,1536]{2,1,0:T(8,128)(2,1)}, bf16[8,2,512,1536]{3,2,1,0:T(8,128)(2,1)}, bf16[8,2,512,4608]{3,2,1,0:T(8,128)(2,1)}, bf16[8,2,16,512,5...) conditional(s32[]{:T(128)} %convert_element_type.576, ...), branch_computations={%region_1.1_spmd, %region_2.8_spmd} | conditional | flops 61386022912 | bytes 477019936 | solution.py:125
  354.7 169.4 %conditional.4 = (bf16[2,512,1536]{2,1,0:T(8,128)(2,1)}, bf16[8,2,512,1536]{3,2,1,0:T(8,128)(2,1)}, bf16[8,2,512,4608]{3,2,1,0:T(8,128)(2,1)}, bf16[8,2,16,512,5...) conditional(s32[]{:T(128)} %convert_element_type.576, ...), branch_computations={%region_1.1_spmd, %region_2.8_spmd} | conditional | flops 61386022912 | bytes 477019936 | solution.py:125
  534.0 169.2 %conditional.4 = (bf16[2,512,1536]{2,1,0:T(8,128)(2,1)}, bf16[8,2,512,1536]{3,2,1,0:T(8,128)(2,1)}, bf16[8,2,512,4608]{3,2,1,0:T(8,128)(2,1)}, bf16[8,2,16,512,5...) conditional(s32[]{:T(128)} %convert_element_type.576, ...), branch_computations={%region_1.1_spmd, %region_2.8_spmd} | conditional | flops 61386022912 | bytes 477019936 | solution.py:125
  742.0 169.1 %conditional.4 = (bf16[2,512,1536]{2,1,0:T(8,128)(2,1)}, bf16[8,2,512,1536]{3,2,1,0:T(8,128)(2,1)}, bf16[8,2,512,4608]{3,2,1,0:T(8,128)(2,1)}, bf16[8,2,16,512,5...) conditional(s32[]{:T(128)} %convert_element_type.576, ...), branch_computations={%region_1.1_spmd, %region_2.8_spmd} | conditional | flops 61386022912 | bytes 477019936 | solution.py:125
  952.2 169.2 %conditional.4 = (bf16[2,512,1536]{2,1,0:T(8,128)(2,1)}, bf16[8,2,512,1536]{3,2,1,0:T(8,128)(2,1)}, bf16[8,2,512,4608]{3,2,1,0:T(8,128)(2,1)}, bf16[8,2,16,512,5...) conditional(s32[]{:T(128)} %convert_element_type.576, ...), branch_computations={%region_1.1_spmd, %region_2.8_spmd} | conditional | flops 61386022912 | bytes 477019936 | solution.py:125
  1162.7 169.2 %conditional.4 = (bf16[2,512,1536]{2,1,0:T(8,128)(2,1)}, bf16[8,2,512,1536]{3,2,1,0:T(8,128)(2,1)}, bf16[8,2,512,4608]{3,2,1,0:T(8,128)(2,1)}, bf16[8,2,16,512,5...) conditional(s32[]{:T(128)} %convert_element_type.576, ...), branch_computations={%region_1.1_spmd, %region_2.8_spmd} | conditional | flops 61386022912 | bytes 477019936 | solution.py:125
  1373.0 169.2 %conditional.4 = (bf16[2,512,1536]{2,1,0:T(8,128)(2,1)}, bf16[8,2,512,1536]{3,2,1,0:T(8,128)(2,1)}, bf16[8,2,512,4608]{3,2,1,0:T(8,128)(2,1)}, bf16[8,2,16,512,5...) conditional(s32[]{:T(128)} %convert_element_type.576, ...), branch_computations={%region_1.1_spmd, %region_2.8_spmd} | conditional | flops 61386022912 | bytes 477019936 | solution.py:125
  1583.3 169.2 %conditional.4 = (bf16[2,512,1536]{2,1,0:T(8,128)(2,1)}, bf16[8,2,512,1536]{3,2,1,0:T(8,128)(2,1)}, bf16[8,2,512,4608]{3,2,1,0:T(8,128)(2,1)}, bf16[8,2,16,512,5...) conditional(s32[]{:T(128)} %convert_element_type.576, ...), branch_computations={%region_1.1_spmd, %region_2.8_spmd} | conditional | flops 61386022912 | bytes 477019936 | solution.py:125
  1795.6 201.7 %collective-permute-start = (bf16[2,512,1536]{2,1,0:T(8,128)(2,1)}, bf16[2,512,1536]{2,1,0:T(8,128)(2,1)S(1)}, u32[]{:S(2)}, u32[]{:S(2)}) collective-permute-start(bf16[2,512,1536]{2,1,0:T(8,128)(2,1)} %get-tuple-element.2417), channel_id=1, source_target_pairs={{0,1},{1,2},{2,3},{3,4},{4,5},{5,6},{6,7}} | collective-permute-start | bytes 9437192 | tf_op jit(solution)/shard_map/while/body/eval_jaxpr/ppermute | solution.py:126
  2048.0 201.8 %collective-permute-start = (bf16[2,512,1536]{2,1,0:T(8,128)(2,1)}, bf16[2,512,1536]{2,1,0:T(8,128)(2,1)S(1)}, u32[]{:S(2)}, u32[]{:S(2)}) collective-permute-start(bf16[2,512,1536]{2,1,0:T(8,128)(2,1)} %get-tuple-element.2417), channel_id=1, source_target_pairs={{0,1},{1,2},{2,3},{3,4},{4,5},{5,6},{6,7}} | collective-permute-start | bytes 9437192 | tf_op jit(solution)/shard_map/while/body/eval_jaxpr/ppermute | solution.py:126
  2300.4 142.3 %collective-permute-start = (bf16[2,512,1536]{2,1,0:T(8,128)(2,1)}, bf16[2,512,1536]{2,1,0:T(8,128)(2,1)S(1)}, u32[]{:S(2)}, u32[]{:S(2)}) collective-permute-start(bf16[2,512,1536]{2,1,0:T(8,128)(2,1)} %get-tuple-element.2417), channel_id=1, source_target_pairs={{0,1},{1,2},{2,3},{3,4},{4,5},{5,6},{6,7}} | collective-permute-start | bytes 9437192 | tf_op jit(solution)/shard_map/while/body/eval_jaxpr/ppermute | solution.py:126
  2494.2 202.7 %collective-permute-start = (bf16[2,512,1536]{2,1,0:T(8,128)(2,1)}, bf16[2,512,1536]{2,1,0:T(8,128)(2,1)S(1)}, u32[]{:S(2)}, u32[]{:S(2)}) collective-permute-start(bf16[2,512,1536]{2,1,0:T(8,128)(2,1)} %get-tuple-element.2417), channel_id=1, source_target_pairs={{0,1},{1,2},{2,3},{3,4},{4,5},{5,6},{6,7}} | collective-permute-start | bytes 9437192 | tf_op jit(solution)/shard_map/while/body/eval_jaxpr/ppermute | solution.py:126
  2703.9 96.8 %copy.56 = bf16[8,2,512,4608]{2,3,1,0:T(8,128)(2,1)} copy(bf16[8,2,512,4608]{3,2,1,0:T(8,128)(2,1)} %get-tuple-element.1918) | data formatting | bytes 150994944 | tf_op jit(solution)/shard_map/while | solution.py:154
  2880.9 6135.3 %while.70 = (s32[]{:T(128)}, bf16[2,512,1536]{2,1,0:T(8,128)(2,1)}, f32[1536]{0:T(1024)}, f32[1536]{0:T(1024)}, f32[1536,4608]{1,0:T(8,128)}, /*index=5*/f32[460...) while((s32[]{:T(128)}, bf16[2,512,1536]{2,1,0:T(8,128)(2,1)}, ...), condition=%wide.region_31.32_spmd, body=%wide.region_11.31_spmd.sunk | while | flops 122960789504 | bytes 837856384 | solution.py:154
  2891.7 38.1 collective-permute-done.1
  2934.6 143.0 %collective-permute-done.1 = bf16[2,512,1536]{2,1,0:T(8,128)(2,1)S(1)} collective-permute-done((bf16[2,512,1536]{2,1,0:T(8,128)(2,1)}, bf16[2,512,1536]{2,1,0:T(8,128)(2,1)S(1)}, u32[]{:S(2)}, u32[]{:S(2)}) %collective-permute-start.1) | collective-permute-done | bytes 3145760 | tf_op jit(solution)/shard_map/while/body/eval_jaxpr/ppermute | solution.py:150
  3082.4 38.1 collective-permute-done.1
  3125.3 202.9 %collective-permute-done.1 = bf16[2,512,1536]{2,1,0:T(8,128)(2,1)S(1)} collective-permute-done((bf16[2,512,1536]{2,1,0:T(8,128)(2,1)}, bf16[2,512,1536]{2,1,0:T(8,128)(2,1)S(1)}, u32[]{:S(2)}, u32[]{:S(2)}) %collective-permute-start.1) | collective-permute-done | bytes 3145760 | tf_op jit(solution)/shard_map/while/body/eval_jaxpr/ppermute | solution.py:150
  3333.1 38.2 collective-permute-done.1
  3376.2 142.9 %collective-permute-done.1 = bf16[2,512,1536]{2,1,0:T(8,128)(2,1)S(1)} collective-permute-done((bf16[2,512,1536]{2,1,0:T(8,128)(2,1)}, bf16[2,512,1536]{2,1,0:T(8,128)(2,1)S(1)}, u32[]{:S(2)}, u32[]{:S(2)}) %collective-permute-start.1) | collective-permute-done | bytes 3145760 | tf_op jit(solution)/shard_map/while/body/eval_jaxpr/ppermute | solution.py:150
  3523.9 2413.5 %collective-permute-done.1 = bf16[2,512,1536]{2,1,0:T(8,128)(2,1)S(1)} collective-permute-done((bf16[2,512,1536]{2,1,0:T(8,128)(2,1)}, bf16[2,512,1536]{2,1,0:T(8,128)(2,1)S(1)}, u32[]{:S(2)}, u32[]{:S(2)}) %collective-permute-start.1) | collective-permute-done | bytes 3145760 | tf_op jit(solution)/shard_map/while/body/eval_jaxpr/ppermute | solution.py:150
  5939.0 347.1 %conditional.5 = (bf16[2,512,1536]{2,1,0:T(8,128)(2,1)}, f32[1536]{0:T(1024)}, f32[1536]{0:T(1024)}, f32[1536,4608]{1,0:T(8,128)}, f32[4608]{0:T(1024)}, /*index...) conditional(s32[]{:T(128)} %convert_element_type.577, ...), branch_computations={%region_12.12_spmd, %region_13.30_spmd} | conditional | flops 122960789504 | bytes 812689920 | solution.py:149
  5947.8 42.0 fusion.196
  6196.2 37.0 bitcast_add_fusion.1
  6244.5 40.6 bitcast_add_fusion
  6287.5 38.8 collective-permute-done.1
  6328.1 347.1 %conditional.5 = (bf16[2,512,1536]{2,1,0:T(8,128)(2,1)}, f32[1536]{0:T(1024)}, f32[1536]{0:T(1024)}, f32[1536,4608]{1,0:T(8,128)}, f32[4608]{0:T(1024)}, /*index...) conditional(s32[]{:T(128)} %convert_element_type.577, ...), branch_computations={%region_12.12_spmd, %region_13.30_spmd} | conditional | flops 122960789504 | bytes 812689920 | solution.py:149
  6336.9 42.0 fusion.196
  6585.3 37.0 bitcast_add_fusion.1
  6633.5 40.6 bitcast_add_fusion
  6676.5 38.4 collective-permute-done.1
  6716.7 347.2 %conditional.5 = (bf16[2,512,1536]{2,1,0:T(8,128)(2,1)}, f32[1536]{0:T(1024)}, f32[1536]{0:T(1024)}, f32[1536,4608]{1,0:T(8,128)}, f32[4608]{0:T(1024)}, /*index...) conditional(s32[]{:T(128)} %convert_element_type.577, ...), branch_computations={%region_12.12_spmd, %region_13.30_spmd} | conditional | flops 122960789504 | bytes 812689920 | solution.py:149
  6725.5 42.0 fusion.196
  6974.0 37.0 bitcast_add_fusion.1
  7022.2 40.6 bitcast_add_fusion
  7065.2 37.3 collective-permute-done.1
  7104.3 346.9 %conditional.5 = (bf16[2,512,1536]{2,1,0:T(8,128)(2,1)}, f32[1536]{0:T(1024)}, f32[1536]{0:T(1024)}, f32[1536,4608]{1,0:T(8,128)}, f32[4608]{0:T(1024)}, /*index...) conditional(s32[]{:T(128)} %convert_element_type.577, ...), branch_computations={%region_12.12_spmd, %region_13.30_spmd} | conditional | flops 122960789504 | bytes 812689920 | solution.py:149
  7113.2 42.0 fusion.196
  7361.3 37.0 bitcast_add_fusion.1
  7409.6 40.6 bitcast_add_fusion
  7452.5 38.5 collective-permute-done.1
  7492.8 347.0 %conditional.5 = (bf16[2,512,1536]{2,1,0:T(8,128)(2,1)}, f32[1536]{0:T(1024)}, f32[1536]{0:T(1024)}, f32[1536,4608]{1,0:T(8,128)}, f32[4608]{0:T(1024)}, /*index...) conditional(s32[]{:T(128)} %convert_element_type.577, ...), branch_computations={%region_12.12_spmd, %region_13.30_spmd} | conditional | flops 122960789504 | bytes 812689920 | solution.py:149
  7501.7 42.0 fusion.196
  7749.9 37.0 bitcast_add_fusion.1
  7798.2 40.6 bitcast_add_fusion
  7841.2 38.5 collective-permute-done.1
  7881.5 347.1 %conditional.5 = (bf16[2,512,1536]{2,1,0:T(8,128)(2,1)}, f32[1536]{0:T(1024)}, f32[1536]{0:T(1024)}, f32[1536,4608]{1,0:T(8,128)}, f32[4608]{0:T(1024)}, /*index...) conditional(s32[]{:T(128)} %convert_element_type.577, ...), branch_computations={%region_12.12_spmd, %region_13.30_spmd} | conditional | flops 122960789504 | bytes 812689920 | solution.py:149
  7890.3 42.0 fusion.196
  8138.7 37.0 bitcast_add_fusion.1
  8186.9 40.6 bitcast_add_fusion
  8229.9 37.4 collective-permute-done.1
  8269.1 346.9 %conditional.5 = (bf16[2,512,1536]{2,1,0:T(8,128)(2,1)}, f32[1536]{0:T(1024)}, f32[1536]{0:T(1024)}, f32[1536,4608]{1,0:T(8,128)}, f32[4608]{0:T(1024)}, /*index...) conditional(s32[]{:T(128)} %convert_element_type.577, ...), branch_computations={%region_12.12_spmd, %region_13.30_spmd} | conditional | flops 122960789504 | bytes 812689920 | solution.py:149
  8278.0 42.0 fusion.196
  8526.1 37.0 bitcast_add_fusion.1
  8574.3 40.6 bitcast_add_fusion
  8617.3 39.3 collective-permute-done.1
  8658.4 347.2 %conditional.5 = (bf16[2,512,1536]{2,1,0:T(8,128)(2,1)}, f32[1536]{0:T(1024)}, f32[1536]{0:T(1024)}, f32[1536,4608]{1,0:T(8,128)}, f32[4608]{0:T(1024)}, /*index...) conditional(s32[]{:T(128)} %convert_element_type.577, ...), branch_computations={%region_12.12_spmd, %region_13.30_spmd} | conditional | flops 122960789504 | bytes 812689920 | solution.py:149
  8667.2 42.0 fusion.196
  8915.7 37.0 bitcast_add_fusion.1
  8963.9 40.6 bitcast_add_fusion
  9045.2 561.1 %all-reduce.3.cloned.1.call-done = (bf16[8,2,512,1536]{3,2,1,0:T(8,128)(2,1)}, bf16[8,2,512,1536]{3,2,1,0:T(8,128)(2,1)}) async-done(((bf16[8,2,512,1536]{3,2,1,0:T(8,128)(2,1)}, bf16[8,2,512,1536]{3,2,1,0:T(8,128)(2,1)}), (bf16[8,2,512,1536]{3,2,1,0:T(8,128)(2,1)}, bf16[8,2,512,1536]{3,2,1,0:T(8,128)(2,1)})) %all-reduce.3.cloned.1.call-update) | async-done | bytes 50331664 | tf_op jit(solution)/shard_map/psum | solution.py:155
  (1357 shorter events, 3897.3 us)
Async XLA Ops:
  7.2 9599.1 %all-reduce.3.cloned.1.call-start = ((), (), s32[]{:S(2)}) async-start(), calls=%async_computation | async-start | bytes 100663296 | tf_op jit(solution)/shard_map/psum | solution.py:155
  346.5 6.6 collective-permute-start
  524.1 8.3 collective-permute-start
  703.2 37.2 collective-permute-start
  911.2 39.4 collective-permute-start
  1121.4 39.7 collective-permute-start
  1331.8 39.6 collective-permute-start
  1542.3 39.4 collective-permute-start
  1752.5 39.6 collective-permute-start
  1795.6 206.8 %collective-permute-start = (bf16[2,512,1536]{2,1,0:T(8,128)(2,1)}, bf16[2,512,1536]{2,1,0:T(8,128)(2,1)S(1)}, u32[]{:S(2)}, u32[]{:S(2)}) collective-permute-start(bf16[2,512,1536]{2,1,0:T(8,128)(2,1)} %get-tuple-element.2417), channel_id=1, source_target_pairs={{0,1},{1,2},{2,3},{3,4},{4,5},{5,6},{6,7}} | collective-permute-start | bytes 9437192 | tf_op jit(solution)/shard_map/while/body/eval_jaxpr/ppermute | solution.py:126
  2005.9 38.6 collective-permute-start
  2048.0 206.8 %collective-permute-start = (bf16[2,512,1536]{2,1,0:T(8,128)(2,1)}, bf16[2,512,1536]{2,1,0:T(8,128)(2,1)S(1)}, u32[]{:S(2)}, u32[]{:S(2)}) collective-permute-start(bf16[2,512,1536]{2,1,0:T(8,128)(2,1)} %get-tuple-element.2417), channel_id=1, source_target_pairs={{0,1},{1,2},{2,3},{3,4},{4,5},{5,6},{6,7}} | collective-permute-start | bytes 9437192 | tf_op jit(solution)/shard_map/while/body/eval_jaxpr/ppermute | solution.py:126
  2258.3 38.6 collective-permute-start
  2300.4 147.3 %collective-permute-start = (bf16[2,512,1536]{2,1,0:T(8,128)(2,1)}, bf16[2,512,1536]{2,1,0:T(8,128)(2,1)S(1)}, u32[]{:S(2)}, u32[]{:S(2)}) collective-permute-start(bf16[2,512,1536]{2,1,0:T(8,128)(2,1)} %get-tuple-element.2417), channel_id=1, source_target_pairs={{0,1},{1,2},{2,3},{3,4},{4,5},{5,6},{6,7}} | collective-permute-start | bytes 9437192 | tf_op jit(solution)/shard_map/while/body/eval_jaxpr/ppermute | solution.py:126
  2451.2 39.5 collective-permute-start
  2494.2 207.7 %collective-permute-start = (bf16[2,512,1536]{2,1,0:T(8,128)(2,1)}, bf16[2,512,1536]{2,1,0:T(8,128)(2,1)S(1)}, u32[]{:S(2)}, u32[]{:S(2)}) collective-permute-start(bf16[2,512,1536]{2,1,0:T(8,128)(2,1)} %get-tuple-element.2417), channel_id=1, source_target_pairs={{0,1},{1,2},{2,3},{3,4},{4,5},{5,6},{6,7}} | collective-permute-start | bytes 9437192 | tf_op jit(solution)/shard_map/while/body/eval_jaxpr/ppermute | solution.py:126
  2703.9 96.8 %copy-start.26 = (bf16[1536]{0:T(1024)(128)(2,1)}, bf16[1536]{0:T(1024)(128)(2,1)S(1)}, u32[]{:S(2)}) copy-start(bf16[1536]{0:T(1024)(128)(2,1)S(1)} %get-tuple-element.2727) | copy-start | bytes 9220
  2890.4 39.4 collective-permute-start.1
  2933.3 144.3 %collective-permute-start.1 = (bf16[2,512,1536]{2,1,0:T(8,128)(2,1)}, bf16[2,512,1536]{2,1,0:T(8,128)(2,1)S(1)}, u32[]{:S(2)}, u32[]{:S(2)}) collective-permute-start(bf16[2,512,1536]{2,1,0:T(8,128)(2,1)} %get-tuple-element.2457), channel_id=1, source_target_pairs={{1,0},{2,1},{3,2},{4,3},{5,4},{6,5},{7,6}} | collective-permute-start | bytes 9437192 | tf_op jit(solution)/shard_map/while/body/eval_jaxpr/ppermute | solution.py:150
  3081.1 39.4 collective-permute-start.1
  3124.1 204.2 %collective-permute-start.1 = (bf16[2,512,1536]{2,1,0:T(8,128)(2,1)}, bf16[2,512,1536]{2,1,0:T(8,128)(2,1)S(1)}, u32[]{:S(2)}, u32[]{:S(2)}) collective-permute-start(bf16[2,512,1536]{2,1,0:T(8,128)(2,1)} %get-tuple-element.2457), channel_id=1, source_target_pairs={{1,0},{2,1},{3,2},{4,3},{5,4},{6,5},{7,6}} | collective-permute-start | bytes 9437192 | tf_op jit(solution)/shard_map/while/body/eval_jaxpr/ppermute | solution.py:150
  3331.8 39.5 collective-permute-start.1
  3374.9 144.1 %collective-permute-start.1 = (bf16[2,512,1536]{2,1,0:T(8,128)(2,1)}, bf16[2,512,1536]{2,1,0:T(8,128)(2,1)S(1)}, u32[]{:S(2)}, u32[]{:S(2)}) collective-permute-start(bf16[2,512,1536]{2,1,0:T(8,128)(2,1)} %get-tuple-element.2457), channel_id=1, source_target_pairs={{1,0},{2,1},{3,2},{4,3},{5,4},{6,5},{7,6}} | collective-permute-start | bytes 9437192 | tf_op jit(solution)/shard_map/while/body/eval_jaxpr/ppermute | solution.py:150
  3522.6 2414.8 %collective-permute-start.1 = (bf16[2,512,1536]{2,1,0:T(8,128)(2,1)}, bf16[2,512,1536]{2,1,0:T(8,128)(2,1)S(1)}, u32[]{:S(2)}, u32[]{:S(2)}) collective-permute-start(bf16[2,512,1536]{2,1,0:T(8,128)(2,1)} %get-tuple-element.2457), channel_id=1, source_target_pairs={{1,0},{2,1},{3,2},{4,3},{5,4},{6,5},{7,6}} | collective-permute-start | bytes 9437192 | tf_op jit(solution)/shard_map/while/body/eval_jaxpr/ppermute | solution.py:150
  5943.4 80.6 copy-start.10
  5947.8 76.1 copy-start.5
  6244.3 40.7 copy-start.36
  6244.3 40.7 copy-start.39
  6286.1 40.1 collective-permute-start.1
  6332.5 80.6 copy-start.10
  6336.9 76.1 copy-start.5
  6633.4 40.7 copy-start.36
  6633.4 40.7 copy-start.39
  6675.2 39.7 collective-permute-start.1
  6721.1 80.6 copy-start.10
  6725.5 76.1 copy-start.5
  7022.1 40.7 copy-start.36
  7022.1 40.7 copy-start.39
  7063.9 38.6 collective-permute-start.1
  7108.7 80.6 copy-start.10
  7113.2 76.1 copy-start.5
  7409.4 40.7 copy-start.36
  7409.4 40.7 copy-start.39
  7451.2 39.8 collective-permute-start.1
  7497.2 80.6 copy-start.10
  7501.7 76.1 copy-start.5
  7798.0 40.7 copy-start.36
  7798.0 40.7 copy-start.39
  7839.8 39.8 collective-permute-start.1
  7885.9 80.6 copy-start.10
  7890.3 76.1 copy-start.5
  8186.8 40.7 copy-start.36
  8186.8 40.7 copy-start.39
  8228.6 38.7 collective-permute-start.1
  8273.5 80.6 copy-start.10
  8278.0 76.1 copy-start.5
  8574.1 40.7 copy-start.36
  8574.2 40.7 copy-start.39
  8616.0 40.6 collective-permute-start.1
  8662.7 80.6 copy-start.10
  8667.2 76.1 copy-start.5
  8963.7 40.7 copy-start.36
  8963.8 40.7 copy-start.39
  9005.6 7.6 collective-permute-start.1
  (334 other events, 5203.5 us)
Sparse Core Ops, SparseCore 0:
  9040.5 565.7 all-reduce.2
where the time goes:
time: 9660 us; the launch traced here: 9650 us
  waiting for transfers between devices  3930 us (41%)
  matrix products  3280 us (34%)
  starting transfers between devices  1080 us (11%)
  local copies, waits for them, and re-layouts  729 us (8%)
  other arithmetic  598 us (6%)
    ppermute x15, waiting for transfers between devices, bwd_step(): return (lax.ppermute(grad_x, 'pp', bwd_pairs), grad_acc, dx_store)  3290 us
    ppermute x15, starting transfers between devices, fwd_step(): return (lax.ppermute(y_act, 'pp', fwd_pairs), saved_all, y_store)  1060 us
    psum x1, waiting for transfers between devices, stage_body(): lax.psum(jnp.where(stage_idx == last_stage, y_store, jnp.zeros_like(y_sto...  561 us
    dot_general x8, matrix products, layer_backward(): jnp.einsum('bsd,fd->bsf', grad_y, w_down, preferred_element_type=jnp.floa...  336 us
    dot_general x8, matrix products, layer_backward(): jnp.einsum('bsf,bsd->fd', hidden_f.astype(jnp.bfloat16), grad_y, preferre...  325 us
    dot_general x8, matrix products, layer_backward(): jnp.einsum('bsd,bsf->df', h_two_f.astype(jnp.bfloat16), grad_pre_bf, pref...  296 us
    dot_general x8, matrix products, layer_forward(): jnp.einsum('bsf,fd->bsd', hidden, w_down, preferred_element_type=jnp.floa...  256 us
    dot_general x8, matrix products, layer_backward(): jnp.einsum('bsd,bse->de', h_one_f.astype(jnp.bfloat16), grad_qkv, preferr...  254 us
  transfers between devices with their start and end apart: 31, of which 31 were waited for; matrix products, arithmetic and copies ran while one was open for 0% of the time, Pallas kernels for 0%

commit v1 on v0

v1 whole, which is shorter than its diff:
```python
import functools
import jax
import jax.numpy as jnp
from jax import lax
from jax.experimental import pallas as pl
from jax.experimental.pallas import tpu as pltpu
from jax.sharding import PartitionSpec as P

LN_EPS = 1e-5
PARAM_RANKS = (2, 2, 3, 2, 4, 2, 2, 2, 3, 2, 3, 2)
BF, F32 = jnp.bfloat16, jnp.float32
LOG2E = 1.4426950408889634
GC0 = 0.7978845608028654
GC1 = GC0 * 0.044715
NT = (((1,), (1,)), ((), ()))
NN = (((1,), (0,)), ((), ()))
TN = (((0,), (0,)), ((), ()))


def mm(a, b, dims=NN):
    return lax.dot_general(a, b, dims, preferred_element_type=F32)


def ln_stats(x_wide):
    mean_val = jnp.mean(x_wide, axis=-1, keepdims=True)
    centered = x_wide - mean_val
    variance = jnp.mean(centered * centered, axis=-1, keepdims=True)
    rstd = lax.rsqrt(variance + LN_EPS)
    return centered * rstd, rstd


def ln_back(dh, xhat, rstd, gain):
    dxh = dh * gain
    c1 = jnp.mean(dxh, axis=-1, keepdims=True)
    c2 = jnp.mean(dxh * xhat, axis=-1, keepdims=True)
    return rstd * (dxh - c1 - xhat * c2)


HEAD_WIN = ((0, 128), (0, 256), (128, 384), (256, 384))


def head_mask(j):
    lo, hi = HEAD_WIN[j]
    lane = lax.broadcasted_iota(jnp.int32, (1, hi - lo), 1) + lo
    keep = (lane >= 96 * j) & (lane < 96 * j + 96)
    return jnp.where(keep, 1.0, 0.0).astype(BF)


def fwd_kernel(n_qkv, n_grp, n_proj, n_mlp, idx, x_ref, g1, s1, wqkv, bqkv, wproj, bproj, g2, s2, wup, bup, wdown, bdown,
               _a0, _a1, _a2, _a3, _a4, _a5, _a6,
               y_ref, xs_ref, h1_ref, qkv_ref, mix_ref, x1_ref, h2_ref, pre_ref,
               qkv_s, mix_s, h_s, act_s, acc_s):
    step = pl.program_id(0)
    b0, b1, b2 = n_qkv, n_qkv + n_grp, n_qkv + n_grp + n_proj
    tq, tp, tf = wqkv.shape[1], wproj.shape[1], wup.shape[1]
    d = x_ref.shape[1]
    n_seq = x_ref.shape[0]
    half = n_seq // 2

    @pl.when(step == 0)
    def _():
        x = x_ref[...]
        xs_ref[0] = x
        xhat, _ = ln_stats(x.astype(F32))
        h = (xhat * g1[...].astype(F32) + s1[...].astype(F32)).astype(BF)
        h_s[...] = h
        h1_ref[0] = h

    @pl.when(step < b0)
    def _():
        t = (mm(h_s[...], wqkv[...]) + bqkv[...].astype(F32)).astype(BF)
        qkv_ref[0] = t
        qkv_s[:, pl.ds(pl.multiple_of(step * tq, 128), tq)] = t

    @pl.when((step >= b0) & (step < b1))
    def _():
        grp = step - b0
        sl = lambda p: pl.ds(pl.multiple_of(p * d + grp * 384, 128), 384)
        q, k, v = qkv_s[:, sl(0)], qkv_s[:, sl(1)], qkv_s[:, sl(2)]
        rows = lax.broadcasted_iota(jnp.int32, (half, half), 0)
        cols = lax.broadcasted_iota(jnp.int32, (half, half), 1)
        causal = rows >= cols
        sc = (96.0 ** -0.5) * LOG2E
        outs = []
        for j in range(4):
            lo, hi = HEAD_WIN[j]
            m = head_mask(j)
            qm, vm, kw = q[:, lo:hi] * m, v[:, lo:hi] * m, k[:, lo:hi]
            s00 = jnp.where(causal, mm(qm[:half], kw[:half], NT), -1e30)
            s10 = mm(qm[half:], kw[:half], NT)
            s11 = jnp.where(causal, mm(qm[half:], kw[half:], NT), -1e30)
            m0 = jnp.max(s00, axis=1, keepdims=True)
            e00 = jnp.exp2((s00 - m0) * sc)
            p00 = (e00 * (1.0 / jnp.sum(e00, axis=1, keepdims=True))).astype(BF)
            o0 = mm(p00, vm[:half])
            m1 = jnp.maximum(jnp.max(s10, axis=1, keepdims=True), jnp.max(s11, axis=1, keepdims=True))
            e10 = jnp.exp2((s10 - m1) * sc)
            e11 = jnp.exp2((s11 - m1) * sc)
            r1 = 1.0 / (jnp.sum(e10, axis=1, keepdims=True) + jnp.sum(e11, axis=1, keepdims=True))
            p10 = (e10 * r1).astype(BF)
            p11 = (e11 * r1).astype(BF)
            o1 = mm(p10, vm[:half]) + mm(p11, vm[half:])
            outs.append(jnp.concatenate([o0, o1], axis=0))
        t0 = outs[0] + outs[1][:, :128]
        t1 = outs[1][:, 128:] + outs[2][:, :128]
        t2 = outs[2][:, 128:] + outs[3]
        o = jnp.concatenate([t0, t1, t2], axis=1).astype(BF)
        mix_ref[0] = o
        mix_s[:, pl.ds(pl.multiple_of(grp * 384, 128), 384)] = o

    @pl.when((step >= b1) & (step < b2))
    def _():
        c = pl.ds(pl.multiple_of((step - b1) * tp, 128), tp)
        acc_s[:, c] = mm(mix_s[...], wproj[...]) + bproj[...].astype(F32)

    @pl.when(step == b2 - 1)
    def _():
        x1 = (x_ref[...].astype(F32) + acc_s[...]).astype(BF)
        x1_ref[0] = x1
        x1w = x1.astype(F32)
        xhat, _ = ln_stats(x1w)
        h = (xhat * g2[...].astype(F32) + s2[...].astype(F32)).astype(BF)
        h_s[...] = h
        h2_ref[0] = h
        acc_s[...] = x1w + bdown[...].astype(F32)

    def up():
        pre = mm(h_s[...], wup[...]) + bup[...].astype(F32)
        pre_ref[0] = pre
        t = jnp.tanh(pre * (GC0 + GC1 * (pre * pre)))
        return (0.5 * pre * (1.0 + t)).astype(BF)

    @pl.when(step == b2)
    def _():
        act_s[0] = up()

    @pl.when((step > b2) & (step < b2 + n_mlp))
    def _():
        slot = lax.rem(step - b2, 2)
        act_s[slot] = up()
        acc_s[...] += mm(act_s[1 - slot], wdown[...])

    @pl.when(step == b2 + n_mlp)
    def _():
        y_ref[...] = (acc_s[...] + mm(act_s[1 - lax.rem(step - b2, 2)], wdown[...])).astype(BF)


def fwd_call(idx, x, weights, saved):
    g1, s1, wqkv, bqkv, wproj, bproj, g2, s2, wup, bup, wdown, bdown = weights
    n_seq, d = x.shape
    e, f = wqkv.shape[1], wup.shape[1]
    tq, tp, tf = 768, 768, 512
    n_qkv, n_grp, n_proj, n_mlp = e // tq, 4, d // tp, f // tf
    b0, b1, b2 = n_qkv, n_qkv + n_grp, n_qkv + n_grp + n_proj
    full = lambda i, ix: (0, 0)
    row3 = lambda i, ix: (ix[0], 0, 0)
    cq = lambda i, ix: (0, jnp.clip(i, 0, n_qkv - 1))
    cp = lambda i, ix: (0, jnp.clip(i - b1, 0, n_proj - 1))
    cu = lambda i, ix: (0, jnp.clip(i - b2, 0, n_mlp - 1))
    rd = lambda i, ix: (jnp.clip(i - b2 - 1, 0, n_mlp - 1), 0)
    any_spec = pl.BlockSpec(memory_space=pl.ANY)
    in_specs = [
        pl.BlockSpec((n_seq, d), full), pl.BlockSpec((1, d), full), pl.BlockSpec((1, d), full),
        pl.BlockSpec((d, tq), cq), pl.BlockSpec((1, tq), cq),
        pl.BlockSpec((d, tp), cp), pl.BlockSpec((1, tp), cp),
        pl.BlockSpec((1, d), full), pl.BlockSpec((1, d), full),
        pl.BlockSpec((d, tf), cu), pl.BlockSpec((1, tf), cu),
        pl.BlockSpec((tf, d), rd), pl.BlockSpec((1, d), full),
    ] + [any_spec] * 7
    out_specs = [
        pl.BlockSpec((n_seq, d), full),
        pl.BlockSpec((1, n_seq, d), row3),
        pl.BlockSpec((1, n_seq, d), row3),
        pl.BlockSpec((1, n_seq, tq), lambda i, ix: (ix[0], 0, jnp.clip(i, 0, n_qkv - 1))),
        pl.BlockSpec((1, n_seq, 384), lambda i, ix: (ix[0], 0, jnp.clip(i - b0, 0, n_grp - 1))),
        pl.BlockSpec((1, n_seq, d), row3),
        pl.BlockSpec((1, n_seq, d), row3),
        pl.BlockSpec((1, n_seq, tf), lambda i, ix: (ix[0], 0, jnp.clip(i - b2, 0, n_mlp - 1))),
    ]
    r2 = lambda t: t.reshape(1, -1)
    args = [idx, x, r2(g1), r2(s1), wqkv, r2(bqkv), wproj.reshape(d, d), r2(bproj), r2(g2), r2(s2), wup, r2(bup), wdown, r2(bdown)]
    outs = pl.pallas_call(
        functools.partial(fwd_kernel, n_qkv, n_grp, n_proj, n_mlp),
        grid_spec=pltpu.PrefetchScalarGridSpec(
            num_scalar_prefetch=1, grid=(b2 + n_mlp + 1,), in_specs=in_specs, out_specs=out_specs,
            scratch_shapes=[pltpu.VMEM((n_seq, e), BF), pltpu.VMEM((n_seq, d), BF), pltpu.VMEM((n_seq, d), BF),
                            pltpu.VMEM((2, n_seq, tf), BF), pltpu.VMEM((n_seq, d), F32)]),
        out_shape=[jax.ShapeDtypeStruct((n_seq, d), BF)] + [jax.ShapeDtypeStruct(s.shape, s.dtype) for s in saved],
        input_output_aliases={14 + i: 1 + i for i in range(7)},
        compiler_params=pltpu.CompilerParams(dimension_semantics=("arbitrary",), vmem_limit_bytes=60 * 1024 * 1024),
        cost_estimate=pl.CostEstimate(flops=int(31e9), bytes_accessed=int(9e7), transcendentals=0),
        name="layer_fwd",
    )(*args, *saved)
    return outs[0], tuple(outs[1:])


def bwd_kernel(n_mlp, n_proj, n_grp, n_qkv, idx, dy_ref, pre_ref, x1_ref, q_ref, k_ref, v_ref, x_ref,
               wdown, wup, wproj, wqkv, g1, g2,
               _a0, _a1, _a2, _a3, _a4, _a5, _a6, _a7,
               dx_ref, act_ref, dpre_ref, dmid_ref, dqkv_ref, dys_ref, sup_ref, sqkv_ref, sd_ref,
               acc_s, dp_s, dm_s, do_s, dqkv_s):
    step = pl.program_id(0)
    b0 = n_mlp + 1
    b1, b2 = b0 + n_proj, b0 + n_proj + n_grp
    d = dy_ref.shape[1]
    n_seq = dy_ref.shape[0]
    half = n_seq // 2
    tp, tq = wproj.shape[0], wqkv.shape[1]
    colsum = lambda t: jnp.sum(t, axis=0, keepdims=True)

    def down_back():
        da = mm(dy_ref[...], wdown[...], NT).astype(BF).astype(F32)
        pre = pre_ref[0]
        p2 = pre * pre
        t = jnp.tanh(pre * (GC0 + GC1 * p2))
        u = 0.5 * (1.0 + t)
        act_ref[0] = (pre * u).astype(BF)
        dpre = da * (u + 0.5 * pre * (1.0 - t * t) * (GC0 + 3.0 * GC1 * p2))
        sup_ref[0] = colsum(dpre)
        dpb = dpre.astype(BF)
        dpre_ref[0] = dpb
        return dpb

    @pl.when(step == 0)
    def _():
        dy = dy_ref[...]
        dys_ref[0] = dy
        sd_ref[0, 5:6, :] = colsum(dy.astype(F32))
        acc_s[...] = jnp.zeros_like(acc_s)
        dp_s[0] = down_back()

    @pl.when((step > 0) & (step < n_mlp))
    def _():
        slot = lax.rem(step, 2)
        dp_s[slot] = down_back()
        acc_s[...] += mm(dp_s[1 - slot], wup[...], NT)

    @pl.when(step == n_mlp)
    def _():
        dh = (acc_s[...] + mm(dp_s[1 - lax.rem(step, 2)], wup[...], NT)).astype(BF).astype(F32)
        xhat, rstd = ln_stats(x1_ref[0].astype(F32))
        sd_ref[0, 2:3, :] = colsum(dh * xhat)
        sd_ref[0, 3:4, :] = colsum(dh)
        dm = (dy_ref[...].astype(F32) + ln_back(dh, xhat, rstd, g2[...].astype(F32))).astype(BF)
        dm_s[...] = dm
        dmid_ref[0] = dm
        sd_ref[0, 4:5, :] = colsum(dm.astype(F32))

    @pl.when((step >= b0) & (step < b1))
    def _():
        c = pl.ds(pl.multiple_of((step - b0) * tp, 128), tp)
        do_s[:, c] = mm(dm_s[...], wproj[...], NT).astype(BF)

    @pl.when((step >= b1) & (step < b2))
    def _():
        grp = step - b1
        q, k, v = q_ref[0], k_ref[0], v_ref[0]
        do = do_s[:, pl.ds(pl.multiple_of(grp * 384, 128), 384)]
        keys = lax.broadcasted_iota(jnp.int32, (half, n_seq), 0)
        qrys = lax.broadcasted_iota(jnp.int32, (half, n_seq), 1)
        ok0 = keys <= qrys
        ok1 = ok0[:, :half]
        scale = 96.0 ** -0.5
        sc = scale * LOG2E
        dqs, dks, dvs = [], [], []
        for j in range(4):
            lo, hi = HEAD_WIN[j]
            m = head_mask(j)
            qm, km, dom = q[:, lo:hi] * m, k[:, lo:hi] * m, do[:, lo:hi] * m
            kw, vw = k[:, lo:hi], v[:, lo:hi]
            st0 = jnp.where(ok0, mm(kw[:half], qm, NT), -1e30)
            st1 = jnp.where(ok1, mm(kw[half:], qm[half:], NT), -1e30)
            mx = jnp.max(st0, axis=0, keepdims=True)
            mr = jnp.maximum(mx[:, half:], jnp.max(st1, axis=0, keepdims=True))
            mx = jnp.concatenate([mx[:, :half], mr], axis=1)
            e0 = jnp.exp2((st0 - mx) * sc)
            e1 = jnp.exp2((st1 - mr) * sc)
            l0 = jnp.sum(e0, axis=0, keepdims=True)
            lr = l0[:, half:] + jnp.sum(e1, axis=0, keepdims=True)
            inv = 1.0 / jnp.concatenate([l0[:, :half], lr], axis=1)
            p0 = e0 * inv
            p1 = e1 * inv[:, half:]
            dp0 = mm(vw[:half], dom, NT).astype(BF).astype(F32)
            dp1 = mm(vw[half:], dom[half:], NT).astype(BF).astype(F32)
            rd = jnp.sum(p0 * dp0, axis=0, keepdims=True)
            rr = rd[:, half:] + jnp.sum(p1 * dp1, axis=0, keepdims=True)
            rd = jnp.concatenate([rd[:, :half], rr], axis=1)
            ds0 = (p0 * (dp0 - rd) * scale).astype(BF)
            ds1 = (p1 * (dp1 - rr) * scale).astype(BF)
            p0b, p1b = p0.astype(BF), p1.astype(BF)
            dvs.append(jnp.concatenate([mm(p0b, dom), mm(p1b, dom[half:])], axis=0))
            dks.append(jnp.concatenate([mm(ds0, qm), mm(ds1, qm[half:])], axis=0))
            dq0 = mm(ds0[:, :half], km[:half], TN)
            dq1 = mm(jnp.concatenate([ds0[:, half:], ds1], axis=0), km, TN)
            dqs.append(jnp.concatenate([dq0, dq1], axis=0))
        for part, t in enumerate((dqs, dks, dvs)):
            g = jnp.concatenate([t[0] + t[1][:, :128], t[1][:, 128:] + t[2][:, :128], t[2][:, 128:] + t[3]], axis=1).astype(BF)
            dqkv_s[:, pl.ds(pl.multiple_of(part * d + grp * 384, 128), 384)] = g

    @pl.when(step == b2)
    def _():
        acc_s[...] = jnp.zeros_like(acc_s)

    @pl.when(step >= b2)
    def _():
        t = dqkv_s[:, pl.ds(pl.multiple_of((step - b2) * tq, 128), tq)]
        dqkv_ref[0] = t
        sqkv_ref[0] = colsum(t.astype(F32))
        acc_s[...] += mm(t, wqkv[...], NT)

    @pl.when(step == b2 + n_qkv - 1)
    def _():
        dh = acc_s[...].astype(BF).astype(F32)
        xhat, rstd = ln_stats(x_ref[0].astype(F32))
        sd_ref[0, 0:1, :] = colsum(dh * xhat)
        sd_ref[0, 1:2, :] = colsum(dh)
        dx_ref[...] = (dm_s[...].astype(F32) + ln_back(dh, xhat, rstd, g1[...].astype(F32))).astype(BF)


def bwd_call(idx, dy, weights, saved, store):
    g1, s1, wqkv, bqkv, wproj, bproj, g2, s2, wup, bup, wdown, bdown = weights
    xs, h1, qkv, mix, x1, h2, pre = saved
    n_seq, d = dy.shape
    e, f = wqkv.shape[1], wup.shape[1]
    tq, tp, tf = 768, 768, 512
    n_qkv, n_grp, n_proj, n_mlp = e // tq, 4, d // tp, f // tf
    b0 = n_mlp + 1
    b1, b2 = b0 + n_proj, b0 + n_proj + n_grp
    full = lambda i, ix: (0, 0)
    row3 = lambda i, ix: (ix[0], 0, 0)
    mlp = lambda i: jnp.clip(i, 0, n_mlp - 1)
    grp = lambda i: jnp.clip(i - b1, 0, n_grp - 1)
    tqi = lambda i: jnp.clip(i - b2, 0, n_qkv - 1)
    any_spec = pl.BlockSpec(memory_space=pl.ANY)
    in_specs = [
        pl.BlockSpec((n_seq, d), full),
        pl.BlockSpec((1, n_seq, tf), lambda i, ix: (ix[0], 0, mlp(i))),
        pl.BlockSpec((1, n_seq, d), row3),
        pl.BlockSpec((1, n_seq, 384), lambda i, ix: (ix[0], 0, grp(i))),
        pl.BlockSpec((1, n_seq, 384), lambda i, ix: (ix[0], 0, 4 + grp(i))),
        pl.BlockSpec((1, n_seq, 384), lambda i, ix: (ix[0], 0, 8 + grp(i))),
        pl.BlockSpec((1, n_seq, d), row3),
        pl.BlockSpec((tf, d), lambda i, ix: (mlp(i), 0)),
        pl.BlockSpec((d, tf), lambda i, ix: (0, mlp(i - 1))),
        pl.BlockSpec((tp, d), lambda i, ix: (jnp.clip(i - b0, 0, n_proj - 1), 0)),
        pl.BlockSpec((d, tq), lambda i, ix: (0, tqi(i))),
        pl.BlockSpec((1, d), full), pl.BlockSpec((1, d), full),
    ] + [any_spec] * 8
    out_specs = [
        pl.BlockSpec((n_seq, d), full),
        pl.BlockSpec((1, n_seq, tf), lambda i, ix: (ix[0], 0, mlp(i))),
        pl.BlockSpec((1, n_seq, tf), lambda i, ix: (ix[0], 0, mlp(i))),
        pl.BlockSpec((1, n_seq, d), row3),
        pl.BlockSpec((1, n_seq, tq), lambda i, ix: (ix[0], 0, tqi(i))),
        pl.BlockSpec((1, n_seq, d), row3),
        pl.BlockSpec((1, 1, tf), lambda i, ix: (ix[0], 0, mlp(i))),
        pl.BlockSpec((1, 1, tq), lambda i, ix: (ix[0], 0, tqi(i))),
        pl.BlockSpec((1, 8, d), row3),
    ]
    r2 = lambda t: t.reshape(1, -1)
    args = [idx, dy, pre, x1, qkv, qkv, qkv, xs, wdown, wup, wproj.reshape(d, d), wqkv, r2(g1), r2(g2)]
    outs = pl.pallas_call(
        functools.partial(bwd_kernel, n_mlp, n_proj, n_grp, n_qkv),
        grid_spec=pltpu.PrefetchScalarGridSpec(
            num_scalar_prefetch=1, grid=(b2 + n_qkv,), in_specs=in_specs, out_specs=out_specs,
            scratch_shapes=[pltpu.VMEM((n_seq, d), F32), pltpu.VMEM((2, n_seq, tf), BF), pltpu.VMEM((n_seq, d), BF),
                            pltpu.VMEM((n_seq, d), BF), pltpu.VMEM((n_seq, e), BF)]),
        out_shape=[jax.ShapeDtypeStruct((n_seq, d), BF)] + [jax.ShapeDtypeStruct(s.shape, s.dtype) for s in store],
        input_output_aliases={14 + i: 1 + i for i in range(8)},
        compiler_params=pltpu.CompilerParams(dimension_semantics=("arbitrary",), vmem_limit_bytes=60 * 1024 * 1024),
        cost_estimate=pl.CostEstimate(flops=int(36e9), bytes_accessed=int(1.1e8), transcendentals=0),
        name="layer_bwd",
    )(*args, *store)
    return outs[0], tuple(outs[1:])


def fresh(shapes):
    return pl.pallas_call(
        lambda *refs: None,
        out_shape=shapes,
        out_specs=[pl.BlockSpec(memory_space=pl.ANY)] * len(shapes),
        name="fresh",
    )()


def solution(mesh):
    n_stages = mesh.shape['pp']
    last_stage = n_stages - 1
    fwd_pairs = [(source, source + 1) for source in range(n_stages - 1)]
    bwd_pairs = [(source + 1, source) for source in range(n_stages - 1)]
    act_spec = P(None, 'dp', None, None)
    param_specs = tuple(P(*(('pp',) + (None,) * (rank_n - 1))) for rank_n in PARAM_RANKS)
    grad_specs = tuple(P(*((('dp', 'pp'),) + (None,) * (rank_n - 1))) for rank_n in PARAM_RANKS)

    def stage_body(acts_in, cotangent, *stacked_w):
        weights = tuple(tensor[0] for tensor in stacked_w)
        stage = lax.axis_index('pp')
        n_micro, n_rows, n_seq, d = acts_in.shape
        n_chunk = n_micro * n_rows
        x_all = acts_in.reshape(n_chunk, n_seq, d)
        ct_all = cotangent.reshape(n_chunk, n_seq, d)
        sds = jax.ShapeDtypeStruct
        st = lambda r, w, t: sds((n_chunk, r, w), t)
        f = 4 * d
        shapes = [st(n_seq, d, BF), st(n_seq, d, BF), st(n_seq, 3 * d, BF), st(n_seq, d, BF), st(n_seq, d, BF), st(n_seq, d, BF), st(n_seq, f, F32),
                  st(n_seq, f, BF), st(n_seq, f, BF), st(n_seq, d, BF), st(n_seq, 3 * d, BF), st(n_seq, d, BF), st(1, f, F32), st(1, 3 * d, F32), st(8, d, F32),
                  st(n_seq, d, BF), st(n_seq, d, BF)]
        bufs = fresh(shapes)
        saved, store, y_all, dx_all = tuple(bufs[:7]), tuple(bufs[7:15]), bufs[15], bufs[16]
        zero = jnp.zeros((n_seq, d), BF)
        as_idx = lambda c: jnp.reshape(c, (1,)).astype(jnp.int32)

        def forward(t, x_in, saved, y_all):
            c = t - stage
            ok = (c >= 0) & (c < n_chunk)
            c = jnp.clip(c, 0, n_chunk - 1)

            def run(ops):
                x_in, saved, y_all = ops
                first = lax.dynamic_index_in_dim(x_all, c, 0, keepdims=False)
                x = jnp.where(stage == 0, first, x_in)
                y, saved = fwd_call(as_idx(c), x, weights, saved)
                return y, saved, lax.dynamic_update_index_in_dim(y_all, y, c, 0)

            return lax.cond(ok, run, lambda ops: (ops[0], ops[1], ops[2]), (x_in, saved, y_all))

        def backward(t, dy_in, saved, store, dx_all):
            c = t - (2 * last_stage - stage)
            ok = (c >= 0) & (c < n_chunk)
            c = jnp.clip(c, 0, n_chunk - 1)

            def run(ops):
                dy_in, store, dx_all = ops
                top = lax.dynamic_index_in_dim(ct_all, c, 0, keepdims=False)
                dy = jnp.where(stage == last_stage, top, dy_in)
                dx, store = bwd_call(as_idx(c), dy, weights, saved, store)
                return dx, store, lax.dynamic_update_index_in_dim(dx_all, dx, c, 0)

            return lax.cond(ok, run, lambda ops: (ops[0], ops[1], ops[2]), (dy_in, store, dx_all))

        def fill(t, state):
            x_in, saved, y_all = state
            y, saved, y_all = forward(t, x_in, saved, y_all)
            return lax.ppermute(y, 'pp', fwd_pairs), saved, y_all

        def steady(t, state):
            x_in, dx, saved, store, y_all, dx_all = state
            dy_in = lax.ppermute(dx, 'pp', bwd_pairs)
            y, saved, y_all = forward(t, x_in, saved, y_all)
            x_in = lax.ppermute(y, 'pp', fwd_pairs)
            dx, store, dx_all = backward(t, dy_in, saved, store, dx_all)
            return x_in, dx, saved, store, y_all, dx_all

        def drain(t, state):
            dx, store, dx_all = state
            dy_in = lax.ppermute(dx, 'pp', bwd_pairs)
            return backward(t, dy_in, saved, store, dx_all)

        x_in, saved, y_all = lax.fori_loop(0, last_stage, fill, (zero, saved, y_all))
        x_in, dx, saved, store, y_all, dx_all = lax.fori_loop(
            last_stage, last_stage + n_chunk, steady, (x_in, zero, saved, store, y_all, dx_all))
        dx, store, dx_all = lax.fori_loop(
            last_stage + n_chunk, 2 * last_stage + n_chunk, drain, (dx, store, dx_all))

        acts_out = lax.psum(jnp.where(stage == last_stage, y_all, jnp.zeros_like(y_all)), 'pp')
        grad_in = lax.psum(jnp.where(stage == 0, dx_all, jnp.zeros_like(dx_all)), 'pp')
        xs, h1, qkv, mix, x1, h2, pre = saved
        act, dpre, dmid, dqkv, dys, sum_up, sum_qkv, sum_d = store
        wgrad = lambda a, b: jnp.einsum('cka,ckb->ab', a, b, preferred_element_type=F32)
        vec = jnp.sum(sum_d, axis=0)
        grads = (vec[0], vec[1], wgrad(h1, dqkv), jnp.sum(sum_qkv, axis=(0, 1)),
                 wgrad(mix, dmid).reshape(stacked_w[4].shape[1:]), vec[4], vec[2], vec[3],
                 wgrad(h2, dpre), jnp.sum(sum_up, axis=(0, 1)), wgrad(act, dys), vec[5])
        shape4 = acts_in.shape
        return (acts_out.reshape(shape4), grad_in.reshape(shape4)) + tuple(g[None] for g in grads)

    return jax.shard_map(stage_body, mesh=mesh, in_specs=(act_spec, act_spec) + param_specs, out_specs=(act_spec, act_spec) + grad_specs, check_vma=False)
```

time: 9660 us -> 4420 us (0.46)
  waiting for transfers between devices: 3930 us -> 338 us
  matrix products: 3280 us -> 524 us
  Pallas kernels: 0 us -> 2160 us
  local copies, waits for them, and re-layouts: 729 us -> 208 us
  other arithmetic: 598 us -> 127 us
    ppermute x30 -> x46, waiting for transfers between devices: 3370 us -> 298 us  [the longest x7 275 us: drain(): dy_in = lax.ppermute(dx, 'pp', bwd_pairs)]
    dot_general x136 -> x4, matrix products: 3140 us -> 524 us  [stage_body(): jnp.einsum('cka,ckb->ab', a, b, preferred_element_type=F32)]
    pallas_call x0 -> x33, Pallas kernels: none -> 2160 us  [the longest x16 1170 us: bwd_call(): pl.pallas_call(functools.partial(bwd_kernel, n_mlp, n_proj, n_grp, n_qkv)...]
    psum x1, waiting for transfers between devices: 561 us -> 39.3 us  [stage_body(): lax.psum(jnp.where(stage == last_stage, y_all, jnp.zeros_like(y_all)), 'pp')]
    dynamic_update_slice x24 -> x0, other arithmetic: 283 us -> none  [the longest x16 232 us: run_layer(): lax.dynamic_update_index_in_dim(buf_all, buf_new, mb_slot, 0)]
    reduce_sum x72 -> x3, other arithmetic: 253 us -> 1.11 us  [the longest x1 0.88 us: stage_body(): jnp.sum(sum_up, axis=(0, 1))]
    broadcast_in_dim x17 -> x3, local copies, waits for them, and re-layouts: 184 us -> 1.97 us  [the longest x2 1.35 us: stage_body(): zero = jnp.zeros((n_seq, d), BF)]
    sub x8 -> x0, matrix products: 142 us -> none  [layer_forward(): jax.nn.softmax(jnp.where(causal, scores, -1e+30), axis=-1)]
  transfers between devices with their start and end apart: 31 -> 47, of which waited for: 31 -> 22; matrix products, arithmetic and copies ran while one was open for 0% -> 15% of each run, Pallas kernels for 0% -> 28%
where the time goes in v1:
time: 4420 us; the launch traced here: 4400 us
  Pallas kernels  2160 us (49%)
  starting transfers between devices  1020 us (23%)
  matrix products  524 us (12%)
  waiting for transfers between devices  338 us (8%)
  local copies, waits for them, and re-layouts  208 us (5%)
  other arithmetic  127 us (3%)
    pallas_call x16, Pallas kernels, bwd_call(): pl.pallas_call(functools.partial(bwd_kernel, n_mlp, n_proj, n_grp, n_qkv)...  1170 us
    pallas_call x16, Pallas kernels, fwd_call(): pl.pallas_call(functools.partial(fwd_kernel, n_qkv, n_grp, n_proj, n_mlp)...  983 us
    ppermute x16, starting transfers between devices, steady(): x_in = lax.ppermute(y, 'pp', fwd_pairs)  895 us
    dot_general x4, matrix products, stage_body(): jnp.einsum('cka,ckb->ab', a, b, preferred_element_type=F32)  524 us
    ppermute x7, waiting for transfers between devices, drain(): dy_in = lax.ppermute(dx, 'pp', bwd_pairs)  275 us
    ppermute x7, starting transfers between devices, fill(): return (lax.ppermute(y, 'pp', fwd_pairs), saved, y_all)  98.1 us
  transfers between devices with their start and end apart: 47, of which 22 were waited for; matrix products, arithmetic and copies ran while one was open for 15% of the time, Pallas kernels for 28%

profile of v1, /device:TPU:0, one launch (start us, length us, event | category | flops | bytes accessed | tf_op | source)
XLA Modules:
  0.0 4402.3 jit_solution(16807720709438662338)
XLA Ops:
  8.5 594.4 %while.111 = (s32[]{:T(128)}, bf16[512,1536]{1,0:T(8,128)(2,1)}, bf16[16,512,1536]{2,1,0:T(8,128)(2,1)}, bf16[16,512,1536]{2,1,0:T(8,128)(2,1)}, bf16[16,512,460...) while((s32[]{:T(128)}, bf16[512,1536]{1,0:T(8,128)(2,1)}, ...), condition=%wide.region_3.4_spmd, body=%wide.region_0.3_spmd.sunk | while | flops 31000786944 | bytes 107302712 | solution.py:459
  8.5 66.9 %conditional.8 = ((bf16[512,1536]{1,0:T(8,128)(2,1)}, bf16[16,512,1536]{2,1,0:T(8,128)(2,1)}, bf16[16,512,1536]{2,1,0:T(8,128)(2,1)}, bf16[16,512,4608]{2,1,0:T(...) conditional(s32[]{:T(128)} %convert_element_type.35, ...), branch_computations={%region_1.1_spmd, %region_2.2_spmd} | conditional | flops 31000786944 | bytes 97864952 | solution.py:425
  11.3 61.4 %layer_fwd.3 = (bf16[512,1536]{1,0:T(8,128)(2,1)}, bf16[16,512,1536]{2,1,0:T(8,128)(2,1)}, bf16[16,512,1536]{2,1,0:T(8,128)(2,1)}, bf16[16,512,4608]{2,1,0:T(8,1...) custom-call(s32[1]{0:T(128)} %bitcast.idx, ...), custom_call_target="tpu_custom_call", output_to_operand_aliasing={{1}: (14, {}), {2}: (15, {}), {3}: (16, {}), {4}: (17, {}),... | custom-call | flops 31000000512 | bytes 90000000 | tf_op jit(solution)/shard_map/while/body/eval_jaxpr/cond/branch_1_fun/layer_fwd/pallas_call | solution.py:182
  80.9 66.8 %conditional.8 = ((bf16[512,1536]{1,0:T(8,128)(2,1)}, bf16[16,512,1536]{2,1,0:T(8,128)(2,1)}, bf16[16,512,1536]{2,1,0:T(8,128)(2,1)}, bf16[16,512,4608]{2,1,0:T(...) conditional(s32[]{:T(128)} %convert_element_type.35, ...), branch_computations={%region_1.1_spmd, %region_2.2_spmd} | conditional | flops 31000786944 | bytes 97864952 | solution.py:425
  83.6 61.4 %layer_fwd.3 = (bf16[512,1536]{1,0:T(8,128)(2,1)}, bf16[16,512,1536]{2,1,0:T(8,128)(2,1)}, bf16[16,512,1536]{2,1,0:T(8,128)(2,1)}, bf16[16,512,4608]{2,1,0:T(8,1...) custom-call(s32[1]{0:T(128)} %bitcast.idx, ...), custom_call_target="tpu_custom_call", output_to_operand_aliasing={{1}: (14, {}), {2}: (15, {}), {3}: (16, {}), {4}: (17, {}),... | custom-call | flops 31000000512 | bytes 90000000 | tf_op jit(solution)/shard_map/while/body/eval_jaxpr/cond/branch_1_fun/layer_fwd/pallas_call | solution.py:182
  154.6 66.8 %conditional.8 = ((bf16[512,1536]{1,0:T(8,128)(2,1)}, bf16[16,512,1536]{2,1,0:T(8,128)(2,1)}, bf16[16,512,1536]{2,1,0:T(8,128)(2,1)}, bf16[16,512,4608]{2,1,0:T(...) conditional(s32[]{:T(128)} %convert_element_type.35, ...), branch_computations={%region_1.1_spmd, %region_2.2_spmd} | conditional | flops 31000786944 | bytes 97864952 | solution.py:425
  242.3 66.8 %conditional.8 = ((bf16[512,1536]{1,0:T(8,128)(2,1)}, bf16[16,512,1536]{2,1,0:T(8,128)(2,1)}, bf16[16,512,1536]{2,1,0:T(8,128)(2,1)}, bf16[16,512,4608]{2,1,0:T(...) conditional(s32[]{:T(128)} %convert_element_type.35, ...), branch_computations={%region_1.1_spmd, %region_2.2_spmd} | conditional | flops 31000786944 | bytes 97864952 | solution.py:425
  332.4 66.8 %conditional.8 = ((bf16[512,1536]{1,0:T(8,128)(2,1)}, bf16[16,512,1536]{2,1,0:T(8,128)(2,1)}, bf16[16,512,1536]{2,1,0:T(8,128)(2,1)}, bf16[16,512,4608]{2,1,0:T(...) conditional(s32[]{:T(128)} %convert_element_type.35, ...), branch_computations={%region_1.1_spmd, %region_2.2_spmd} | conditional | flops 31000786944 | bytes 97864952 | solution.py:425
  335.1 61.5 %layer_fwd.3 = (bf16[512,1536]{1,0:T(8,128)(2,1)}, bf16[16,512,1536]{2,1,0:T(8,128)(2,1)}, bf16[16,512,1536]{2,1,0:T(8,128)(2,1)}, bf16[16,512,4608]{2,1,0:T(8,1...) custom-call(s32[1]{0:T(128)} %bitcast.idx, ...), custom_call_target="tpu_custom_call", output_to_operand_aliasing={{1}: (14, {}), {2}: (15, {}), {3}: (16, {}), {4}: (17, {}),... | custom-call | flops 31000000512 | bytes 90000000 | tf_op jit(solution)/shard_map/while/body/eval_jaxpr/cond/branch_1_fun/layer_fwd/pallas_call | solution.py:182
  422.6 66.9 %conditional.8 = ((bf16[512,1536]{1,0:T(8,128)(2,1)}, bf16[16,512,1536]{2,1,0:T(8,128)(2,1)}, bf16[16,512,1536]{2,1,0:T(8,128)(2,1)}, bf16[16,512,4608]{2,1,0:T(...) conditional(s32[]{:T(128)} %convert_element_type.35, ...), branch_computations={%region_1.1_spmd, %region_2.2_spmd} | conditional | flops 31000786944 | bytes 97864952 | solution.py:425
  425.3 61.5 %layer_fwd.3 = (bf16[512,1536]{1,0:T(8,128)(2,1)}, bf16[16,512,1536]{2,1,0:T(8,128)(2,1)}, bf16[16,512,1536]{2,1,0:T(8,128)(2,1)}, bf16[16,512,4608]{2,1,0:T(8,1...) custom-call(s32[1]{0:T(128)} %bitcast.idx, ...), custom_call_target="tpu_custom_call", output_to_operand_aliasing={{1}: (14, {}), {2}: (15, {}), {3}: (16, {}), {4}: (17, {}),... | custom-call | flops 31000000512 | bytes 90000000 | tf_op jit(solution)/shard_map/while/body/eval_jaxpr/cond/branch_1_fun/layer_fwd/pallas_call | solution.py:182
  512.7 66.8 %conditional.8 = ((bf16[512,1536]{1,0:T(8,128)(2,1)}, bf16[16,512,1536]{2,1,0:T(8,128)(2,1)}, bf16[16,512,1536]{2,1,0:T(8,128)(2,1)}, bf16[16,512,4608]{2,1,0:T(...) conditional(s32[]{:T(128)} %convert_element_type.35, ...), branch_computations={%region_1.1_spmd, %region_2.2_spmd} | conditional | flops 31000786944 | bytes 97864952 | solution.py:425
  603.0 2309.3 %while.112 = (s32[]{:T(128)}, bf16[512,1536]{1,0:T(8,128)(2,1)}, bf16[512,1536]{1,0:T(8,128)(2,1)S(1)}, bf16[16,512,1536]{2,1,0:T(8,128)(2,1)}, bf16[16,512,1536...) while((s32[]{:T(128)}, bf16[512,1536]{1,0:T(8,128)(2,1)}, ...), condition=%wide.region_9.10_spmd, body=%wide.region_4.9_spmd.sunk | while | flops 67001573376 | bytes 234605328 | solution.py:460
  604.6 66.8 %conditional.9 = ((bf16[512,1536]{1,0:T(8,128)(2,1)}, bf16[16,512,1536]{2,1,0:T(8,128)(2,1)}, bf16[16,512,1536]{2,1,0:T(8,128)(2,1)}, bf16[16,512,4608]{2,1,0:T(...) conditional(s32[]{:T(128)} %convert_element_type.36, ...), branch_computations={%region_5.5_spmd, %region_6.6_spmd} | conditional | flops 31000786944 | bytes 97864952 | solution.py:425
  698.2 66.8 %conditional.9 = ((bf16[512,1536]{1,0:T(8,128)(2,1)}, bf16[16,512,1536]{2,1,0:T(8,128)(2,1)}, bf16[16,512,1536]{2,1,0:T(8,128)(2,1)}, bf16[16,512,4608]{2,1,0:T(...) conditional(s32[]{:T(128)} %convert_element_type.36, ...), branch_computations={%region_5.5_spmd, %region_6.6_spmd} | conditional | flops 31000786944 | bytes 97864952 | solution.py:425
  791.9 66.8 %conditional.9 = ((bf16[512,1536]{1,0:T(8,128)(2,1)}, bf16[16,512,1536]{2,1,0:T(8,128)(2,1)}, bf16[16,512,1536]{2,1,0:T(8,128)(2,1)}, bf16[16,512,4608]{2,1,0:T(...) conditional(s32[]{:T(128)} %convert_element_type.36, ...), branch_computations={%region_5.5_spmd, %region_6.6_spmd} | conditional | flops 31000786944 | bytes 97864952 | solution.py:425
  885.5 66.8 %conditional.9 = ((bf16[512,1536]{1,0:T(8,128)(2,1)}, bf16[16,512,1536]{2,1,0:T(8,128)(2,1)}, bf16[16,512,1536]{2,1,0:T(8,128)(2,1)}, bf16[16,512,4608]{2,1,0:T(...) conditional(s32[]{:T(128)} %convert_element_type.36, ...), branch_computations={%region_5.5_spmd, %region_6.6_spmd} | conditional | flops 31000786944 | bytes 97864952 | solution.py:425
  979.1 66.8 %conditional.9 = ((bf16[512,1536]{1,0:T(8,128)(2,1)}, bf16[16,512,1536]{2,1,0:T(8,128)(2,1)}, bf16[16,512,1536]{2,1,0:T(8,128)(2,1)}, bf16[16,512,4608]{2,1,0:T(...) conditional(s32[]{:T(128)} %convert_element_type.36, ...), branch_computations={%region_5.5_spmd, %region_6.6_spmd} | conditional | flops 31000786944 | bytes 97864952 | solution.py:425
  1072.7 66.8 %conditional.9 = ((bf16[512,1536]{1,0:T(8,128)(2,1)}, bf16[16,512,1536]{2,1,0:T(8,128)(2,1)}, bf16[16,512,1536]{2,1,0:T(8,128)(2,1)}, bf16[16,512,4608]{2,1,0:T(...) conditional(s32[]{:T(128)} %convert_element_type.36, ...), branch_computations={%region_5.5_spmd, %region_6.6_spmd} | conditional | flops 31000786944 | bytes 97864952 | solution.py:425
  1166.2 66.8 %conditional.9 = ((bf16[512,1536]{1,0:T(8,128)(2,1)}, bf16[16,512,1536]{2,1,0:T(8,128)(2,1)}, bf16[16,512,1536]{2,1,0:T(8,128)(2,1)}, bf16[16,512,4608]{2,1,0:T(...) conditional(s32[]{:T(128)} %convert_element_type.36, ...), branch_computations={%region_5.5_spmd, %region_6.6_spmd} | conditional | flops 31000786944 | bytes 97864952 | solution.py:425
  1259.8 66.8 %conditional.9 = ((bf16[512,1536]{1,0:T(8,128)(2,1)}, bf16[16,512,1536]{2,1,0:T(8,128)(2,1)}, bf16[16,512,1536]{2,1,0:T(8,128)(2,1)}, bf16[16,512,4608]{2,1,0:T(...) conditional(s32[]{:T(128)} %convert_element_type.36, ...), branch_computations={%region_5.5_spmd, %region_6.6_spmd} | conditional | flops 31000786944 | bytes 97864952 | solution.py:425
  1326.6 419.6 %collective-permute-start.1 = (bf16[512,1536]{1,0:T(8,128)(2,1)}, bf16[512,1536]{1,0:T(8,128)(2,1)}, u32[]{:S(2)}, u32[]{:S(2)}) collective-permute-start(bf16[512,1536]{1,0:T(8,128)(2,1)} %get-tuple-element.2961), channel_id=1, source_target_pairs={{0,1},{1,2},{2,3},{3,4},{4,5},{5,6},{6,7}} | collective-permute-start | bytes 4718600 | tf_op jit(solution)/shard_map/while/body/eval_jaxpr/ppermute | solution.py:450
  1746.3 79.2 %conditional.10 = ((bf16[512,1536]{1,0:T(8,128)(2,1)}, bf16[16,512,6144]{2,1,0:T(8,128)(2,1)}, bf16[16,512,6144]{2,1,0:T(8,128)(2,1)}, bf16[16,512,1536]{2,1,0:T...) conditional(s32[]{:T(128)} %convert_element_type.37, ...), branch_computations={%region_7.7_spmd, %region_8.8_spmd} | conditional | flops 36000784384 | bytes 117864960 | solution.py:439
  1749.5 73.3 %layer_bwd.3 = (bf16[512,1536]{1,0:T(8,128)(2,1)}, bf16[16,512,6144]{2,1,0:T(8,128)(2,1)}, bf16[16,512,6144]{2,1,0:T(8,128)(2,1)}, bf16[16,512,1536]{2,1,0:T(8,1...) custom-call(s32[1]{0:T(128)} %bitcast.8.idx, ...), custom_call_target="tpu_custom_call", output_to_operand_aliasing={{1}: (14, {}), {2}: (15, {}), {3}: (16, {}), {4}: (17, {}),... | custom-call | flops 35999997952 | bytes 110000000 | tf_op jit(solution)/shard_map/while/body/eval_jaxpr/cond/branch_1_fun/layer_bwd/pallas_call | solution.py:362
  1830.8 66.8 %conditional.9 = ((bf16[512,1536]{1,0:T(8,128)(2,1)}, bf16[16,512,1536]{2,1,0:T(8,128)(2,1)}, bf16[16,512,1536]{2,1,0:T(8,128)(2,1)}, bf16[16,512,4608]{2,1,0:T(...) conditional(s32[]{:T(128)} %convert_element_type.36, ...), branch_computations={%region_5.5_spmd, %region_6.6_spmd} | conditional | flops 31000786944 | bytes 97864952 | solution.py:425
  1903.2 79.2 %conditional.10 = ((bf16[512,1536]{1,0:T(8,128)(2,1)}, bf16[16,512,6144]{2,1,0:T(8,128)(2,1)}, bf16[16,512,6144]{2,1,0:T(8,128)(2,1)}, bf16[16,512,1536]{2,1,0:T...) conditional(s32[]{:T(128)} %convert_element_type.37, ...), branch_computations={%region_7.7_spmd, %region_8.8_spmd} | conditional | flops 36000784384 | bytes 117864960 | solution.py:439
  1906.4 73.3 %layer_bwd.3 = (bf16[512,1536]{1,0:T(8,128)(2,1)}, bf16[16,512,6144]{2,1,0:T(8,128)(2,1)}, bf16[16,512,6144]{2,1,0:T(8,128)(2,1)}, bf16[16,512,1536]{2,1,0:T(8,1...) custom-call(s32[1]{0:T(128)} %bitcast.8.idx, ...), custom_call_target="tpu_custom_call", output_to_operand_aliasing={{1}: (14, {}), {2}: (15, {}), {3}: (16, {}), {4}: (17, {}),... | custom-call | flops 35999997952 | bytes 110000000 | tf_op jit(solution)/shard_map/while/body/eval_jaxpr/cond/branch_1_fun/layer_bwd/pallas_call | solution.py:362
  1987.8 72.6 %collective-permute-start.1 = (bf16[512,1536]{1,0:T(8,128)(2,1)}, bf16[512,1536]{1,0:T(8,128)(2,1)}, u32[]{:S(2)}, u32[]{:S(2)}) collective-permute-start(bf16[512,1536]{1,0:T(8,128)(2,1)} %get-tuple-element.2961), channel_id=1, source_target_pairs={{0,1},{1,2},{2,3},{3,4},{4,5},{5,6},{6,7}} | collective-permute-start | bytes 4718600 | tf_op jit(solution)/shard_map/while/body/eval_jaxpr/ppermute | solution.py:450
  2060.4 79.2 %conditional.10 = ((bf16[512,1536]{1,0:T(8,128)(2,1)}, bf16[16,512,6144]{2,1,0:T(8,128)(2,1)}, bf16[16,512,6144]{2,1,0:T(8,128)(2,1)}, bf16[16,512,1536]{2,1,0:T...) conditional(s32[]{:T(128)} %convert_element_type.37, ...), branch_computations={%region_7.7_spmd, %region_8.8_spmd} | conditional | flops 36000784384 | bytes 117864960 | solution.py:439
  2063.6 73.3 %layer_bwd.3 = (bf16[512,1536]{1,0:T(8,128)(2,1)}, bf16[16,512,6144]{2,1,0:T(8,128)(2,1)}, bf16[16,512,6144]{2,1,0:T(8,128)(2,1)}, bf16[16,512,1536]{2,1,0:T(8,1...) custom-call(s32[1]{0:T(128)} %bitcast.8.idx, ...), custom_call_target="tpu_custom_call", output_to_operand_aliasing={{1}: (14, {}), {2}: (15, {}), {3}: (16, {}), {4}: (17, {}),... | custom-call | flops 35999997952 | bytes 110000000 | tf_op jit(solution)/shard_map/while/body/eval_jaxpr/cond/branch_1_fun/layer_bwd/pallas_call | solution.py:362
  2150.2 79.2 %conditional.10 = ((bf16[512,1536]{1,0:T(8,128)(2,1)}, bf16[16,512,6144]{2,1,0:T(8,128)(2,1)}, bf16[16,512,6144]{2,1,0:T(8,128)(2,1)}, bf16[16,512,1536]{2,1,0:T...) conditional(s32[]{:T(128)} %convert_element_type.37, ...), branch_computations={%region_7.7_spmd, %region_8.8_spmd} | conditional | flops 36000784384 | bytes 117864960 | solution.py:439
  2153.4 73.3 %layer_bwd.3 = (bf16[512,1536]{1,0:T(8,128)(2,1)}, bf16[16,512,6144]{2,1,0:T(8,128)(2,1)}, bf16[16,512,6144]{2,1,0:T(8,128)(2,1)}, bf16[16,512,1536]{2,1,0:T(8,1...) custom-call(s32[1]{0:T(128)} %bitcast.8.idx, ...), custom_call_target="tpu_custom_call", output_to_operand_aliasing={{1}: (14, {}), {2}: (15, {}), {3}: (16, {}), {4}: (17, {}),... | custom-call | flops 35999997952 | bytes 110000000 | tf_op jit(solution)/shard_map/while/body/eval_jaxpr/cond/branch_1_fun/layer_bwd/pallas_call | solution.py:362
  2234.8 72.2 %collective-permute-start.1 = (bf16[512,1536]{1,0:T(8,128)(2,1)}, bf16[512,1536]{1,0:T(8,128)(2,1)}, u32[]{:S(2)}, u32[]{:S(2)}) collective-permute-start(bf16[512,1536]{1,0:T(8,128)(2,1)} %get-tuple-element.2961), channel_id=1, source_target_pairs={{0,1},{1,2},{2,3},{3,4},{4,5},{5,6},{6,7}} | collective-permute-start | bytes 4718600 | tf_op jit(solution)/shard_map/while/body/eval_jaxpr/ppermute | solution.py:450
  2307.0 79.1 %conditional.10 = ((bf16[512,1536]{1,0:T(8,128)(2,1)}, bf16[16,512,6144]{2,1,0:T(8,128)(2,1)}, bf16[16,512,6144]{2,1,0:T(8,128)(2,1)}, bf16[16,512,1536]{2,1,0:T...) conditional(s32[]{:T(128)} %convert_element_type.37, ...), branch_computations={%region_7.7_spmd, %region_8.8_spmd} | conditional | flops 36000784384 | bytes 117864960 | solution.py:439
  2310.2 73.2 %layer_bwd.3 = (bf16[512,1536]{1,0:T(8,128)(2,1)}, bf16[16,512,6144]{2,1,0:T(8,128)(2,1)}, bf16[16,512,6144]{2,1,0:T(8,128)(2,1)}, bf16[16,512,1536]{2,1,0:T(8,1...) custom-call(s32[1]{0:T(128)} %bitcast.8.idx, ...), custom_call_target="tpu_custom_call", output_to_operand_aliasing={{1}: (14, {}), {2}: (15, {}), {3}: (16, {}), {4}: (17, {}),... | custom-call | flops 35999997952 | bytes 110000000 | tf_op jit(solution)/shard_map/while/body/eval_jaxpr/cond/branch_1_fun/layer_bwd/pallas_call | solution.py:362
  2413.3 79.3 %conditional.10 = ((bf16[512,1536]{1,0:T(8,128)(2,1)}, bf16[16,512,6144]{2,1,0:T(8,128)(2,1)}, bf16[16,512,6144]{2,1,0:T(8,128)(2,1)}, bf16[16,512,1536]{2,1,0:T...) conditional(s32[]{:T(128)} %convert_element_type.37, ...), branch_computations={%region_7.7_spmd, %region_8.8_spmd} | conditional | flops 36000784384 | bytes 117864960 | solution.py:439
  2416.5 73.3 %layer_bwd.3 = (bf16[512,1536]{1,0:T(8,128)(2,1)}, bf16[16,512,6144]{2,1,0:T(8,128)(2,1)}, bf16[16,512,6144]{2,1,0:T(8,128)(2,1)}, bf16[16,512,1536]{2,1,0:T(8,1...) custom-call(s32[1]{0:T(128)} %bitcast.8.idx, ...), custom_call_target="tpu_custom_call", output_to_operand_aliasing={{1}: (14, {}), {2}: (15, {}), {3}: (16, {}), {4}: (17, {}),... | custom-call | flops 35999997952 | bytes 110000000 | tf_op jit(solution)/shard_map/while/body/eval_jaxpr/cond/branch_1_fun/layer_bwd/pallas_call | solution.py:362
  2498.0 72.0 %collective-permute-start.1 = (bf16[512,1536]{1,0:T(8,128)(2,1)}, bf16[512,1536]{1,0:T(8,128)(2,1)}, u32[]{:S(2)}, u32[]{:S(2)}) collective-permute-start(bf16[512,1536]{1,0:T(8,128)(2,1)} %get-tuple-element.2961), channel_id=1, source_target_pairs={{0,1},{1,2},{2,3},{3,4},{4,5},{5,6},{6,7}} | collective-permute-start | bytes 4718600 | tf_op jit(solution)/shard_map/while/body/eval_jaxpr/ppermute | solution.py:450
  2570.0 79.1 %conditional.10 = ((bf16[512,1536]{1,0:T(8,128)(2,1)}, bf16[16,512,6144]{2,1,0:T(8,128)(2,1)}, bf16[16,512,6144]{2,1,0:T(8,128)(2,1)}, bf16[16,512,1536]{2,1,0:T...) conditional(s32[]{:T(128)} %convert_element_type.37, ...), branch_computations={%region_7.7_spmd, %region_8.8_spmd} | conditional | flops 36000784384 | bytes 117864960 | solution.py:439
  2573.2 73.3 %layer_bwd.3 = (bf16[512,1536]{1,0:T(8,128)(2,1)}, bf16[16,512,6144]{2,1,0:T(8,128)(2,1)}, bf16[16,512,6144]{2,1,0:T(8,128)(2,1)}, bf16[16,512,1536]{2,1,0:T(8,1...) custom-call(s32[1]{0:T(128)} %bitcast.8.idx, ...), custom_call_target="tpu_custom_call", output_to_operand_aliasing={{1}: (14, {}), {2}: (15, {}), {3}: (16, {}), {4}: (17, {}),... | custom-call | flops 35999997952 | bytes 110000000 | tf_op jit(solution)/shard_map/while/body/eval_jaxpr/cond/branch_1_fun/layer_bwd/pallas_call | solution.py:362
  2674.9 79.2 %conditional.10 = ((bf16[512,1536]{1,0:T(8,128)(2,1)}, bf16[16,512,6144]{2,1,0:T(8,128)(2,1)}, bf16[16,512,6144]{2,1,0:T(8,128)(2,1)}, bf16[16,512,1536]{2,1,0:T...) conditional(s32[]{:T(128)} %convert_element_type.37, ...), branch_computations={%region_7.7_spmd, %region_8.8_spmd} | conditional | flops 36000784384 | bytes 117864960 | solution.py:439
  2678.2 73.3 %layer_bwd.3 = (bf16[512,1536]{1,0:T(8,128)(2,1)}, bf16[16,512,6144]{2,1,0:T(8,128)(2,1)}, bf16[16,512,6144]{2,1,0:T(8,128)(2,1)}, bf16[16,512,1536]{2,1,0:T(8,1...) custom-call(s32[1]{0:T(128)} %bitcast.8.idx, ...), custom_call_target="tpu_custom_call", output_to_operand_aliasing={{1}: (14, {}), {2}: (15, {}), {3}: (16, {}), {4}: (17, {}),... | custom-call | flops 35999997952 | bytes 110000000 | tf_op jit(solution)/shard_map/while/body/eval_jaxpr/cond/branch_1_fun/layer_bwd/pallas_call | solution.py:362
  2818.3 79.3 %conditional.10 = ((bf16[512,1536]{1,0:T(8,128)(2,1)}, bf16[16,512,6144]{2,1,0:T(8,128)(2,1)}, bf16[16,512,6144]{2,1,0:T(8,128)(2,1)}, bf16[16,512,1536]{2,1,0:T...) conditional(s32[]{:T(128)} %convert_element_type.37, ...), branch_computations={%region_7.7_spmd, %region_8.8_spmd} | conditional | flops 36000784384 | bytes 117864960 | solution.py:439
  2821.5 73.4 %layer_bwd.3 = (bf16[512,1536]{1,0:T(8,128)(2,1)}, bf16[16,512,6144]{2,1,0:T(8,128)(2,1)}, bf16[16,512,6144]{2,1,0:T(8,128)(2,1)}, bf16[16,512,1536]{2,1,0:T(8,1...) custom-call(s32[1]{0:T(128)} %bitcast.8.idx, ...), custom_call_target="tpu_custom_call", output_to_operand_aliasing={{1}: (14, {}), {2}: (15, {}), {3}: (16, {}), {4}: (17, {}),... | custom-call | flops 35999997952 | bytes 110000000 | tf_op jit(solution)/shard_map/while/body/eval_jaxpr/cond/branch_1_fun/layer_bwd/pallas_call | solution.py:362
  2912.3 848.3 %while.113 = (s32[]{:T(128)}, bf16[512,1536]{1,0:T(8,128)(2,1)S(1)}, bf16[16,512,6144]{2,1,0:T(8,128)(2,1)}, bf16[16,512,6144]{2,1,0:T(8,128)(2,1)}, bf16[16,512...) while((s32[]{:T(128)}, bf16[512,1536]{1,0:T(8,128)(2,1)S(1)}, ...), condition=%wide.region_14.15_spmd, body=%wide.region_11.14_spmd.sunk | while | flops 36000784384 | bytes 127302744 | solution.py:462
  2934.3 79.1 %conditional.11 = ((bf16[512,1536]{1,0:T(8,128)(2,1)}, bf16[16,512,6144]{2,1,0:T(8,128)(2,1)}, bf16[16,512,6144]{2,1,0:T(8,128)(2,1)}, bf16[16,512,1536]{2,1,0:T...) conditional(s32[]{:T(128)} %convert_element_type.38, ...), branch_computations={%region_12.12_spmd, %region_13.13_spmd} | conditional | flops 36000784384 | bytes 117864960 | solution.py:439
  2937.5 73.2 %layer_bwd.4 = (bf16[512,1536]{1,0:T(8,128)(2,1)}, bf16[16,512,6144]{2,1,0:T(8,128)(2,1)}, bf16[16,512,6144]{2,1,0:T(8,128)(2,1)}, bf16[16,512,1536]{2,1,0:T(8,1...) custom-call(s32[1]{0:T(128)} %bitcast.12.idx, ...), custom_call_target="tpu_custom_call", output_to_operand_aliasing={{1}: (14, {}), {2}: (15, {}), {3}: (16, {}), {4}: (17, {}),... | custom-call | flops 35999997952 | bytes 110000000 | tf_op jit(solution)/shard_map/while/body/eval_jaxpr/cond/branch_1_fun/layer_bwd/pallas_call | solution.py:362
  3016.1 67.9 %collective-permute-done.3 = bf16[512,1536]{1,0:T(8,128)(2,1)} collective-permute-done((bf16[512,1536]{1,0:T(8,128)(2,1)S(1)}, bf16[512,1536]{1,0:T(8,128)(2,1)}, u32[]{:S(2)}, u32[]{:S(2)}) %collective-permute-start.3) | collective-permute-done | bytes 1572896 | tf_op jit(solution)/shard_map/while/body/eval_jaxpr/ppermute | solution.py:456
  3084.0 79.2 %conditional.11 = ((bf16[512,1536]{1,0:T(8,128)(2,1)}, bf16[16,512,6144]{2,1,0:T(8,128)(2,1)}, bf16[16,512,6144]{2,1,0:T(8,128)(2,1)}, bf16[16,512,1536]{2,1,0:T...) conditional(s32[]{:T(128)} %convert_element_type.38, ...), branch_computations={%region_12.12_spmd, %region_13.13_spmd} | conditional | flops 36000784384 | bytes 117864960 | solution.py:439
  3087.2 73.3 %layer_bwd.4 = (bf16[512,1536]{1,0:T(8,128)(2,1)}, bf16[16,512,6144]{2,1,0:T(8,128)(2,1)}, bf16[16,512,6144]{2,1,0:T(8,128)(2,1)}, bf16[16,512,1536]{2,1,0:T(8,1...) custom-call(s32[1]{0:T(128)} %bitcast.12.idx, ...), custom_call_target="tpu_custom_call", output_to_operand_aliasing={{1}: (14, {}), {2}: (15, {}), {3}: (16, {}), {4}: (17, {}),... | custom-call | flops 35999997952 | bytes 110000000 | tf_op jit(solution)/shard_map/while/body/eval_jaxpr/cond/branch_1_fun/layer_bwd/pallas_call | solution.py:362
  3187.2 79.2 %conditional.11 = ((bf16[512,1536]{1,0:T(8,128)(2,1)}, bf16[16,512,6144]{2,1,0:T(8,128)(2,1)}, bf16[16,512,6144]{2,1,0:T(8,128)(2,1)}, bf16[16,512,1536]{2,1,0:T...) conditional(s32[]{:T(128)} %convert_element_type.38, ...), branch_computations={%region_12.12_spmd, %region_13.13_spmd} | conditional | flops 36000784384 | bytes 117864960 | solution.py:439
  3190.4 73.3 %layer_bwd.4 = (bf16[512,1536]{1,0:T(8,128)(2,1)}, bf16[16,512,6144]{2,1,0:T(8,128)(2,1)}, bf16[16,512,6144]{2,1,0:T(8,128)(2,1)}, bf16[16,512,1536]{2,1,0:T(8,1...) custom-call(s32[1]{0:T(128)} %bitcast.12.idx, ...), custom_call_target="tpu_custom_call", output_to_operand_aliasing={{1}: (14, {}), {2}: (15, {}), {3}: (16, {}), {4}: (17, {}),... | custom-call | flops 35999997952 | bytes 110000000 | tf_op jit(solution)/shard_map/while/body/eval_jaxpr/cond/branch_1_fun/layer_bwd/pallas_call | solution.py:362
  3322.2 79.1 %conditional.11 = ((bf16[512,1536]{1,0:T(8,128)(2,1)}, bf16[16,512,6144]{2,1,0:T(8,128)(2,1)}, bf16[16,512,6144]{2,1,0:T(8,128)(2,1)}, bf16[16,512,1536]{2,1,0:T...) conditional(s32[]{:T(128)} %convert_element_type.38, ...), branch_computations={%region_12.12_spmd, %region_13.13_spmd} | conditional | flops 36000784384 | bytes 117864960 | solution.py:439
  3325.4 73.3 %layer_bwd.4 = (bf16[512,1536]{1,0:T(8,128)(2,1)}, bf16[16,512,6144]{2,1,0:T(8,128)(2,1)}, bf16[16,512,6144]{2,1,0:T(8,128)(2,1)}, bf16[16,512,1536]{2,1,0:T(8,1...) custom-call(s32[1]{0:T(128)} %bitcast.12.idx, ...), custom_call_target="tpu_custom_call", output_to_operand_aliasing={{1}: (14, {}), {2}: (15, {}), {3}: (16, {}), {4}: (17, {}),... | custom-call | flops 35999997952 | bytes 110000000 | tf_op jit(solution)/shard_map/while/body/eval_jaxpr/cond/branch_1_fun/layer_bwd/pallas_call | solution.py:362
  3425.9 79.3 %conditional.11 = ((bf16[512,1536]{1,0:T(8,128)(2,1)}, bf16[16,512,6144]{2,1,0:T(8,128)(2,1)}, bf16[16,512,6144]{2,1,0:T(8,128)(2,1)}, bf16[16,512,1536]{2,1,0:T...) conditional(s32[]{:T(128)} %convert_element_type.38, ...), branch_computations={%region_12.12_spmd, %region_13.13_spmd} | conditional | flops 36000784384 | bytes 117864960 | solution.py:439
  3429.1 73.4 %layer_bwd.4 = (bf16[512,1536]{1,0:T(8,128)(2,1)}, bf16[16,512,6144]{2,1,0:T(8,128)(2,1)}, bf16[16,512,6144]{2,1,0:T(8,128)(2,1)}, bf16[16,512,1536]{2,1,0:T(8,1...) custom-call(s32[1]{0:T(128)} %bitcast.12.idx, ...), custom_call_target="tpu_custom_call", output_to_operand_aliasing={{1}: (14, {}), {2}: (15, {}), {3}: (16, {}), {4}: (17, {}),... | custom-call | flops 35999997952 | bytes 110000000 | tf_op jit(solution)/shard_map/while/body/eval_jaxpr/cond/branch_1_fun/layer_bwd/pallas_call | solution.py:362
  3507.9 68.1 %collective-permute-done.3 = bf16[512,1536]{1,0:T(8,128)(2,1)} collective-permute-done((bf16[512,1536]{1,0:T(8,128)(2,1)S(1)}, bf16[512,1536]{1,0:T(8,128)(2,1)}, u32[]{:S(2)}, u32[]{:S(2)}) %collective-permute-start.3) | collective-permute-done | bytes 1572896 | tf_op jit(solution)/shard_map/while/body/eval_jaxpr/ppermute | solution.py:456
  3576.0 79.1 %conditional.11 = ((bf16[512,1536]{1,0:T(8,128)(2,1)}, bf16[16,512,6144]{2,1,0:T(8,128)(2,1)}, bf16[16,512,6144]{2,1,0:T(8,128)(2,1)}, bf16[16,512,1536]{2,1,0:T...) conditional(s32[]{:T(128)} %convert_element_type.38, ...), branch_computations={%region_12.12_spmd, %region_13.13_spmd} | conditional | flops 36000784384 | bytes 117864960 | solution.py:439
  3579.2 73.2 %layer_bwd.4 = (bf16[512,1536]{1,0:T(8,128)(2,1)}, bf16[16,512,6144]{2,1,0:T(8,128)(2,1)}, bf16[16,512,6144]{2,1,0:T(8,128)(2,1)}, bf16[16,512,1536]{2,1,0:T(8,1...) custom-call(s32[1]{0:T(128)} %bitcast.12.idx, ...), custom_call_target="tpu_custom_call", output_to_operand_aliasing={{1}: (14, {}), {2}: (15, {}), {3}: (16, {}), {4}: (17, {}),... | custom-call | flops 35999997952 | bytes 110000000 | tf_op jit(solution)/shard_map/while/body/eval_jaxpr/cond/branch_1_fun/layer_bwd/pallas_call | solution.py:362
  3679.6 79.2 %conditional.11 = ((bf16[512,1536]{1,0:T(8,128)(2,1)}, bf16[16,512,6144]{2,1,0:T(8,128)(2,1)}, bf16[16,512,6144]{2,1,0:T(8,128)(2,1)}, bf16[16,512,1536]{2,1,0:T...) conditional(s32[]{:T(128)} %convert_element_type.38, ...), branch_computations={%region_12.12_spmd, %region_13.13_spmd} | conditional | flops 36000784384 | bytes 117864960 | solution.py:439
  3682.8 73.3 %layer_bwd.4 = (bf16[512,1536]{1,0:T(8,128)(2,1)}, bf16[16,512,6144]{2,1,0:T(8,128)(2,1)}, bf16[16,512,6144]{2,1,0:T(8,128)(2,1)}, bf16[16,512,1536]{2,1,0:T(8,1...) custom-call(s32[1]{0:T(128)} %bitcast.12.idx, ...), custom_call_target="tpu_custom_call", output_to_operand_aliasing={{1}: (14, {}), {2}: (15, {}), {3}: (16, {}), {4}: (17, {}),... | custom-call | flops 35999997952 | bytes 110000000 | tf_op jit(solution)/shard_map/while/body/eval_jaxpr/cond/branch_1_fun/layer_bwd/pallas_call | solution.py:362
  3797.5 171.7 %convolution_bitcast_fusion = f32[1,6144,1536]{2,1,0:T(8,128)} fusion(bf16[16,512,6144]{2,1,0:T(8,128)(2,1)} %get-tuple-element.2253, bf16[16,512,1536]{2,1,0:T(8,128)(2,1)} %get-tuple-element.2254), kind=kOutput, calls=%fused_computation.8 | convolution fusion | flops 154618822656 | bytes 163577856 | tf_op jit(solution)/shard_map/cka,ckb->ab/dot_general | solution.py:469
  3969.2 171.8 %convolution_bitcast_fusion.1 = f32[1,1536,6144]{2,1,0:T(8,128)} fusion(bf16[16,512,1536]{2,1,0:T(8,128)(2,1)} %get-tuple-element.2250, bf16[16,512,6144]{2,1,0:T(8,128)(2,1)} %get-tuple-element.2251), kind=kOutput, calls=%fused_computation.9 | convolution fusion | flops 154618822656 | bytes 163577856 | tf_op jit(solution)/shard_map/cka,ckb->ab/dot_general | solution.py:469
  4189.7 132.1 %convolution_bitcast_fusion.2 = f32[1,1536,4608]{2,1,0:T(8,128)} fusion(bf16[16,512,1536]{2,1,0:T(8,128)(2,1)} %get-tuple-element.2245, bf16[16,512,4608]{2,1,0:T(8,128)(2,1)} %get-tuple-element.2246), kind=kOutput, calls=%fused_computation.12 | convolution fusion | flops 115964116992 | bytes 128974848 | tf_op jit(solution)/shard_map/cka,ckb->ab/dot_general | solution.py:469
  (248 shorter events, 1708.7 us)
Async XLA Ops:
  7.2 4353.9 %all-reduce.3.cloned.1.call-start = ((), (), s32[]{:S(2)}) async-start(), calls=%async_computation | async-start | bytes 100663296 | tf_op jit(solution)/shard_map/psum | solution.py:465
  8.5 594.5 %copy-start = (f32[16,8,1536]{2,1,0:T(8,128)S(1)}, f32[16,8,1536]{2,1,0:T(8,128)}, u32[]{:S(2)}) copy-start(f32[16,8,1536]{2,1,0:T(8,128)} %get-tuple-element.3188) | copy-start | bytes 2359300
  8.5 594.5 %copy-start.1 = (f32[16,1,6144]{2,1,0:T(1,128)S(1)}, f32[16,1,6144]{2,1,0:T(1,128)}, u32[]{:S(2)}) copy-start(f32[16,1,6144]{2,1,0:T(1,128)} %get-tuple-element.3186) | copy-start | bytes 1179652
  8.5 594.5 %copy-start.2 = (f32[16,1,4608]{2,1,0:T(1,128)S(1)}, f32[16,1,4608]{2,1,0:T(1,128)}, u32[]{:S(2)}) copy-start(f32[16,1,4608]{2,1,0:T(1,128)} %get-tuple-element.3187) | copy-start | bytes 884740
  75.4 4.3 collective-permute-start
  147.7 5.8 collective-permute-start
  221.4 19.8 collective-permute-start
  309.1 22.2 collective-permute-start
  399.2 22.2 collective-permute-start
  489.5 22.1 collective-permute-start
  579.5 22.2 collective-permute-start
  603.3 89.0 %collective-permute-start.2 = (bf16[512,1536]{1,0:T(8,128)(2,1)S(1)}, bf16[512,1536]{1,0:T(8,128)(2,1)}, u32[]{:S(2)}, u32[]{:S(2)}) collective-permute-start(bf16[512,1536]{1,0:T(8,128)(2,1)S(1)} %get-tuple-element.3213), channel_id=1, source_target_pairs={{1,0},{2,1},{3,2},{4,3},{5,4},{6,5},{7,6}} | collective-permute-start | bytes 4718600 | tf_op jit(solution)/shard_map/while/body/eval_jaxpr/ppermute | solution.py:448
  671.4 22.8 collective-permute-start.1
  696.9 89.1 %collective-permute-start.2 = (bf16[512,1536]{1,0:T(8,128)(2,1)S(1)}, bf16[512,1536]{1,0:T(8,128)(2,1)}, u32[]{:S(2)}, u32[]{:S(2)}) collective-permute-start(bf16[512,1536]{1,0:T(8,128)(2,1)S(1)} %get-tuple-element.3213), channel_id=1, source_target_pairs={{1,0},{2,1},{3,2},{4,3},{5,4},{6,5},{7,6}} | collective-permute-start | bytes 4718600 | tf_op jit(solution)/shard_map/while/body/eval_jaxpr/ppermute | solution.py:448
  765.0 22.9 collective-permute-start.1
  790.6 89.1 %collective-permute-start.2 = (bf16[512,1536]{1,0:T(8,128)(2,1)S(1)}, bf16[512,1536]{1,0:T(8,128)(2,1)}, u32[]{:S(2)}, u32[]{:S(2)}) collective-permute-start(bf16[512,1536]{1,0:T(8,128)(2,1)S(1)} %get-tuple-element.3213), channel_id=1, source_target_pairs={{1,0},{2,1},{3,2},{4,3},{5,4},{6,5},{7,6}} | collective-permute-start | bytes 4718600 | tf_op jit(solution)/shard_map/while/body/eval_jaxpr/ppermute | solution.py:448
  858.7 22.9 collective-permute-start.1
  884.2 89.0 %collective-permute-start.2 = (bf16[512,1536]{1,0:T(8,128)(2,1)S(1)}, bf16[512,1536]{1,0:T(8,128)(2,1)}, u32[]{:S(2)}, u32[]{:S(2)}) collective-permute-start(bf16[512,1536]{1,0:T(8,128)(2,1)S(1)} %get-tuple-element.3213), channel_id=1, source_target_pairs={{1,0},{2,1},{3,2},{4,3},{5,4},{6,5},{7,6}} | collective-permute-start | bytes 4718600 | tf_op jit(solution)/shard_map/while/body/eval_jaxpr/ppermute | solution.py:448
  952.3 22.8 collective-permute-start.1
  977.8 89.1 %collective-permute-start.2 = (bf16[512,1536]{1,0:T(8,128)(2,1)S(1)}, bf16[512,1536]{1,0:T(8,128)(2,1)}, u32[]{:S(2)}, u32[]{:S(2)}) collective-permute-start(bf16[512,1536]{1,0:T(8,128)(2,1)S(1)} %get-tuple-element.3213), channel_id=1, source_target_pairs={{1,0},{2,1},{3,2},{4,3},{5,4},{6,5},{7,6}} | collective-permute-start | bytes 4718600 | tf_op jit(solution)/shard_map/while/body/eval_jaxpr/ppermute | solution.py:448
  1045.9 22.9 collective-permute-start.1
  1071.4 89.1 %collective-permute-start.2 = (bf16[512,1536]{1,0:T(8,128)(2,1)S(1)}, bf16[512,1536]{1,0:T(8,128)(2,1)}, u32[]{:S(2)}, u32[]{:S(2)}) collective-permute-start(bf16[512,1536]{1,0:T(8,128)(2,1)S(1)} %get-tuple-element.3213), channel_id=1, source_target_pairs={{1,0},{2,1},{3,2},{4,3},{5,4},{6,5},{7,6}} | collective-permute-start | bytes 4718600 | tf_op jit(solution)/shard_map/while/body/eval_jaxpr/ppermute | solution.py:448
  1139.5 22.8 collective-permute-start.1
  1165.0 89.1 %collective-permute-start.2 = (bf16[512,1536]{1,0:T(8,128)(2,1)S(1)}, bf16[512,1536]{1,0:T(8,128)(2,1)}, u32[]{:S(2)}, u32[]{:S(2)}) collective-permute-start(bf16[512,1536]{1,0:T(8,128)(2,1)S(1)} %get-tuple-element.3213), channel_id=1, source_target_pairs={{1,0},{2,1},{3,2},{4,3},{5,4},{6,5},{7,6}} | collective-permute-start | bytes 4718600 | tf_op jit(solution)/shard_map/while/body/eval_jaxpr/ppermute | solution.py:448
  1233.0 22.8 collective-permute-start.1
  1258.5 487.7 %collective-permute-start.2 = (bf16[512,1536]{1,0:T(8,128)(2,1)S(1)}, bf16[512,1536]{1,0:T(8,128)(2,1)}, u32[]{:S(2)}, u32[]{:S(2)}) collective-permute-start(bf16[512,1536]{1,0:T(8,128)(2,1)S(1)} %get-tuple-element.3213), channel_id=1, source_target_pairs={{1,0},{2,1},{3,2},{4,3},{5,4},{6,5},{7,6}} | collective-permute-start | bytes 4718600 | tf_op jit(solution)/shard_map/while/body/eval_jaxpr/ppermute | solution.py:448
  1326.6 500.3 %collective-permute-start.1 = (bf16[512,1536]{1,0:T(8,128)(2,1)}, bf16[512,1536]{1,0:T(8,128)(2,1)}, u32[]{:S(2)}, u32[]{:S(2)}) collective-permute-start(bf16[512,1536]{1,0:T(8,128)(2,1)} %get-tuple-element.2961), channel_id=1, source_target_pairs={{0,1},{1,2},{2,3},{3,4},{4,5},{5,6},{6,7}} | collective-permute-start | bytes 4718600 | tf_op jit(solution)/shard_map/while/body/eval_jaxpr/ppermute | solution.py:450
  1829.6 73.7 %collective-permute-start.2 = (bf16[512,1536]{1,0:T(8,128)(2,1)S(1)}, bf16[512,1536]{1,0:T(8,128)(2,1)}, u32[]{:S(2)}, u32[]{:S(2)}) collective-permute-start(bf16[512,1536]{1,0:T(8,128)(2,1)S(1)} %get-tuple-element.3213), channel_id=1, source_target_pairs={{1,0},{2,1},{3,2},{4,3},{5,4},{6,5},{7,6}} | collective-permute-start | bytes 4718600 | tf_op jit(solution)/shard_map/while/body/eval_jaxpr/ppermute | solution.py:448
  1897.7 86.1 %collective-permute-start.1 = (bf16[512,1536]{1,0:T(8,128)(2,1)}, bf16[512,1536]{1,0:T(8,128)(2,1)}, u32[]{:S(2)}, u32[]{:S(2)}) collective-permute-start(bf16[512,1536]{1,0:T(8,128)(2,1)} %get-tuple-element.2961), channel_id=1, source_target_pairs={{0,1},{1,2},{2,3},{3,4},{4,5},{5,6},{6,7}} | collective-permute-start | bytes 4718600 | tf_op jit(solution)/shard_map/while/body/eval_jaxpr/ppermute | solution.py:450
  1986.4 73.9 %collective-permute-start.2 = (bf16[512,1536]{1,0:T(8,128)(2,1)S(1)}, bf16[512,1536]{1,0:T(8,128)(2,1)}, u32[]{:S(2)}, u32[]{:S(2)}) collective-permute-start(bf16[512,1536]{1,0:T(8,128)(2,1)S(1)} %get-tuple-element.3213), channel_id=1, source_target_pairs={{1,0},{2,1},{3,2},{4,3},{5,4},{6,5},{7,6}} | collective-permute-start | bytes 4718600 | tf_op jit(solution)/shard_map/while/body/eval_jaxpr/ppermute | solution.py:448
  1987.8 153.2 %collective-permute-start.1 = (bf16[512,1536]{1,0:T(8,128)(2,1)}, bf16[512,1536]{1,0:T(8,128)(2,1)}, u32[]{:S(2)}, u32[]{:S(2)}) collective-permute-start(bf16[512,1536]{1,0:T(8,128)(2,1)} %get-tuple-element.2961), channel_id=1, source_target_pairs={{0,1},{1,2},{2,3},{3,4},{4,5},{5,6},{6,7}} | collective-permute-start | bytes 4718600 | tf_op jit(solution)/shard_map/while/body/eval_jaxpr/ppermute | solution.py:450
  2143.6 6.6 collective-permute-start.2
  2145.0 85.8 %collective-permute-start.1 = (bf16[512,1536]{1,0:T(8,128)(2,1)}, bf16[512,1536]{1,0:T(8,128)(2,1)}, u32[]{:S(2)}, u32[]{:S(2)}) collective-permute-start(bf16[512,1536]{1,0:T(8,128)(2,1)} %get-tuple-element.2961), channel_id=1, source_target_pairs={{0,1},{1,2},{2,3},{3,4},{4,5},{5,6},{6,7}} | collective-permute-start | bytes 4718600 | tf_op jit(solution)/shard_map/while/body/eval_jaxpr/ppermute | solution.py:450
  2233.5 73.5 %collective-permute-start.2 = (bf16[512,1536]{1,0:T(8,128)(2,1)S(1)}, bf16[512,1536]{1,0:T(8,128)(2,1)}, u32[]{:S(2)}, u32[]{:S(2)}) collective-permute-start(bf16[512,1536]{1,0:T(8,128)(2,1)S(1)} %get-tuple-element.3213), channel_id=1, source_target_pairs={{1,0},{2,1},{3,2},{4,3},{5,4},{6,5},{7,6}} | collective-permute-start | bytes 4718600 | tf_op jit(solution)/shard_map/while/body/eval_jaxpr/ppermute | solution.py:448
  2234.8 152.7 %collective-permute-start.1 = (bf16[512,1536]{1,0:T(8,128)(2,1)}, bf16[512,1536]{1,0:T(8,128)(2,1)}, u32[]{:S(2)}, u32[]{:S(2)}) collective-permute-start(bf16[512,1536]{1,0:T(8,128)(2,1)} %get-tuple-element.2961), channel_id=1, source_target_pairs={{0,1},{1,2},{2,3},{3,4},{4,5},{5,6},{6,7}} | collective-permute-start | bytes 4718600 | tf_op jit(solution)/shard_map/while/body/eval_jaxpr/ppermute | solution.py:450
  2390.2 23.1 collective-permute-start.2
  2391.5 102.5 %collective-permute-start.1 = (bf16[512,1536]{1,0:T(8,128)(2,1)}, bf16[512,1536]{1,0:T(8,128)(2,1)}, u32[]{:S(2)}, u32[]{:S(2)}) collective-permute-start(bf16[512,1536]{1,0:T(8,128)(2,1)} %get-tuple-element.2961), channel_id=1, source_target_pairs={{0,1},{1,2},{2,3},{3,4},{4,5},{5,6},{6,7}} | collective-permute-start | bytes 4718600 | tf_op jit(solution)/shard_map/while/body/eval_jaxpr/ppermute | solution.py:450
  2496.6 73.3 %collective-permute-start.2 = (bf16[512,1536]{1,0:T(8,128)(2,1)S(1)}, bf16[512,1536]{1,0:T(8,128)(2,1)}, u32[]{:S(2)}, u32[]{:S(2)}) collective-permute-start(bf16[512,1536]{1,0:T(8,128)(2,1)S(1)} %get-tuple-element.3213), channel_id=1, source_target_pairs={{1,0},{2,1},{3,2},{4,3},{5,4},{6,5},{7,6}} | collective-permute-start | bytes 4718600 | tf_op jit(solution)/shard_map/while/body/eval_jaxpr/ppermute | solution.py:448
  2498.0 152.5 %collective-permute-start.1 = (bf16[512,1536]{1,0:T(8,128)(2,1)}, bf16[512,1536]{1,0:T(8,128)(2,1)}, u32[]{:S(2)}, u32[]{:S(2)}) collective-permute-start(bf16[512,1536]{1,0:T(8,128)(2,1)} %get-tuple-element.2961), channel_id=1, source_target_pairs={{0,1},{1,2},{2,3},{3,4},{4,5},{5,6},{6,7}} | collective-permute-start | bytes 4718600 | tf_op jit(solution)/shard_map/while/body/eval_jaxpr/ppermute | solution.py:450
  2653.2 21.8 collective-permute-start.2
  2654.5 101.1 %collective-permute-start.1 = (bf16[512,1536]{1,0:T(8,128)(2,1)}, bf16[512,1536]{1,0:T(8,128)(2,1)}, u32[]{:S(2)}, u32[]{:S(2)}) collective-permute-start(bf16[512,1536]{1,0:T(8,128)(2,1)} %get-tuple-element.2961), channel_id=1, source_target_pairs={{0,1},{1,2},{2,3},{3,4},{4,5},{5,6},{6,7}} | collective-permute-start | bytes 4718600 | tf_op jit(solution)/shard_map/while/body/eval_jaxpr/ppermute | solution.py:450
  2758.2 60.1 %collective-permute-start.2 = (bf16[512,1536]{1,0:T(8,128)(2,1)S(1)}, bf16[512,1536]{1,0:T(8,128)(2,1)}, u32[]{:S(2)}, u32[]{:S(2)}) collective-permute-start(bf16[512,1536]{1,0:T(8,128)(2,1)S(1)} %get-tuple-element.3213), channel_id=1, source_target_pairs={{1,0},{2,1},{3,2},{4,3},{5,4},{6,5},{7,6}} | collective-permute-start | bytes 4718600 | tf_op jit(solution)/shard_map/while/body/eval_jaxpr/ppermute | solution.py:448
  2759.5 139.5 %collective-permute-start.1 = (bf16[512,1536]{1,0:T(8,128)(2,1)}, bf16[512,1536]{1,0:T(8,128)(2,1)}, u32[]{:S(2)}, u32[]{:S(2)}) collective-permute-start(bf16[512,1536]{1,0:T(8,128)(2,1)} %get-tuple-element.2961), channel_id=1, source_target_pairs={{0,1},{1,2},{2,3},{3,4},{4,5},{5,6},{6,7}} | collective-permute-start | bytes 4718600 | tf_op jit(solution)/shard_map/while/body/eval_jaxpr/ppermute | solution.py:450
  2912.3 22.0 collective-permute-start.3
  3014.8 69.2 %collective-permute-start.3 = (bf16[512,1536]{1,0:T(8,128)(2,1)S(1)}, bf16[512,1536]{1,0:T(8,128)(2,1)}, u32[]{:S(2)}, u32[]{:S(2)}) collective-permute-start(bf16[512,1536]{1,0:T(8,128)(2,1)S(1)} %get-tuple-element.3320), channel_id=1, source_target_pairs={{1,0},{2,1},{3,2},{4,3},{5,4},{6,5},{7,6}} | collective-permute-start | bytes 4718600 | tf_op jit(solution)/shard_map/while/body/eval_jaxpr/ppermute | solution.py:456
  3164.7 22.5 collective-permute-start.3
  3267.8 54.4 %collective-permute-start.3 = (bf16[512,1536]{1,0:T(8,128)(2,1)S(1)}, bf16[512,1536]{1,0:T(8,128)(2,1)}, u32[]{:S(2)}, u32[]{:S(2)}) collective-permute-start(bf16[512,1536]{1,0:T(8,128)(2,1)S(1)} %get-tuple-element.3320), channel_id=1, source_target_pairs={{1,0},{2,1},{3,2},{4,3},{5,4},{6,5},{7,6}} | collective-permute-start | bytes 4718600 | tf_op jit(solution)/shard_map/while/body/eval_jaxpr/ppermute | solution.py:456
  3402.8 23.1 collective-permute-start.3
  3506.6 69.4 %collective-permute-start.3 = (bf16[512,1536]{1,0:T(8,128)(2,1)S(1)}, bf16[512,1536]{1,0:T(8,128)(2,1)}, u32[]{:S(2)}, u32[]{:S(2)}) collective-permute-start(bf16[512,1536]{1,0:T(8,128)(2,1)S(1)} %get-tuple-element.3320), channel_id=1, source_target_pairs={{1,0},{2,1},{3,2},{4,3},{5,4},{6,5},{7,6}} | collective-permute-start | bytes 4718600 | tf_op jit(solution)/shard_map/while/body/eval_jaxpr/ppermute | solution.py:456
  3656.5 23.1 collective-permute-start.3
  3760.6 25.0 copy-start.4
  4361.1 25.0 copy-start.3
Sparse Core Ops, SparseCore 0:
  3795.2 565.7 all-reduce.2

commit v2 on v0

v2 whole, which is shorter than its diff:
```python
import functools
import jax
import jax.numpy as jnp
from jax import lax
from jax.experimental import pallas as pl
from jax.experimental.pallas import tpu as pltpu
from jax.sharding import PartitionSpec as P

LN_EPS = 1e-5
PARAM_RANKS = (2, 2, 3, 2, 4, 2, 2, 2, 3, 2, 3, 2)
BF, F32 = jnp.bfloat16, jnp.float32
LOG2E = 1.4426950408889634
GC0 = 0.7978845608028654
GC1 = GC0 * 0.044715
NT = (((1,), (1,)), ((), ()))
NN = (((1,), (0,)), ((), ()))
TN = (((0,), (0,)), ((), ()))
TQ, TF, TD = 512, 512, 512
ROWS, BLK = 32, 128
NC = 512
HEAD_WIN = ((0, 128), (0, 256), (128, 384), (256, 384))
ANY = pl.BlockSpec(memory_space=pl.ANY)
SCALE = 96.0 ** -0.5
VMEM_LIMIT = 62 * 1024 * 1024


def mm(a, b, dims=NN):
    return lax.dot_general(a, b, dims, preferred_element_type=F32)


def ln_stats(x_wide):
    mean_val = jnp.mean(x_wide, axis=-1, keepdims=True)
    centered = x_wide - mean_val
    variance = jnp.mean(centered * centered, axis=-1, keepdims=True)
    rstd = lax.rsqrt(variance + LN_EPS)
    return centered * rstd, rstd


def ln_back(dh, xhat, rstd, gain):
    dxh = dh * gain
    c1 = jnp.mean(dxh, axis=-1, keepdims=True)
    c2 = jnp.mean(dxh * xhat, axis=-1, keepdims=True)
    return rstd * (dxh - c1 - xhat * c2)


def head_mask(j):
    lo, hi = HEAD_WIN[j]
    lane = lax.broadcasted_iota(jnp.int32, (1, hi - lo), 1) + lo
    keep = (lane >= 96 * j) & (lane < 96 * j + 96)
    return jnp.where(keep, 1.0, 0.0).astype(BF)


def lanes(start, size):
    return pl.ds(pl.multiple_of(start, 128), size)


def join_heads(t):
    return jnp.concatenate([t[0] + t[1][:, :128], t[1][:, 128:] + t[2][:, :128], t[2][:, 128:] + t[3]], axis=1)


def row_blocks(n_seq, body):
    def outer(i, carry):
        for u in range(BLK // ROWS):
            body(pl.ds(pl.multiple_of(i * BLK + u * ROWS, ROWS), ROWS))
        return carry

    lax.fori_loop(0, n_seq // BLK, outer, 0)


def fold8(t):
    return jnp.sum(t.reshape(t.shape[0] // 8, 8, t.shape[1]), axis=0)


def fwd_kernel(idx, x_in, x_all, conv_in, g1, s1, bqkv, bproj, g2, s2, bup, bdown, wqkv, wproj, wup, wdown, *rest):
    n_alias = 11
    (y_o, conv_o, xs_o, h1_o, qkv_o, mix_o, x1_o, h2_o, pre_o, lse_o, act_o,
     x_s, h1_s, qkv_s, mix_s, x1_s, h2_s, act_s, stage_s, pre_s, acc_s, y_s, lse_s, vt_s, ot_s, conv_s, wq_s, wp_s, wu_s, wd_s,
     sem_in, sem_q, sem_u, sem_d, sem_pre, sem_act, sem_out) = rest[n_alias:]
    c, first, last = idx[0], idx[1], idx[2]
    n_seq, d = x_s.shape
    half = n_seq // 2
    n_q, n_f = wqkv.shape[1] // TQ, wup.shape[1] // TF
    copy = pltpu.make_async_copy
    four = lambda j: lax.rem(j, 4)
    wq = lambda j: copy(wqkv.at[:, lanes(j * TQ, TQ)], wq_s.at[lax.rem(j, 6)], sem_q.at[lax.rem(j, 6)])
    act_out = lambda j: copy(stage_s.at[four(j)], act_o.at[c, :, lanes(j * TF, TF)], sem_act.at[four(j)])
    wu = lambda j: copy(wup.at[:, lanes(j * TF, TF)], wu_s.at[four(j)], sem_u.at[four(j)])
    wd = lambda j: copy(wdown.at[pl.ds(pl.multiple_of(j * TF, TF), TF), :], wd_s.at[four(j)], sem_d.at[four(j)])
    pre_out = lambda j: copy(pre_s.at[four(j)], pre_o.at[c, :, lanes(j * TF, TF)], sem_pre.at[four(j)])
    x_copy = copy(x_in, x_s, sem_in.at[0])
    wp_copy = copy(wproj, wp_s, sem_in.at[1])

    @pl.when(first == 1)
    def _():
        copy(x_all.at[c], x_s, sem_in.at[0]).start()

    @pl.when(first == 0)
    def _():
        x_copy.start()

    wq(0).start()
    x_copy.wait()
    for j in range(1, 6):
        wq(j).start()

    def ln_first(rows):
        xhat, _ = ln_stats(x_s[rows].astype(F32))
        h1_s[rows] = (xhat * g1[...].astype(F32) + s1[...].astype(F32)).astype(BF)

    row_blocks(n_seq, ln_first)
    conv_load = copy(conv_in, conv_s, sem_in.at[2])
    conv_put = copy(conv_s, conv_o, sem_in.at[3])

    @pl.when(last == 0)
    def _():
        conv_load.start()

    outs = [copy(x_s, xs_o.at[c], sem_out.at[0]), copy(h1_s, h1_o.at[c], sem_out.at[1])]
    for o in outs:
        o.start()

    def qkv_tiles(i, carry):
        for u in range(3):
            wq(3 * i + u).wait()
        for u in range(3):
            j = 3 * i + u
            cols = lanes(j * TQ, TQ)
            qkv_s[:, cols] = (mm(h1_s[...], wq_s[lax.rem(j, 6)]) + bqkv[:, cols].astype(F32)).astype(BF)
        for u in range(3):
            @pl.when(3 * i + u + 6 < n_q)
            def _(j=3 * i + u + 6):
                wq(j).start()

        return carry

    lax.fori_loop(0, n_q // 3, qkv_tiles, 0)
    wp_copy.start()
    for j in range(4):
        wu(j).start()
        wd(j).start()
    outs.append(copy(qkv_s, qkv_o.at[c], sem_out.at[2]))
    outs[-1].start()

    def attend(grp, carry):
        part = lambda p, lo, hi: qkv_s[:, lanes(p * d + grp * 384 + lo, hi - lo)]
        vt_s[...] = part(2, 0, 384).T
        keep = lax.broadcasted_iota(jnp.int32, (128, 128), 0) <= lax.broadcasted_iota(jnp.int32, (128, 128), 1)
        sc = SCALE * LOG2E

        def scores(j):
            lo, hi = HEAD_WIN[j]
            qm, kw = part(0, lo, hi) * head_mask(j), part(1, lo, hi)
            pre_s[j % 2, :half] = mm(kw[:half], qm, NT)
            pre_s[j % 2, half:, half:] = mm(kw[half:], qm[half:], NT)

        def soften(j):
            for b in range(4):
                cols = slice(b * 128, (b + 1) * 128)

                def block(r):
                    t = pre_s[j % 2, r * 64:(r + 1) * 64, cols] * sc
                    if r // 2 == b:
                        t = jnp.where(keep[(r % 2) * 64:(r % 2 + 1) * 64], t, -1e30)
                    return t.reshape(8, 8, 128)

                n_blk = 2 * (b + 1)
                mx = jnp.max(block(0), axis=0)
                for r in range(1, n_blk):
                    mx = jnp.maximum(mx, jnp.max(block(r), axis=0))
                mx = jnp.max(mx, axis=0, keepdims=True)
                tot = jnp.zeros((8, 128), F32)
                for r in range(n_blk):
                    tot = tot + jnp.sum(jnp.exp2(block(r) - mx), axis=0)
                lse = mx + jnp.log2(jnp.sum(tot, axis=0, keepdims=True))
                lse_s[grp, j:j + 1, cols] = lse
                for r in range(n_blk):
                    act_s[j % 2, r * 64:(r + 1) * 64, cols] = jnp.exp2(block(r) - lse).astype(BF).reshape(64, 128)
                if b % 2 == 0:
                    act_s[j % 2, (b + 1) * 128:(b + 2) * 128, cols] = jnp.zeros((128, 128), BF)

        def mixed(j):
            rows = slice(96 * j, 96 * j + 96)
            ot_s[rows, :half] = mm(vt_s[rows, :half], act_s[j % 2, :half, :half]).astype(BF)
            ot_s[rows, half:] = mm(vt_s[rows, :], act_s[j % 2, :, half:n_seq]).astype(BF)

        scores(0)
        for j in range(4):
            if j < 3:
                scores(j + 1)
            soften(j)
            mixed(j)
        mix_s[:, lanes(grp * 384, 384)] = ot_s[...].T
        return carry

    lax.fori_loop(0, 4, attend, 0)

    @pl.when(last == 0)
    def _():
        conv_load.wait()
        conv_put.start()

    outs.append(copy(mix_s, mix_o.at[c], sem_out.at[3]))
    outs[-1].start()
    outs.append(copy(lse_s, lse_o.at[c], sem_out.at[4]))
    outs[-1].start()
    wp_copy.wait()

    def proj(i, carry):
        cols = lanes(i * NC, NC)
        acc_s[:, cols] = mm(mix_s[...], wp_s[:, cols])
        return carry

    lax.fori_loop(0, d // NC, proj, 0)

    def ln_second(rows):
        x1 = (x_s[rows].astype(F32) + acc_s[rows] + bproj[...].astype(F32)).astype(BF)
        x1_s[rows] = x1
        x1w = x1.astype(F32)
        xhat, _ = ln_stats(x1w)
        h2_s[rows] = (xhat * g2[...].astype(F32) + s2[...].astype(F32)).astype(BF)
        acc_s[rows] = x1w + bdown[...].astype(F32)

    row_blocks(n_seq, ln_second)
    outs.append(copy(x1_s, x1_o.at[c], sem_out.at[5]))
    outs[-1].start()
    outs.append(copy(h2_s, h2_o.at[c], sem_out.at[6]))
    outs[-1].start()

    def up(j, par):
        pre = mm(h2_s[...], wu_s[four(j)]) + bup[:, lanes(j * TF, TF)].astype(F32)
        pre_s[four(j)] = pre
        t = jnp.tanh(pre * (GC0 + GC1 * (pre * pre)))
        a = (0.5 * pre * (1.0 + t)).astype(BF)
        act_s[par] = a
        stage_s[four(j)] = a

    def down(j, par):
        for n in range(0, d, NC):
            acc_s[:, n:n + NC] += mm(act_s[par], wd_s[four(j), :, n:n + NC])

    def put(j):
        pre_out(j).start()
        act_out(j).start()

    def put_done(j):
        pre_out(j).wait()
        act_out(j).wait()

    wu(0).wait()
    up(0, 0)
    put(0)
    wu(4).start()

    def mlp(i, carry):
        j = 1 + 2 * i
        for u in range(2):
            wu(j + u).wait()
            wd(j + u - 1).wait()

            @pl.when(j + u >= 4)
            def _(u=u):
                put_done(j + u - 4)
        for u in range(2):
            up(j + u, (1 + u) % 2)
            down(j + u - 1, u % 2)
        for u in range(2):
            put(j + u)

            @pl.when(j + u + 4 < n_f)
            def _(u=u):
                wu(j + u + 4).start()

            @pl.when(j + u + 3 < n_f)
            def _(u=u):
                wd(j + u + 3).start()
        return carry

    lax.fori_loop(0, (n_f - 2) // 2, mlp, 0)
    j = n_f - 1
    wu(j).wait()
    wd(j - 1).wait()
    wd(j).wait()
    put_done(j - 4)
    up(j, 1)
    down(j - 1, 0)
    put(j)
    for n in range(0, d, NC):
        y_s[:, n:n + NC] = (acc_s[:, n:n + NC] + mm(act_s[1], wd_s[j % 4, :, n:n + NC])).astype(BF)
    y_copy = copy(y_s, y_o, sem_in.at[0])
    y_copy.start()

    @pl.when(last == 1)
    def _():
        copy(y_s, conv_o, sem_in.at[3]).start()

    for o in outs:
        o.wait()
    for i in range(4):
        put_done(j - 3 + i)
    y_copy.wait()

    conv_put.wait()


def fwd_call(idx, x_in, x_all, conv_in, weights, y, conv, saved):
    g1, s1, wqkv, bqkv, wproj, bproj, g2, s2, wup, bup, wdown, bdown = weights
    n_seq, d = x_in.shape
    e, f = wqkv.shape[1], wup.shape[1]
    r2 = lambda t: t.reshape(1, -1)
    vm = pl.BlockSpec(memory_space=pltpu.VMEM)
    args = [idx, x_in, x_all, conv_in, r2(g1), r2(s1), r2(bqkv), r2(bproj), r2(g2), r2(s2), r2(bup), r2(bdown),
            wqkv, wproj.reshape(d, d), wup, wdown]
    alias = [y, conv] + list(saved)
    dma = pltpu.SemaphoreType.DMA
    vmem = lambda *s: pltpu.VMEM(s[:-1], s[-1])
    outs = pl.pallas_call(
        fwd_kernel,
        in_specs=[pl.BlockSpec(memory_space=pltpu.SMEM), ANY, ANY, ANY] + [vm] * 8 + [ANY] * (4 + len(alias)),
        out_specs=[ANY] * len(alias),
        out_shape=[jax.ShapeDtypeStruct(t.shape, t.dtype) for t in alias],
        input_output_aliases={len(args) + i: i for i in range(len(alias))},
        scratch_shapes=[
            vmem(n_seq, d, BF), vmem(n_seq, d, BF), vmem(n_seq, e, BF), vmem(n_seq, d, BF), vmem(n_seq, d, BF), vmem(n_seq, d, BF),
            vmem(2, n_seq, TF, BF), vmem(4, n_seq, TF, BF), vmem(4, n_seq, TF, F32), vmem(n_seq, d, F32), vmem(n_seq, d, BF),
            vmem(4, 8, n_seq, F32), vmem(384, n_seq, BF), vmem(384, n_seq, BF), vmem(n_seq, d, BF),
            vmem(6, d, TQ, BF), vmem(d, d, BF), vmem(4, d, TF, BF), vmem(4, TF, d, BF),
            dma((4,)), dma((6,)), dma((4,)), dma((4,)), dma((4,)), dma((4,)), dma((7,)),
        ],
        compiler_params=pltpu.CompilerParams(vmem_limit_bytes=VMEM_LIMIT),
        cost_estimate=pl.CostEstimate(flops=int(31e9), bytes_accessed=int(9e7), transcendentals=0),
        name="layer_fwd",
    )(*args, *alias)
    return outs[0], outs[1], tuple(outs[2:])


def bwd_kernel(idx, dy_in, ct_all, conv, xs, qkv, mix, x1, pre, lse, g1, g2, wqkv, wproj, wup, wdown, *rest):
    n_alias = 10
    (dx_o, dxs_o, ys_o, dpre_o, dmid_o, dqkv_o, dys_o, sup_o, sqkv_o, sd_o,
     dy_s, acc_s, dp_s, p_s, stage_s, x1_s, dm_s, do_s, qkv_s, mix_s, x_s, conv_s, lse_s, rd_s, kt_s, dqt_s, sup_s, sqkv_s, sd_s, fold_s, pre_s,
     wq_s, wp_s, wu_s, wd_s,
     sem_in, sem_q, sem_u, sem_d, sem_pre, sem_dp, sem_out) = rest[n_alias:]
    c, first, last = idx[0], idx[1], idx[2]
    n_seq, d = dy_s.shape
    half = n_seq // 2
    n_q, n_f = wqkv.shape[1] // TQ, wup.shape[1] // TF
    copy = pltpu.make_async_copy
    four = lambda j: lax.rem(j, 4)
    n_t = wqkv.shape[0] // TD
    wq = lambda j: copy(wqkv.at[pl.ds(pl.multiple_of(j * TD, TD), TD), :], wq_s.at[lax.rem(j, 2)], sem_q.at[lax.rem(j, 2)])
    wu = lambda j: copy(wup.at[:, lanes(j * TF, TF)], wu_s.at[four(j)], sem_u.at[four(j)])
    wd = lambda j: copy(wdown.at[pl.ds(pl.multiple_of(j * TF, TF), TF), :], wd_s.at[four(j)], sem_d.at[four(j)])
    pre_in = lambda j: copy(pre.at[c, :, lanes(j * TF, TF)], pre_s.at[four(j)], sem_pre.at[four(j)])
    dp_out = lambda j: copy(stage_s.at[four(j)], dpre_o.at[c, :, lanes(j * TF, TF)], sem_dp.at[four(j)])
    dy_copy = copy(dy_in, dy_s, sem_in.at[0])
    ins = [copy(x1.at[c], x1_s, sem_in.at[1]), copy(wproj, wp_s, sem_in.at[2]), copy(qkv.at[c], qkv_s, sem_in.at[3]),
           copy(mix.at[c], mix_s, sem_in.at[4]), copy(lse.at[c], lse_s, sem_in.at[5]), copy(xs.at[c], x_s, sem_in.at[6]),
           copy(conv, conv_s, sem_in.at[7])]
    colsum = lambda t: jnp.sum(t, axis=0, keepdims=True)

    @pl.when(last == 1)
    def _():
        copy(ct_all.at[c], dy_s, sem_in.at[0]).start()

    @pl.when(last == 0)
    def _():
        dy_copy.start()

    wd(0).start()
    pre_in(0).start()
    dy_copy.wait()
    for j in range(1, 4):
        wd(j).start()
        pre_in(j).start()
        wu(j - 1).start()
    wu(3).start()
    outs = [copy(dy_s, dys_o.at[c], sem_out.at[0])]
    outs[0].start()

    def down_back(j, par):
        slot = four(j)
        da = mm(dy_s[...], wd_s[slot], NT).astype(BF).astype(F32)
        p = pre_s[slot]
        p2 = p * p
        t = jnp.tanh(p * (GC0 + GC1 * p2))
        dpre = da * ((0.5 + 0.5 * t) * (1.0 + (1.0 - t) * (p * (GC0 + (3.0 * GC1) * p2))))
        sup_s[:, lanes(j * TF, TF)] = colsum(dpre)
        b = dpre.astype(BF)
        dp_s[par] = b
        stage_s[slot] = b

    def up_back(j, par):
        for n in range(0, d, NC):
            acc_s[:, n:n + NC] += mm(dp_s[par], wu_s[four(j), n:n + NC, :], NT)

    wd(0).wait()
    pre_in(0).wait()
    acc_s[...] = jnp.zeros_like(acc_s)
    down_back(0, 0)
    dp_out(0).start()
    wd(4).start()
    pre_in(4).start()

    def mlp(i, carry):
        j = 1 + 2 * i
        for u in range(2):
            wd(j + u).wait()
            pre_in(j + u).wait()
            wu(j + u - 1).wait()

            @pl.when(j + u >= 4)
            def _(u=u):
                dp_out(j + u - 4).wait()
        for u in range(2):
            down_back(j + u, (1 + u) % 2)
            up_back(j + u - 1, u % 2)
        for u in range(2):
            dp_out(j + u).start()

            @pl.when(j + u + 4 < n_f)
            def _(u=u):
                wd(j + u + 4).start()
                pre_in(j + u + 4).start()

            @pl.when(j + u + 3 < n_f)
            def _(u=u):
                wu(j + u + 3).start()

        @pl.when(i == (n_f - 2) // 2 - 1)
        def _():
            for t in ins[:2]:
                t.start()

        return carry

    lax.fori_loop(0, (n_f - 2) // 2, mlp, 0)
    j = n_f - 1
    wd(j).wait()
    pre_in(j).wait()
    wu(j - 1).wait()
    wu(j).wait()
    dp_out(j - 4).wait()
    down_back(j, 1)
    up_back(j - 1, 0)
    dp_out(j).start()
    for t in ins[2:]:
        t.start()
    up_back(j, 1)
    ins[6].wait()
    outs.append(copy(conv_s, ys_o.at[c], sem_out.at[1]))
    outs[-1].start()
    ins[0].wait()

    def ln_bwd(src, base, base2, gain, dst, rows_at):
        fold_s[...] = jnp.zeros_like(fold_s)

        def body(rows):
            dh = acc_s[rows].astype(BF).astype(F32)
            xhat, rstd = ln_stats(src[rows].astype(F32))
            out = (base[rows].astype(F32) + ln_back(dh, xhat, rstd, gain[...].astype(F32))).astype(BF)
            dst[rows] = out
            fold_s[0] += fold8(dh * xhat)
            fold_s[1] += fold8(dh)
            if base2:
                fold_s[2] += fold8(out.astype(F32))
                fold_s[3] += fold8(dy_s[rows].astype(F32))

        row_blocks(n_seq, body)
        for i, at in enumerate(rows_at):
            sd_s[at:at + 1, :] = colsum(fold_s[i])

    ln_bwd(x1_s, dy_s, True, g2, dm_s, (2, 3, 4, 5))
    outs.append(copy(dm_s, dmid_o.at[c], sem_out.at[2]))
    outs[-1].start()
    ins[1].wait()

    def proj(i, carry):
        do_s[:, lanes(i * NC, NC)] = mm(dm_s[...], wp_s[pl.ds(pl.multiple_of(i * NC, NC), NC), :], NT).astype(BF)
        return carry

    lax.fori_loop(0, d // NC, proj, 0)
    for j in range(2):
        wq(j).start()
    for i in range(4):
        dp_out(n_f - 4 + i).wait()
    for t in ins[2:6]:
        t.wait()

    def attend(grp, carry):
        part = lambda p, lo, hi: qkv_s[:, lanes(p * d + grp * 384 + lo, hi - lo)]
        do_at = lambda lo, hi: do_s[:, lanes(grp * 384 + lo, hi - lo)]
        kt_s[...] = part(1, 0, 384).T
        prod = do_at(0, 384).T.astype(F32) * mix_s[:, lanes(grp * 384, 384)].T.astype(F32)
        for j in range(4):
            rd_s[j:j + 1, :] = colsum(prod[96 * j:96 * j + 96])
        causal = lax.broadcasted_iota(jnp.int32, (half, half), 0) <= lax.broadcasted_iota(jnp.int32, (half, half), 1)
        sc = SCALE * LOG2E
        dks, dvs = [], []
        lrow = lse_s[grp]
        def scores(j):
            lo, hi = HEAD_WIN[j]
            m = head_mask(j)
            qm, dom = part(0, lo, hi) * m, do_at(lo, hi) * m
            kw, vw = part(1, lo, hi), part(2, lo, hi)
            for at, a, b in ((0, kw, qm), (2, vw, dom)):
                pre_s[at + j % 2, :half] = mm(a[:half], b, NT)
                pre_s[at + j % 2, half:, half:] = mm(a[half:], b[half:], NT)

        def soften(j):
            for kb, qb in ((0, 0), (0, 1), (1, 1)):
                for r in range(kb * half, (kb + 1) * half, 32):
                    rows, cols = slice(r, r + 32), slice(qb * half, (qb + 1) * half)
                    p = jnp.exp2(pre_s[j % 2, rows, cols] * sc - lrow[j:j + 1, cols])
                    if kb == qb:
                        p = jnp.where(causal[r - kb * half:r - kb * half + 32], p, 0.0)
                    dp = pre_s[2 + j % 2, rows, cols].astype(BF).astype(F32)
                    p_s[j % 2, rows, cols] = p.astype(BF)
                    dp_s[j % 2, rows, cols] = (p * (dp - rd_s[j:j + 1, cols])).astype(BF)

        def products(j):
            lo, hi = HEAD_WIN[j]
            m = head_mask(j)
            qm, dom = part(0, lo, hi) * m, do_at(lo, hi) * m
            rows = slice(96 * j, 96 * j + 96)
            p, ds = p_s.at[j % 2], dp_s.at[j % 2]
            dvs.append(jnp.concatenate([mm(p[:half, :n_seq], dom), mm(p[half:, half:n_seq], dom[half:])], axis=0))
            dks.append(jnp.concatenate([mm(ds[:half, :n_seq], qm), mm(ds[half:, half:n_seq], qm[half:])], axis=0))
            dqt_s[rows, :half] = (mm(kt_s[rows, :half], ds[:half, :half]) * SCALE).astype(BF)
            dqt_s[rows, half:] = (mm(kt_s[rows, :], ds[:, half:n_seq]) * SCALE).astype(BF)

        scores(0)
        for j in range(4):
            if j < 3:
                scores(j + 1)
            soften(j)
            products(j)
        qkv_s[:, lanes(grp * 384, 384)] = dqt_s[...].T
        qkv_s[:, lanes(d + grp * 384, 384)] = (join_heads(dks) * SCALE).astype(BF)
        qkv_s[:, lanes(2 * d + grp * 384, 384)] = join_heads(dvs).astype(BF)
        return carry

    lax.fori_loop(0, 4, attend, 0)
    outs.append(copy(qkv_s, dqkv_o.at[c], sem_out.at[3]))
    outs[-1].start()

    def qkv_back(j, carry):
        wq(j).wait()
        acc_s[:, lanes(j * TD, TD)] = mm(qkv_s[...], wq_s[lax.rem(j, 2)], NT)
        for u in range(3):
            cols = lanes((3 * j + u) * TQ, TQ)
            sqkv_s[:, cols] = colsum(qkv_s[:, cols].astype(F32))

        @pl.when(j + 2 < n_t)
        def _():
            wq(j + 2).start()

        return carry

    lax.fori_loop(0, n_t, qkv_back, 0)
    ln_bwd(x_s, dm_s, False, g1, x1_s, (0, 1))
    dx_copy = copy(x1_s, dx_o, sem_in.at[0])
    dx_copy.start()

    @pl.when(first == 1)
    def _():
        copy(x1_s, dxs_o.at[c], sem_in.at[1]).start()

    sd_s[6:8, :] = jnp.zeros((2, d), F32)
    for i, (src, dst) in enumerate(((sup_s, sup_o), (sqkv_s, sqkv_o), (sd_s, sd_o))):
        outs.append(copy(src, dst.at[c], sem_out.at[4 + i]))
        outs[-1].start()
    for o in outs:
        o.wait()
    dx_copy.wait()

    @pl.when(first == 1)
    def _():
        copy(x1_s, dxs_o.at[c], sem_in.at[1]).wait()


def bwd_call(idx, dy_in, ct_all, conv, weights, saved, dx, dx_all, y_all, store):
    g1, s1, wqkv, bqkv, wproj, bproj, g2, s2, wup, bup, wdown, bdown = weights
    xs, h1, qkv, mix, x1, h2, pre, lse, act = saved
    n_seq, d = dy_in.shape
    e, f = wqkv.shape[1], wup.shape[1]
    r2 = lambda t: t.reshape(1, -1)
    vm = pl.BlockSpec(memory_space=pltpu.VMEM)
    args = [idx, dy_in, ct_all, conv, xs, qkv, mix, x1, pre, lse, r2(g1), r2(g2), wqkv, wproj.reshape(d, d), wup, wdown]
    alias = [dx, dx_all, y_all] + list(store)
    dma = pltpu.SemaphoreType.DMA
    vmem = lambda *s: pltpu.VMEM(s[:-1], s[-1])
    outs = pl.pallas_call(
        bwd_kernel,
        in_specs=[pl.BlockSpec(memory_space=pltpu.SMEM)] + [ANY] * 9 + [vm] * 2 + [ANY] * (4 + len(alias)),
        out_specs=[ANY] * len(alias),
        out_shape=[jax.ShapeDtypeStruct(t.shape, t.dtype) for t in alias],
        input_output_aliases={len(args) + i: i for i in range(len(alias))},
        scratch_shapes=[
            vmem(n_seq, d, BF), vmem(n_seq, d, F32), vmem(2, n_seq, TF, BF), vmem(2, n_seq, n_seq, BF), vmem(4, n_seq, TF, BF), vmem(n_seq, d, BF), vmem(n_seq, d, BF),
            vmem(n_seq, d, BF), vmem(n_seq, e, BF), vmem(n_seq, d, BF), vmem(n_seq, d, BF),
            vmem(n_seq, d, BF), vmem(4, 8, n_seq, F32), vmem(8, n_seq, F32), vmem(384, n_seq, BF), vmem(384, n_seq, BF), vmem(1, f, F32), vmem(1, e, F32), vmem(8, d, F32), vmem(4, 8, d, F32),
            vmem(4, n_seq, TF, F32), vmem(2, TD, e, BF), vmem(d, d, BF), vmem(4, d, TF, BF), vmem(4, TF, d, BF),
            dma((8,)), dma((2,)), dma((4,)), dma((4,)), dma((4,)), dma((4,)), dma((7,)),
        ],
        compiler_params=pltpu.CompilerParams(vmem_limit_bytes=VMEM_LIMIT),
        cost_estimate=pl.CostEstimate(flops=int(36e9), bytes_accessed=int(1.1e8), transcendentals=0),
        name="layer_bwd",
    )(*args, *alias)
    return outs[0], outs[1], outs[2], tuple(outs[3:])


def fresh(shapes):
    return pl.pallas_call(
        lambda *refs: None,
        out_shape=shapes,
        out_specs=[ANY] * len(shapes),
        name="fresh",
    )()


def relay_kernel(src, _alias, dst, buf, sems):
    load = pltpu.make_async_copy(src, buf, sems.at[0])
    load.start()
    load.wait()
    put = pltpu.make_async_copy(buf, dst, sems.at[1])
    put.start()
    put.wait()


def relay(src, dst):
    return pl.pallas_call(
        relay_kernel,
        in_specs=[ANY, ANY],
        out_specs=ANY,
        out_shape=jax.ShapeDtypeStruct(dst.shape, dst.dtype),
        input_output_aliases={1: 0},
        scratch_shapes=[pltpu.VMEM(src.shape, src.dtype), pltpu.SemaphoreType.DMA((2,))],
        name="relay",
    )(src, dst)


def solution(mesh):
    n_stages = mesh.shape['pp']
    last_stage = n_stages - 1
    fwd_pairs = [(source, source + 1) for source in range(n_stages - 1)]
    bwd_pairs = [(source + 1, source) for source in range(n_stages - 1)]
    act_spec = P(None, 'dp', None, None)
    param_specs = tuple(P(*(('pp',) + (None,) * (rank_n - 1))) for rank_n in PARAM_RANKS)
    grad_specs = tuple(P(*((('dp', 'pp'),) + (None,) * (rank_n - 1))) for rank_n in PARAM_RANKS)

    def stage_body(acts_in, cotangent, *stacked_w):
        weights = tuple(tensor[0] for tensor in stacked_w)
        stage = lax.axis_index('pp')
        n_micro, n_rows, n_seq, d = acts_in.shape
        n_chunk = n_micro * n_rows
        x_all = acts_in.reshape(n_chunk, n_seq, d)
        ct_all = cotangent.reshape(n_chunk, n_seq, d)
        f = 4 * d
        sds = jax.ShapeDtypeStruct
        many = lambda w, t=BF: sds((n_chunk, n_seq, w), t)
        tall = lambda r, w: sds((n_chunk, r, w), F32)
        one = sds((n_seq, d), BF)
        shapes = [many(d), many(d), many(3 * d), many(d), many(d), many(d), many(f, F32), sds((n_chunk, 4, 8, n_seq), F32), many(f),
                  many(f), many(d), many(3 * d), many(d), tall(1, f), tall(1, 3 * d), tall(8, d),
                  many(d), many(d), one, one, one, one, one]
        bufs = fresh(shapes)
        saved, store = tuple(bufs[:9]), tuple(bufs[9:16])
        dx_all, y_all, x_in, conv_in, y, dx, conv = bufs[16:]

        def forward(t, x_in, conv_in, y, conv, saved):
            c = t - stage
            ok = (c >= 0) & (c < n_chunk)
            idx = jnp.stack([jnp.clip(c, 0, n_chunk - 1), stage == 0, stage == last_stage]).astype(jnp.int32)
            run = lambda x_in, conv_in, y, conv, saved: fwd_call(idx, x_in, x_all, conv_in, weights, y, conv, saved)
            skip = lambda x_in, conv_in, y, conv, saved: (y, relay(conv_in, conv), saved)
            return lax.cond(ok, run, skip, x_in, conv_in, y, conv, saved)

        def backward(t, dy_in, conv, saved, dx, dx_all, y_all, store):
            c = t - (2 * last_stage - stage)
            ok = (c >= 0) & (c < n_chunk)
            idx = jnp.stack([jnp.clip(c, 0, n_chunk - 1), stage == 0, stage == last_stage]).astype(jnp.int32)
            run = lambda dy_in, conv, saved, dx, dx_all, y_all, store: bwd_call(idx, dy_in, ct_all, conv, weights, saved, dx, dx_all, y_all, store)
            skip = lambda dy_in, conv, saved, dx, dx_all, y_all, store: (dx, dx_all, y_all, store)
            return lax.cond(ok, run, skip, dy_in, conv, saved, dx, dx_all, y_all, store)

        def step(t, state):
            x_in, conv_in, y, dx, conv, saved, store, dx_all, y_all = state
            dy_in = lax.ppermute(dx, 'pp', bwd_pairs)
            y, conv, saved = forward(t, x_in, conv_in, y, conv, saved)
            x_in = lax.ppermute(y, 'pp', fwd_pairs)
            conv_in = lax.ppermute(conv, 'pp', bwd_pairs)
            dx, dx_all, y_all, store = backward(t, dy_in, conv, saved, dx, dx_all, y_all, store)
            return x_in, conv_in, y, dx, conv, saved, store, dx_all, y_all

        state = (x_in, conv_in, y, dx, conv, saved, store, dx_all, y_all)
        x_in, conv_in, y, dx, conv, saved, store, dx_all, y_all = lax.fori_loop(0, n_chunk + 2 * last_stage, step, state)

        grad_in = lax.psum(jnp.where(stage == 0, dx_all, jnp.zeros_like(dx_all)), 'pp')
        xs, h1, qkv, mix, x1, h2, pre, lse, act = saved
        dpre, dmid, dqkv, dys, sum_up, sum_qkv, sum_d = store
        wgrad = lambda a, b: jnp.einsum('cka,ckb->ab', a, b, preferred_element_type=F32)
        vec = jnp.sum(sum_d, axis=0)
        grads = (vec[0], vec[1], wgrad(h1, dqkv), jnp.sum(sum_qkv, axis=(0, 1)),
                 wgrad(mix, dmid).reshape(stacked_w[4].shape[1:]), vec[4], vec[2], vec[3],
                 wgrad(h2, dpre), jnp.sum(sum_up, axis=(0, 1)), wgrad(act, dys), vec[5])
        shape4 = acts_in.shape
        return (y_all.reshape(shape4), grad_in.reshape(shape4)) + tuple(g[None] for g in grads)

    return jax.shard_map(stage_body, mesh=mesh, in_specs=(act_spec, act_spec) + param_specs, out_specs=(act_spec, act_spec) + grad_specs, check_vma=False)
```

time: 9660 us -> 3660 us (0.38)
  waiting for transfers between devices: 3930 us -> 102 us
  matrix products: 3280 us -> 525 us
  Pallas kernels: 0 us -> 1820 us
  local copies, waits for them, and re-layouts: 729 us -> 36 us
  other arithmetic: 598 us -> 26.3 us
    ppermute x30 -> x90, waiting for transfers between devices: 3370 us -> 102 us  [the longest x30 95.7 us: step(): conv_in = lax.ppermute(conv, 'pp', bwd_pairs)]
    dot_general x136 -> x4, matrix products: 3140 us -> 525 us  [stage_body(): jnp.einsum('cka,ckb->ab', a, b, preferred_element_type=F32)]
    pallas_call x0 -> x47, Pallas kernels: none -> 1820 us  [the longest x16 1010 us: bwd_call(): pl.pallas_call(bwd_kernel, in_specs=[pl.BlockSpec(memory_space=pltpu.SMEM...]
    psum x1, waiting for transfers between devices: 561 us -> 0.01 us  [stage_body(): lax.psum(jnp.where(stage == 0, dx_all, jnp.zeros_like(dx_all)), 'pp')]
    dynamic_update_slice x24 -> x0, other arithmetic: 283 us -> none  [the longest x16 232 us: run_layer(): lax.dynamic_update_index_in_dim(buf_all, buf_new, mb_slot, 0)]
    reduce_sum x72 -> x3, other arithmetic: 253 us -> 1.11 us  [the longest x1 0.88 us: stage_body(): jnp.sum(sum_up, axis=(0, 1))]
    broadcast_in_dim x17 -> x1, local copies, waits for them, and re-layouts: 184 us -> 0.62 us  [stage_body(): g[None]]
    while x62 -> x120, local copies, waits for them, and re-layouts: 167 us -> 14.2 us  [the longest x2 118 us: stage_body(): lax.fori_loop(0, n_steps, bwd_step, bwd_init)]
  transfers between devices with their start and end apart: 31 -> 91, of which waited for: 31 -> 28; matrix products, arithmetic and copies ran while one was open for 0% -> 15% of each run, Pallas kernels for 0% -> 50%
where the time goes in v2:
time: 3660 us; the launch traced here: 3640 us
  Pallas kernels  1820 us (50%)
  starting transfers between devices  1110 us (30%)
  matrix products  525 us (14%)
  waiting for transfers between devices  102 us (3%)
    ppermute x30, starting transfers between devices, step(): x_in = lax.ppermute(y, 'pp', fwd_pairs)  1030 us
    pallas_call x16, Pallas kernels, bwd_call(): pl.pallas_call(bwd_kernel, in_specs=[pl.BlockSpec(memory_space=pltpu.SMEM...  1010 us
    pallas_call x16, Pallas kernels, fwd_call(): pl.pallas_call(fwd_kernel, in_specs=[pl.BlockSpec(memory_space=pltpu.SMEM...  774 us
    dot_general x4, matrix products, stage_body(): jnp.einsum('cka,ckb->ab', a, b, preferred_element_type=F32)  525 us
    ppermute x30, waiting for transfers between devices, step(): conv_in = lax.ppermute(conv, 'pp', bwd_pairs)  95.7 us
  transfers between devices with their start and end apart: 91, of which 28 were waited for; matrix products, arithmetic and copies ran while one was open for 15% of the time, Pallas kernels for 50%

profile of v2, /device:TPU:0, one launch (start us, length us, event | category | flops | bytes accessed | tf_op | source)
XLA Modules:
  0.0 3635.4 jit_solution(10083175199391155445)
XLA Ops:
  7.3 3052.8 %while.58 = (s32[]{:T(128)}, bf16[512,1536]{1,0:T(8,128)(2,1)}, bf16[512,1536]{1,0:T(8,128)(2,1)}, bf16[512,1536]{1,0:T(8,128)(2,1)}, bf16[512,1536]{1,0:T(8,128...) while((s32[]{:T(128)}, bf16[512,1536]{1,0:T(8,128)(2,1)}, ...), condition=%wide.region_5.6_spmd, body=%wide.region_0.5_spmd.sunk | while | flops 67000000512 | bytes 225167200 | solution.py:695
  8.7 48.4 %conditional.4 = ((bf16[512,1536]{1,0:T(8,128)(2,1)}, bf16[512,1536]{1,0:T(8,128)(2,1)}, bf16[16,512,1536]{2,1,0:T(8,128)(2,1)}, bf16[16,512,1536]{2,1,0:T(8,128...) conditional(s32[]{:T(128)} %convert_element_type.32, ...), branch_computations={%region_1.1_spmd, %region_2.2_spmd} | conditional | flops 31000000512 | bytes 90000008 | solution.py:675
  8.7 48.4 %layer_fwd.1 = (bf16[512,1536]{1,0:T(8,128)(2,1)}, bf16[512,1536]{1,0:T(8,128)(2,1)}, bf16[16,512,1536]{2,1,0:T(8,128)(2,1)}, bf16[16,512,1536]{2,1,0:T(8,128)(2...) custom-call(s32[3]{0:T(128)S(1)} %get-tuple-element.952.idx, ...), custom_call_target="tpu_custom_call", output_to_operand_aliasing={{0}: (16, {}), {1}: (17, {}), {2}: (18, {}), {3}: (19, {}),... | custom-call | flops 31000000512 | bytes 90000000 | tf_op jit(solution)/shard_map/while/body/eval_jaxpr/cond/branch_1_fun/layer_fwd/pallas_call | solution.py:316
  66.2 48.4 %conditional.4 = ((bf16[512,1536]{1,0:T(8,128)(2,1)}, bf16[512,1536]{1,0:T(8,128)(2,1)}, bf16[16,512,1536]{2,1,0:T(8,128)(2,1)}, bf16[16,512,1536]{2,1,0:T(8,128...) conditional(s32[]{:T(128)} %convert_element_type.32, ...), branch_computations={%region_1.1_spmd, %region_2.2_spmd} | conditional | flops 31000000512 | bytes 90000008 | solution.py:675
  125.4 48.4 %conditional.4 = ((bf16[512,1536]{1,0:T(8,128)(2,1)}, bf16[512,1536]{1,0:T(8,128)(2,1)}, bf16[16,512,1536]{2,1,0:T(8,128)(2,1)}, bf16[16,512,1536]{2,1,0:T(8,128...) conditional(s32[]{:T(128)} %convert_element_type.32, ...), branch_computations={%region_1.1_spmd, %region_2.2_spmd} | conditional | flops 31000000512 | bytes 90000008 | solution.py:675
  199.6 48.4 %conditional.4 = ((bf16[512,1536]{1,0:T(8,128)(2,1)}, bf16[512,1536]{1,0:T(8,128)(2,1)}, bf16[16,512,1536]{2,1,0:T(8,128)(2,1)}, bf16[16,512,1536]{2,1,0:T(8,128...) conditional(s32[]{:T(128)} %convert_element_type.32, ...), branch_computations={%region_1.1_spmd, %region_2.2_spmd} | conditional | flops 31000000512 | bytes 90000008 | solution.py:675
  275.4 48.4 %conditional.4 = ((bf16[512,1536]{1,0:T(8,128)(2,1)}, bf16[512,1536]{1,0:T(8,128)(2,1)}, bf16[16,512,1536]{2,1,0:T(8,128)(2,1)}, bf16[16,512,1536]{2,1,0:T(8,128...) conditional(s32[]{:T(128)} %convert_element_type.32, ...), branch_computations={%region_1.1_spmd, %region_2.2_spmd} | conditional | flops 31000000512 | bytes 90000008 | solution.py:675
  275.4 48.4 %layer_fwd.1 = (bf16[512,1536]{1,0:T(8,128)(2,1)}, bf16[512,1536]{1,0:T(8,128)(2,1)}, bf16[16,512,1536]{2,1,0:T(8,128)(2,1)}, bf16[16,512,1536]{2,1,0:T(8,128)(2...) custom-call(s32[3]{0:T(128)S(1)} %get-tuple-element.952.idx, ...), custom_call_target="tpu_custom_call", output_to_operand_aliasing={{0}: (16, {}), {1}: (17, {}), {2}: (18, {}), {3}: (19, {}),... | custom-call | flops 31000000512 | bytes 90000000 | tf_op jit(solution)/shard_map/while/body/eval_jaxpr/cond/branch_1_fun/layer_fwd/pallas_call | solution.py:316
  362.3 48.4 %conditional.4 = ((bf16[512,1536]{1,0:T(8,128)(2,1)}, bf16[512,1536]{1,0:T(8,128)(2,1)}, bf16[16,512,1536]{2,1,0:T(8,128)(2,1)}, bf16[16,512,1536]{2,1,0:T(8,128...) conditional(s32[]{:T(128)} %convert_element_type.32, ...), branch_computations={%region_1.1_spmd, %region_2.2_spmd} | conditional | flops 31000000512 | bytes 90000008 | solution.py:675
  449.2 48.4 %conditional.4 = ((bf16[512,1536]{1,0:T(8,128)(2,1)}, bf16[512,1536]{1,0:T(8,128)(2,1)}, bf16[16,512,1536]{2,1,0:T(8,128)(2,1)}, bf16[16,512,1536]{2,1,0:T(8,128...) conditional(s32[]{:T(128)} %convert_element_type.32, ...), branch_computations={%region_1.1_spmd, %region_2.2_spmd} | conditional | flops 31000000512 | bytes 90000008 | solution.py:675
  536.1 48.4 %conditional.4 = ((bf16[512,1536]{1,0:T(8,128)(2,1)}, bf16[512,1536]{1,0:T(8,128)(2,1)}, bf16[16,512,1536]{2,1,0:T(8,128)(2,1)}, bf16[16,512,1536]{2,1,0:T(8,128...) conditional(s32[]{:T(128)} %convert_element_type.32, ...), branch_computations={%region_1.1_spmd, %region_2.2_spmd} | conditional | flops 31000000512 | bytes 90000008 | solution.py:675
  623.0 48.4 %conditional.4 = ((bf16[512,1536]{1,0:T(8,128)(2,1)}, bf16[512,1536]{1,0:T(8,128)(2,1)}, bf16[16,512,1536]{2,1,0:T(8,128)(2,1)}, bf16[16,512,1536]{2,1,0:T(8,128...) conditional(s32[]{:T(128)} %convert_element_type.32, ...), branch_computations={%region_1.1_spmd, %region_2.2_spmd} | conditional | flops 31000000512 | bytes 90000008 | solution.py:675
  623.0 48.4 %layer_fwd.1 = (bf16[512,1536]{1,0:T(8,128)(2,1)}, bf16[512,1536]{1,0:T(8,128)(2,1)}, bf16[16,512,1536]{2,1,0:T(8,128)(2,1)}, bf16[16,512,1536]{2,1,0:T(8,128)(2...) custom-call(s32[3]{0:T(128)S(1)} %get-tuple-element.952.idx, ...), custom_call_target="tpu_custom_call", output_to_operand_aliasing={{0}: (16, {}), {1}: (17, {}), {2}: (18, {}), {3}: (19, {}),... | custom-call | flops 31000000512 | bytes 90000000 | tf_op jit(solution)/shard_map/while/body/eval_jaxpr/cond/branch_1_fun/layer_fwd/pallas_call | solution.py:316
  709.9 48.4 %conditional.4 = ((bf16[512,1536]{1,0:T(8,128)(2,1)}, bf16[512,1536]{1,0:T(8,128)(2,1)}, bf16[16,512,1536]{2,1,0:T(8,128)(2,1)}, bf16[16,512,1536]{2,1,0:T(8,128...) conditional(s32[]{:T(128)} %convert_element_type.32, ...), branch_computations={%region_1.1_spmd, %region_2.2_spmd} | conditional | flops 31000000512 | bytes 90000008 | solution.py:675
  709.9 48.4 %layer_fwd.1 = (bf16[512,1536]{1,0:T(8,128)(2,1)}, bf16[512,1536]{1,0:T(8,128)(2,1)}, bf16[16,512,1536]{2,1,0:T(8,128)(2,1)}, bf16[16,512,1536]{2,1,0:T(8,128)(2...) custom-call(s32[3]{0:T(128)S(1)} %get-tuple-element.952.idx, ...), custom_call_target="tpu_custom_call", output_to_operand_aliasing={{0}: (16, {}), {1}: (17, {}), {2}: (18, {}), {3}: (19, {}),... | custom-call | flops 31000000512 | bytes 90000000 | tf_op jit(solution)/shard_map/while/body/eval_jaxpr/cond/branch_1_fun/layer_fwd/pallas_call | solution.py:316
  796.9 48.4 %conditional.4 = ((bf16[512,1536]{1,0:T(8,128)(2,1)}, bf16[512,1536]{1,0:T(8,128)(2,1)}, bf16[16,512,1536]{2,1,0:T(8,128)(2,1)}, bf16[16,512,1536]{2,1,0:T(8,128...) conditional(s32[]{:T(128)} %convert_element_type.32, ...), branch_computations={%region_1.1_spmd, %region_2.2_spmd} | conditional | flops 31000000512 | bytes 90000008 | solution.py:675
  796.9 48.4 %layer_fwd.1 = (bf16[512,1536]{1,0:T(8,128)(2,1)}, bf16[512,1536]{1,0:T(8,128)(2,1)}, bf16[16,512,1536]{2,1,0:T(8,128)(2,1)}, bf16[16,512,1536]{2,1,0:T(8,128)(2...) custom-call(s32[3]{0:T(128)S(1)} %get-tuple-element.952.idx, ...), custom_call_target="tpu_custom_call", output_to_operand_aliasing={{0}: (16, {}), {1}: (17, {}), {2}: (18, {}), {3}: (19, {}),... | custom-call | flops 31000000512 | bytes 90000000 | tf_op jit(solution)/shard_map/while/body/eval_jaxpr/cond/branch_1_fun/layer_fwd/pallas_call | solution.py:316
  883.8 48.4 %conditional.4 = ((bf16[512,1536]{1,0:T(8,128)(2,1)}, bf16[512,1536]{1,0:T(8,128)(2,1)}, bf16[16,512,1536]{2,1,0:T(8,128)(2,1)}, bf16[16,512,1536]{2,1,0:T(8,128...) conditional(s32[]{:T(128)} %convert_element_type.32, ...), branch_computations={%region_1.1_spmd, %region_2.2_spmd} | conditional | flops 31000000512 | bytes 90000008 | solution.py:675
  968.3 48.4 %conditional.4 = ((bf16[512,1536]{1,0:T(8,128)(2,1)}, bf16[512,1536]{1,0:T(8,128)(2,1)}, bf16[16,512,1536]{2,1,0:T(8,128)(2,1)}, bf16[16,512,1536]{2,1,0:T(8,128...) conditional(s32[]{:T(128)} %convert_element_type.32, ...), branch_computations={%region_1.1_spmd, %region_2.2_spmd} | conditional | flops 31000000512 | bytes 90000008 | solution.py:675
  1016.7 111.7 %collective-permute-start = (bf16[512,1536]{1,0:T(8,128)(2,1)}, bf16[512,1536]{1,0:T(8,128)(2,1)}, u32[]{:S(2)}, u32[]{:S(2)}) collective-permute-start(bf16[512,1536]{1,0:T(8,128)(2,1)} %get-tuple-element.1677), channel_id=1, source_target_pairs={{0,1},{1,2},{2,3},{3,4},{4,5},{5,6},{6,7}} | collective-permute-start | bytes 4718600 | tf_op jit(solution)/shard_map/while/body/eval_jaxpr/ppermute | solution.py:689
  1146.8 48.4 %conditional.4 = ((bf16[512,1536]{1,0:T(8,128)(2,1)}, bf16[512,1536]{1,0:T(8,128)(2,1)}, bf16[16,512,1536]{2,1,0:T(8,128)(2,1)}, bf16[16,512,1536]{2,1,0:T(8,128...) conditional(s32[]{:T(128)} %convert_element_type.32, ...), branch_computations={%region_1.1_spmd, %region_2.2_spmd} | conditional | flops 31000000512 | bytes 90000008 | solution.py:675
  1195.2 96.5 %collective-permute-start = (bf16[512,1536]{1,0:T(8,128)(2,1)}, bf16[512,1536]{1,0:T(8,128)(2,1)}, u32[]{:S(2)}, u32[]{:S(2)}) collective-permute-start(bf16[512,1536]{1,0:T(8,128)(2,1)} %get-tuple-element.1677), channel_id=1, source_target_pairs={{0,1},{1,2},{2,3},{3,4},{4,5},{5,6},{6,7}} | collective-permute-start | bytes 4718600 | tf_op jit(solution)/shard_map/while/body/eval_jaxpr/ppermute | solution.py:689
  1325.2 48.4 %conditional.4 = ((bf16[512,1536]{1,0:T(8,128)(2,1)}, bf16[512,1536]{1,0:T(8,128)(2,1)}, bf16[16,512,1536]{2,1,0:T(8,128)(2,1)}, bf16[16,512,1536]{2,1,0:T(8,128...) conditional(s32[]{:T(128)} %convert_element_type.32, ...), branch_computations={%region_1.1_spmd, %region_2.2_spmd} | conditional | flops 31000000512 | bytes 90000008 | solution.py:675
  1373.6 64.4 %collective-permute-start = (bf16[512,1536]{1,0:T(8,128)(2,1)}, bf16[512,1536]{1,0:T(8,128)(2,1)}, u32[]{:S(2)}, u32[]{:S(2)}) collective-permute-start(bf16[512,1536]{1,0:T(8,128)(2,1)} %get-tuple-element.1677), channel_id=1, source_target_pairs={{0,1},{1,2},{2,3},{3,4},{4,5},{5,6},{6,7}} | collective-permute-start | bytes 4718600 | tf_op jit(solution)/shard_map/while/body/eval_jaxpr/ppermute | solution.py:689
  1439.4 63.0 %conditional.5 = ((bf16[512,1536]{1,0:T(8,128)(2,1)}, bf16[16,512,1536]{2,1,0:T(8,128)(2,1)}, bf16[16,512,1536]{2,1,0:T(8,128)(2,1)}, bf16[16,512,6144]{2,1,0:T(...) conditional(s32[]{:T(128)} %convert_element_type.33, ...), branch_computations={%region_3.3_spmd, %region_4.4_spmd} | conditional | flops 35999997952 | bytes 110000008 | solution.py:683
  1439.4 63.0 %layer_bwd.1 = (bf16[512,1536]{1,0:T(8,128)(2,1)}, bf16[16,512,1536]{2,1,0:T(8,128)(2,1)}, bf16[16,512,1536]{2,1,0:T(8,128)(2,1)}, bf16[16,512,6144]{2,1,0:T(8,1...) custom-call(s32[3]{0:T(128)S(1)} %get-tuple-element.979.idx, ...), custom_call_target="tpu_custom_call", output_to_operand_aliasing={{0}: (16, {}), {1}: (17, {}), {2}: (18, {}), {3}: (19, {}),... | custom-call | flops 35999997952 | bytes 110000000 | tf_op jit(solution)/shard_map/while/body/eval_jaxpr/cond/branch_1_fun/layer_bwd/pallas_call | solution.py:591
  1504.7 48.4 %conditional.4 = ((bf16[512,1536]{1,0:T(8,128)(2,1)}, bf16[512,1536]{1,0:T(8,128)(2,1)}, bf16[16,512,1536]{2,1,0:T(8,128)(2,1)}, bf16[16,512,1536]{2,1,0:T(8,128...) conditional(s32[]{:T(128)} %convert_element_type.32, ...), branch_computations={%region_1.1_spmd, %region_2.2_spmd} | conditional | flops 31000000512 | bytes 90000008 | solution.py:675
  1504.7 48.4 %layer_fwd.1 = (bf16[512,1536]{1,0:T(8,128)(2,1)}, bf16[512,1536]{1,0:T(8,128)(2,1)}, bf16[16,512,1536]{2,1,0:T(8,128)(2,1)}, bf16[16,512,1536]{2,1,0:T(8,128)(2...) custom-call(s32[3]{0:T(128)S(1)} %get-tuple-element.952.idx, ...), custom_call_target="tpu_custom_call", output_to_operand_aliasing={{0}: (16, {}), {1}: (17, {}), {2}: (18, {}), {3}: (19, {}),... | custom-call | flops 31000000512 | bytes 90000000 | tf_op jit(solution)/shard_map/while/body/eval_jaxpr/cond/branch_1_fun/layer_fwd/pallas_call | solution.py:316
  1559.8 63.0 %conditional.5 = ((bf16[512,1536]{1,0:T(8,128)(2,1)}, bf16[16,512,1536]{2,1,0:T(8,128)(2,1)}, bf16[16,512,1536]{2,1,0:T(8,128)(2,1)}, bf16[16,512,6144]{2,1,0:T(...) conditional(s32[]{:T(128)} %convert_element_type.33, ...), branch_computations={%region_3.3_spmd, %region_4.4_spmd} | conditional | flops 35999997952 | bytes 110000008 | solution.py:683
  1559.8 63.0 %layer_bwd.1 = (bf16[512,1536]{1,0:T(8,128)(2,1)}, bf16[16,512,1536]{2,1,0:T(8,128)(2,1)}, bf16[16,512,1536]{2,1,0:T(8,128)(2,1)}, bf16[16,512,6144]{2,1,0:T(8,1...) custom-call(s32[3]{0:T(128)S(1)} %get-tuple-element.979.idx, ...), custom_call_target="tpu_custom_call", output_to_operand_aliasing={{0}: (16, {}), {1}: (17, {}), {2}: (18, {}), {3}: (19, {}),... | custom-call | flops 35999997952 | bytes 110000000 | tf_op jit(solution)/shard_map/while/body/eval_jaxpr/cond/branch_1_fun/layer_bwd/pallas_call | solution.py:591
  1627.8 51.0 %collective-permute-start = (bf16[512,1536]{1,0:T(8,128)(2,1)}, bf16[512,1536]{1,0:T(8,128)(2,1)}, u32[]{:S(2)}, u32[]{:S(2)}) collective-permute-start(bf16[512,1536]{1,0:T(8,128)(2,1)} %get-tuple-element.1677), channel_id=1, source_target_pairs={{0,1},{1,2},{2,3},{3,4},{4,5},{5,6},{6,7}} | collective-permute-start | bytes 4718600 | tf_op jit(solution)/shard_map/while/body/eval_jaxpr/ppermute | solution.py:689
  1680.3 63.0 %conditional.5 = ((bf16[512,1536]{1,0:T(8,128)(2,1)}, bf16[16,512,1536]{2,1,0:T(8,128)(2,1)}, bf16[16,512,1536]{2,1,0:T(8,128)(2,1)}, bf16[16,512,6144]{2,1,0:T(...) conditional(s32[]{:T(128)} %convert_element_type.33, ...), branch_computations={%region_3.3_spmd, %region_4.4_spmd} | conditional | flops 35999997952 | bytes 110000008 | solution.py:683
  1680.3 63.0 %layer_bwd.1 = (bf16[512,1536]{1,0:T(8,128)(2,1)}, bf16[16,512,1536]{2,1,0:T(8,128)(2,1)}, bf16[16,512,1536]{2,1,0:T(8,128)(2,1)}, bf16[16,512,6144]{2,1,0:T(8,1...) custom-call(s32[3]{0:T(128)S(1)} %get-tuple-element.979.idx, ...), custom_call_target="tpu_custom_call", output_to_operand_aliasing={{0}: (16, {}), {1}: (17, {}), {2}: (18, {}), {3}: (19, {}),... | custom-call | flops 35999997952 | bytes 110000000 | tf_op jit(solution)/shard_map/while/body/eval_jaxpr/cond/branch_1_fun/layer_bwd/pallas_call | solution.py:591
  1755.0 63.0 %conditional.5 = ((bf16[512,1536]{1,0:T(8,128)(2,1)}, bf16[16,512,1536]{2,1,0:T(8,128)(2,1)}, bf16[16,512,1536]{2,1,0:T(8,128)(2,1)}, bf16[16,512,6144]{2,1,0:T(...) conditional(s32[]{:T(128)} %convert_element_type.33, ...), branch_computations={%region_3.3_spmd, %region_4.4_spmd} | conditional | flops 35999997952 | bytes 110000008 | solution.py:683
  1755.0 63.0 %layer_bwd.1 = (bf16[512,1536]{1,0:T(8,128)(2,1)}, bf16[16,512,1536]{2,1,0:T(8,128)(2,1)}, bf16[16,512,1536]{2,1,0:T(8,128)(2,1)}, bf16[16,512,6144]{2,1,0:T(8,1...) custom-call(s32[3]{0:T(128)S(1)} %get-tuple-element.979.idx, ...), custom_call_target="tpu_custom_call", output_to_operand_aliasing={{0}: (16, {}), {1}: (17, {}), {2}: (18, {}), {3}: (19, {}),... | custom-call | flops 35999997952 | bytes 110000000 | tf_op jit(solution)/shard_map/while/body/eval_jaxpr/cond/branch_1_fun/layer_bwd/pallas_call | solution.py:591
  1823.0 51.0 %collective-permute-start = (bf16[512,1536]{1,0:T(8,128)(2,1)}, bf16[512,1536]{1,0:T(8,128)(2,1)}, u32[]{:S(2)}, u32[]{:S(2)}) collective-permute-start(bf16[512,1536]{1,0:T(8,128)(2,1)} %get-tuple-element.1677), channel_id=1, source_target_pairs={{0,1},{1,2},{2,3},{3,4},{4,5},{5,6},{6,7}} | collective-permute-start | bytes 4718600 | tf_op jit(solution)/shard_map/while/body/eval_jaxpr/ppermute | solution.py:689
  1875.4 63.0 %conditional.5 = ((bf16[512,1536]{1,0:T(8,128)(2,1)}, bf16[16,512,1536]{2,1,0:T(8,128)(2,1)}, bf16[16,512,1536]{2,1,0:T(8,128)(2,1)}, bf16[16,512,6144]{2,1,0:T(...) conditional(s32[]{:T(128)} %convert_element_type.33, ...), branch_computations={%region_3.3_spmd, %region_4.4_spmd} | conditional | flops 35999997952 | bytes 110000008 | solution.py:683
  1875.4 63.0 %layer_bwd.1 = (bf16[512,1536]{1,0:T(8,128)(2,1)}, bf16[16,512,1536]{2,1,0:T(8,128)(2,1)}, bf16[16,512,1536]{2,1,0:T(8,128)(2,1)}, bf16[16,512,6144]{2,1,0:T(8,1...) custom-call(s32[3]{0:T(128)S(1)} %get-tuple-element.979.idx, ...), custom_call_target="tpu_custom_call", output_to_operand_aliasing={{0}: (16, {}), {1}: (17, {}), {2}: (18, {}), {3}: (19, {}),... | custom-call | flops 35999997952 | bytes 110000000 | tf_op jit(solution)/shard_map/while/body/eval_jaxpr/cond/branch_1_fun/layer_bwd/pallas_call | solution.py:591
  1969.8 63.0 %conditional.5 = ((bf16[512,1536]{1,0:T(8,128)(2,1)}, bf16[16,512,1536]{2,1,0:T(8,128)(2,1)}, bf16[16,512,1536]{2,1,0:T(8,128)(2,1)}, bf16[16,512,6144]{2,1,0:T(...) conditional(s32[]{:T(128)} %convert_element_type.33, ...), branch_computations={%region_3.3_spmd, %region_4.4_spmd} | conditional | flops 35999997952 | bytes 110000008 | solution.py:683
  1969.8 63.0 %layer_bwd.1 = (bf16[512,1536]{1,0:T(8,128)(2,1)}, bf16[16,512,1536]{2,1,0:T(8,128)(2,1)}, bf16[16,512,1536]{2,1,0:T(8,128)(2,1)}, bf16[16,512,6144]{2,1,0:T(8,1...) custom-call(s32[3]{0:T(128)S(1)} %get-tuple-element.979.idx, ...), custom_call_target="tpu_custom_call", output_to_operand_aliasing={{0}: (16, {}), {1}: (17, {}), {2}: (18, {}), {3}: (19, {}),... | custom-call | flops 35999997952 | bytes 110000000 | tf_op jit(solution)/shard_map/while/body/eval_jaxpr/cond/branch_1_fun/layer_bwd/pallas_call | solution.py:591
  2081.8 63.0 %conditional.5 = ((bf16[512,1536]{1,0:T(8,128)(2,1)}, bf16[16,512,1536]{2,1,0:T(8,128)(2,1)}, bf16[16,512,1536]{2,1,0:T(8,128)(2,1)}, bf16[16,512,6144]{2,1,0:T(...) conditional(s32[]{:T(128)} %convert_element_type.33, ...), branch_computations={%region_3.3_spmd, %region_4.4_spmd} | conditional | flops 35999997952 | bytes 110000008 | solution.py:683
  2081.8 63.0 %layer_bwd.1 = (bf16[512,1536]{1,0:T(8,128)(2,1)}, bf16[16,512,1536]{2,1,0:T(8,128)(2,1)}, bf16[16,512,1536]{2,1,0:T(8,128)(2,1)}, bf16[16,512,6144]{2,1,0:T(8,1...) custom-call(s32[3]{0:T(128)S(1)} %get-tuple-element.979.idx, ...), custom_call_target="tpu_custom_call", output_to_operand_aliasing={{0}: (16, {}), {1}: (17, {}), {2}: (18, {}), {3}: (19, {}),... | custom-call | flops 35999997952 | bytes 110000000 | tf_op jit(solution)/shard_map/while/body/eval_jaxpr/cond/branch_1_fun/layer_bwd/pallas_call | solution.py:591
  2166.9 63.0 %conditional.5 = ((bf16[512,1536]{1,0:T(8,128)(2,1)}, bf16[16,512,1536]{2,1,0:T(8,128)(2,1)}, bf16[16,512,1536]{2,1,0:T(8,128)(2,1)}, bf16[16,512,6144]{2,1,0:T(...) conditional(s32[]{:T(128)} %convert_element_type.33, ...), branch_computations={%region_3.3_spmd, %region_4.4_spmd} | conditional | flops 35999997952 | bytes 110000008 | solution.py:683
  2166.9 63.0 %layer_bwd.1 = (bf16[512,1536]{1,0:T(8,128)(2,1)}, bf16[16,512,1536]{2,1,0:T(8,128)(2,1)}, bf16[16,512,1536]{2,1,0:T(8,128)(2,1)}, bf16[16,512,6144]{2,1,0:T(8,1...) custom-call(s32[3]{0:T(128)S(1)} %get-tuple-element.979.idx, ...), custom_call_target="tpu_custom_call", output_to_operand_aliasing={{0}: (16, {}), {1}: (17, {}), {2}: (18, {}), {3}: (19, {}),... | custom-call | flops 35999997952 | bytes 110000000 | tf_op jit(solution)/shard_map/while/body/eval_jaxpr/cond/branch_1_fun/layer_bwd/pallas_call | solution.py:591
  2276.9 63.0 %conditional.5 = ((bf16[512,1536]{1,0:T(8,128)(2,1)}, bf16[16,512,1536]{2,1,0:T(8,128)(2,1)}, bf16[16,512,1536]{2,1,0:T(8,128)(2,1)}, bf16[16,512,6144]{2,1,0:T(...) conditional(s32[]{:T(128)} %convert_element_type.33, ...), branch_computations={%region_3.3_spmd, %region_4.4_spmd} | conditional | flops 35999997952 | bytes 110000008 | solution.py:683
  2276.9 63.0 %layer_bwd.1 = (bf16[512,1536]{1,0:T(8,128)(2,1)}, bf16[16,512,1536]{2,1,0:T(8,128)(2,1)}, bf16[16,512,1536]{2,1,0:T(8,128)(2,1)}, bf16[16,512,6144]{2,1,0:T(8,1...) custom-call(s32[3]{0:T(128)S(1)} %get-tuple-element.979.idx, ...), custom_call_target="tpu_custom_call", output_to_operand_aliasing={{0}: (16, {}), {1}: (17, {}), {2}: (18, {}), {3}: (19, {}),... | custom-call | flops 35999997952 | bytes 110000000 | tf_op jit(solution)/shard_map/while/body/eval_jaxpr/cond/branch_1_fun/layer_bwd/pallas_call | solution.py:591
  2370.9 63.0 %conditional.5 = ((bf16[512,1536]{1,0:T(8,128)(2,1)}, bf16[16,512,1536]{2,1,0:T(8,128)(2,1)}, bf16[16,512,1536]{2,1,0:T(8,128)(2,1)}, bf16[16,512,6144]{2,1,0:T(...) conditional(s32[]{:T(128)} %convert_element_type.33, ...), branch_computations={%region_3.3_spmd, %region_4.4_spmd} | conditional | flops 35999997952 | bytes 110000008 | solution.py:683
  2370.9 63.0 %layer_bwd.1 = (bf16[512,1536]{1,0:T(8,128)(2,1)}, bf16[16,512,1536]{2,1,0:T(8,128)(2,1)}, bf16[16,512,1536]{2,1,0:T(8,128)(2,1)}, bf16[16,512,6144]{2,1,0:T(8,1...) custom-call(s32[3]{0:T(128)S(1)} %get-tuple-element.979.idx, ...), custom_call_target="tpu_custom_call", output_to_operand_aliasing={{0}: (16, {}), {1}: (17, {}), {2}: (18, {}), {3}: (19, {}),... | custom-call | flops 35999997952 | bytes 110000000 | tf_op jit(solution)/shard_map/while/body/eval_jaxpr/cond/branch_1_fun/layer_bwd/pallas_call | solution.py:591
  2482.8 63.0 %conditional.5 = ((bf16[512,1536]{1,0:T(8,128)(2,1)}, bf16[16,512,1536]{2,1,0:T(8,128)(2,1)}, bf16[16,512,1536]{2,1,0:T(8,128)(2,1)}, bf16[16,512,6144]{2,1,0:T(...) conditional(s32[]{:T(128)} %convert_element_type.33, ...), branch_computations={%region_3.3_spmd, %region_4.4_spmd} | conditional | flops 35999997952 | bytes 110000008 | solution.py:683
  2482.9 63.0 %layer_bwd.1 = (bf16[512,1536]{1,0:T(8,128)(2,1)}, bf16[16,512,1536]{2,1,0:T(8,128)(2,1)}, bf16[16,512,1536]{2,1,0:T(8,128)(2,1)}, bf16[16,512,6144]{2,1,0:T(8,1...) custom-call(s32[3]{0:T(128)S(1)} %get-tuple-element.979.idx, ...), custom_call_target="tpu_custom_call", output_to_operand_aliasing={{0}: (16, {}), {1}: (17, {}), {2}: (18, {}), {3}: (19, {}),... | custom-call | flops 35999997952 | bytes 110000000 | tf_op jit(solution)/shard_map/while/body/eval_jaxpr/cond/branch_1_fun/layer_bwd/pallas_call | solution.py:591
  2568.8 63.0 %conditional.5 = ((bf16[512,1536]{1,0:T(8,128)(2,1)}, bf16[16,512,1536]{2,1,0:T(8,128)(2,1)}, bf16[16,512,1536]{2,1,0:T(8,128)(2,1)}, bf16[16,512,6144]{2,1,0:T(...) conditional(s32[]{:T(128)} %convert_element_type.33, ...), branch_computations={%region_3.3_spmd, %region_4.4_spmd} | conditional | flops 35999997952 | bytes 110000008 | solution.py:683
  2568.8 63.0 %layer_bwd.1 = (bf16[512,1536]{1,0:T(8,128)(2,1)}, bf16[16,512,1536]{2,1,0:T(8,128)(2,1)}, bf16[16,512,1536]{2,1,0:T(8,128)(2,1)}, bf16[16,512,6144]{2,1,0:T(8,1...) custom-call(s32[3]{0:T(128)S(1)} %get-tuple-element.979.idx, ...), custom_call_target="tpu_custom_call", output_to_operand_aliasing={{0}: (16, {}), {1}: (17, {}), {2}: (18, {}), {3}: (19, {}),... | custom-call | flops 35999997952 | bytes 110000000 | tf_op jit(solution)/shard_map/while/body/eval_jaxpr/cond/branch_1_fun/layer_bwd/pallas_call | solution.py:591
  2677.9 63.0 %conditional.5 = ((bf16[512,1536]{1,0:T(8,128)(2,1)}, bf16[16,512,1536]{2,1,0:T(8,128)(2,1)}, bf16[16,512,1536]{2,1,0:T(8,128)(2,1)}, bf16[16,512,6144]{2,1,0:T(...) conditional(s32[]{:T(128)} %convert_element_type.33, ...), branch_computations={%region_3.3_spmd, %region_4.4_spmd} | conditional | flops 35999997952 | bytes 110000008 | solution.py:683
  2677.9 63.0 %layer_bwd.1 = (bf16[512,1536]{1,0:T(8,128)(2,1)}, bf16[16,512,1536]{2,1,0:T(8,128)(2,1)}, bf16[16,512,1536]{2,1,0:T(8,128)(2,1)}, bf16[16,512,6144]{2,1,0:T(8,1...) custom-call(s32[3]{0:T(128)S(1)} %get-tuple-element.979.idx, ...), custom_call_target="tpu_custom_call", output_to_operand_aliasing={{0}: (16, {}), {1}: (17, {}), {2}: (18, {}), {3}: (19, {}),... | custom-call | flops 35999997952 | bytes 110000000 | tf_op jit(solution)/shard_map/while/body/eval_jaxpr/cond/branch_1_fun/layer_bwd/pallas_call | solution.py:591
  2772.2 63.0 %conditional.5 = ((bf16[512,1536]{1,0:T(8,128)(2,1)}, bf16[16,512,1536]{2,1,0:T(8,128)(2,1)}, bf16[16,512,1536]{2,1,0:T(8,128)(2,1)}, bf16[16,512,6144]{2,1,0:T(...) conditional(s32[]{:T(128)} %convert_element_type.33, ...), branch_computations={%region_3.3_spmd, %region_4.4_spmd} | conditional | flops 35999997952 | bytes 110000008 | solution.py:683
  2772.2 63.0 %layer_bwd.1 = (bf16[512,1536]{1,0:T(8,128)(2,1)}, bf16[16,512,1536]{2,1,0:T(8,128)(2,1)}, bf16[16,512,1536]{2,1,0:T(8,128)(2,1)}, bf16[16,512,6144]{2,1,0:T(8,1...) custom-call(s32[3]{0:T(128)S(1)} %get-tuple-element.979.idx, ...), custom_call_target="tpu_custom_call", output_to_operand_aliasing={{0}: (16, {}), {1}: (17, {}), {2}: (18, {}), {3}: (19, {}),... | custom-call | flops 35999997952 | bytes 110000000 | tf_op jit(solution)/shard_map/while/body/eval_jaxpr/cond/branch_1_fun/layer_bwd/pallas_call | solution.py:591
  2884.2 63.0 %conditional.5 = ((bf16[512,1536]{1,0:T(8,128)(2,1)}, bf16[16,512,1536]{2,1,0:T(8,128)(2,1)}, bf16[16,512,1536]{2,1,0:T(8,128)(2,1)}, bf16[16,512,6144]{2,1,0:T(...) conditional(s32[]{:T(128)} %convert_element_type.33, ...), branch_computations={%region_3.3_spmd, %region_4.4_spmd} | conditional | flops 35999997952 | bytes 110000008 | solution.py:683
  2884.2 63.0 %layer_bwd.1 = (bf16[512,1536]{1,0:T(8,128)(2,1)}, bf16[16,512,1536]{2,1,0:T(8,128)(2,1)}, bf16[16,512,1536]{2,1,0:T(8,128)(2,1)}, bf16[16,512,6144]{2,1,0:T(8,1...) custom-call(s32[3]{0:T(128)S(1)} %get-tuple-element.979.idx, ...), custom_call_target="tpu_custom_call", output_to_operand_aliasing={{0}: (16, {}), {1}: (17, {}), {2}: (18, {}), {3}: (19, {}),... | custom-call | flops 35999997952 | bytes 110000000 | tf_op jit(solution)/shard_map/while/body/eval_jaxpr/cond/branch_1_fun/layer_bwd/pallas_call | solution.py:591
  2995.8 63.0 %conditional.5 = ((bf16[512,1536]{1,0:T(8,128)(2,1)}, bf16[16,512,1536]{2,1,0:T(8,128)(2,1)}, bf16[16,512,1536]{2,1,0:T(8,128)(2,1)}, bf16[16,512,6144]{2,1,0:T(...) conditional(s32[]{:T(128)} %convert_element_type.33, ...), branch_computations={%region_3.3_spmd, %region_4.4_spmd} | conditional | flops 35999997952 | bytes 110000008 | solution.py:683
  2995.8 63.0 %layer_bwd.1 = (bf16[512,1536]{1,0:T(8,128)(2,1)}, bf16[16,512,1536]{2,1,0:T(8,128)(2,1)}, bf16[16,512,1536]{2,1,0:T(8,128)(2,1)}, bf16[16,512,6144]{2,1,0:T(8,1...) custom-call(s32[3]{0:T(128)S(1)} %get-tuple-element.979.idx, ...), custom_call_target="tpu_custom_call", output_to_operand_aliasing={{0}: (16, {}), {1}: (17, {}), {2}: (18, {}), {3}: (19, {}),... | custom-call | flops 35999997952 | bytes 110000000 | tf_op jit(solution)/shard_map/while/body/eval_jaxpr/cond/branch_1_fun/layer_bwd/pallas_call | solution.py:591
  3080.6 171.7 %convolution_bitcast_fusion = f32[1,6144,1536]{2,1,0:T(8,128)} fusion(bf16[16,512,6144]{2,1,0:T(8,128)(2,1)} %get-tuple-element.1153, bf16[16,512,1536]{2,1,0:T(8,128)(2,1)} %get-tuple-element.1154), kind=kOutput, calls=%fused_computation.2 | convolution fusion | flops 154618822656 | bytes 163577856 | tf_op jit(solution)/shard_map/cka,ckb->ab/dot_general | solution.py:700
  3252.3 172.0 %convolution_bitcast_fusion.1 = f32[1,1536,6144]{2,1,0:T(8,128)} fusion(bf16[16,512,1536]{2,1,0:T(8,128)(2,1)} %get-tuple-element.1150, bf16[16,512,6144]{2,1,0:T(8,128)(2,1)} %get-tuple-element.1151), kind=kOutput, calls=%fused_computation.3 | convolution fusion | flops 154618822656 | bytes 163577856 | tf_op jit(solution)/shard_map/cka,ckb->ab/dot_general | solution.py:700
  3424.4 132.1 %convolution_bitcast_fusion.2 = f32[1,1536,4608]{2,1,0:T(8,128)} fusion(bf16[16,512,1536]{2,1,0:T(8,128)(2,1)} %get-tuple-element.1145, bf16[16,512,4608]{2,1,0:T(8,128)(2,1)} %get-tuple-element.1146), kind=kOutput, calls=%fused_computation.5 | convolution fusion | flops 115964116992 | bytes 128974848 | tf_op jit(solution)/shard_map/cka,ckb->ab/dot_general | solution.py:700
  3558.9 48.7 %fusion.1 = f32[1536,1536,1]{1,0,2:T(8,128)} fusion(bf16[16,512,1536]{2,1,0:T(8,128)(2,1)} %get-tuple-element.1148, bf16[16,512,1536]{2,1,0:T(8,128)(2,1)} %get-tuple-element.1149), kind=kOutput, calls=%fused_computation.7 | convolution fusion | flops 38654705664 | bytes 59768832 | tf_op jit(solution)/shard_map/cka,ckb->ab/dot_general | solution.py:700
  (424 shorter events, 1457.1 us)
Async XLA Ops:
  7.2 3600.4 %all-reduce.2.cloned.1.call-start = ((), (), s32[]{:S(2)}) async-start(), calls=%async_computation | async-start | bytes 50331648 | tf_op jit(solution)/shard_map/psum | solution.py:697
  7.3 53.6 %collective-permute-start.2 = (bf16[512,1536]{1,0:T(8,128)(2,1)}, bf16[512,1536]{1,0:T(8,128)(2,1)}, u32[]{:S(2)}, u32[]{:S(2)}) collective-permute-start(bf16[512,1536]{1,0:T(8,128)(2,1)} %get-tuple-element.1632), channel_id=1, source_target_pairs={{1,0},{2,1},{3,2},{4,3},{5,4},{6,5},{7,6}} | collective-permute-start | bytes 4718600 | tf_op jit(solution)/shard_map/while/body/eval_jaxpr/ppermute | solution.py:687
  64.8 55.4 %collective-permute-start.2 = (bf16[512,1536]{1,0:T(8,128)(2,1)}, bf16[512,1536]{1,0:T(8,128)(2,1)}, u32[]{:S(2)}, u32[]{:S(2)}) collective-permute-start(bf16[512,1536]{1,0:T(8,128)(2,1)} %get-tuple-element.1632), channel_id=1, source_target_pairs={{1,0},{2,1},{3,2},{4,3},{5,4},{6,5},{7,6}} | collective-permute-start | bytes 4718600 | tf_op jit(solution)/shard_map/while/body/eval_jaxpr/ppermute | solution.py:687
  124.0 70.2 %collective-permute-start.2 = (bf16[512,1536]{1,0:T(8,128)(2,1)}, bf16[512,1536]{1,0:T(8,128)(2,1)}, u32[]{:S(2)}, u32[]{:S(2)}) collective-permute-start(bf16[512,1536]{1,0:T(8,128)(2,1)} %get-tuple-element.1632), channel_id=1, source_target_pairs={{1,0},{2,1},{3,2},{4,3},{5,4},{6,5},{7,6}} | collective-permute-start | bytes 4718600 | tf_op jit(solution)/shard_map/while/body/eval_jaxpr/ppermute | solution.py:687
  198.2 71.9 %collective-permute-start.2 = (bf16[512,1536]{1,0:T(8,128)(2,1)}, bf16[512,1536]{1,0:T(8,128)(2,1)}, u32[]{:S(2)}, u32[]{:S(2)}) collective-permute-start(bf16[512,1536]{1,0:T(8,128)(2,1)} %get-tuple-element.1632), channel_id=1, source_target_pairs={{1,0},{2,1},{3,2},{4,3},{5,4},{6,5},{7,6}} | collective-permute-start | bytes 4718600 | tf_op jit(solution)/shard_map/while/body/eval_jaxpr/ppermute | solution.py:687
  274.0 83.0 %collective-permute-start.2 = (bf16[512,1536]{1,0:T(8,128)(2,1)}, bf16[512,1536]{1,0:T(8,128)(2,1)}, u32[]{:S(2)}, u32[]{:S(2)}) collective-permute-start(bf16[512,1536]{1,0:T(8,128)(2,1)} %get-tuple-element.1632), channel_id=1, source_target_pairs={{1,0},{2,1},{3,2},{4,3},{5,4},{6,5},{7,6}} | collective-permute-start | bytes 4718600 | tf_op jit(solution)/shard_map/while/body/eval_jaxpr/ppermute | solution.py:687
  323.8 33.6 collective-permute-start
  360.9 83.0 %collective-permute-start.2 = (bf16[512,1536]{1,0:T(8,128)(2,1)}, bf16[512,1536]{1,0:T(8,128)(2,1)}, u32[]{:S(2)}, u32[]{:S(2)}) collective-permute-start(bf16[512,1536]{1,0:T(8,128)(2,1)} %get-tuple-element.1632), channel_id=1, source_target_pairs={{1,0},{2,1},{3,2},{4,3},{5,4},{6,5},{7,6}} | collective-permute-start | bytes 4718600 | tf_op jit(solution)/shard_map/while/body/eval_jaxpr/ppermute | solution.py:687
  410.7 33.6 collective-permute-start
  447.8 83.0 %collective-permute-start.2 = (bf16[512,1536]{1,0:T(8,128)(2,1)}, bf16[512,1536]{1,0:T(8,128)(2,1)}, u32[]{:S(2)}, u32[]{:S(2)}) collective-permute-start(bf16[512,1536]{1,0:T(8,128)(2,1)} %get-tuple-element.1632), channel_id=1, source_target_pairs={{1,0},{2,1},{3,2},{4,3},{5,4},{6,5},{7,6}} | collective-permute-start | bytes 4718600 | tf_op jit(solution)/shard_map/while/body/eval_jaxpr/ppermute | solution.py:687
  497.6 33.6 collective-permute-start
  534.7 83.0 %collective-permute-start.2 = (bf16[512,1536]{1,0:T(8,128)(2,1)}, bf16[512,1536]{1,0:T(8,128)(2,1)}, u32[]{:S(2)}, u32[]{:S(2)}) collective-permute-start(bf16[512,1536]{1,0:T(8,128)(2,1)} %get-tuple-element.1632), channel_id=1, source_target_pairs={{1,0},{2,1},{3,2},{4,3},{5,4},{6,5},{7,6}} | collective-permute-start | bytes 4718600 | tf_op jit(solution)/shard_map/while/body/eval_jaxpr/ppermute | solution.py:687
  584.5 33.7 collective-permute-start
  621.6 82.9 %collective-permute-start.2 = (bf16[512,1536]{1,0:T(8,128)(2,1)}, bf16[512,1536]{1,0:T(8,128)(2,1)}, u32[]{:S(2)}, u32[]{:S(2)}) collective-permute-start(bf16[512,1536]{1,0:T(8,128)(2,1)} %get-tuple-element.1632), channel_id=1, source_target_pairs={{1,0},{2,1},{3,2},{4,3},{5,4},{6,5},{7,6}} | collective-permute-start | bytes 4718600 | tf_op jit(solution)/shard_map/while/body/eval_jaxpr/ppermute | solution.py:687
  708.5 83.1 %collective-permute-start.2 = (bf16[512,1536]{1,0:T(8,128)(2,1)}, bf16[512,1536]{1,0:T(8,128)(2,1)}, u32[]{:S(2)}, u32[]{:S(2)}) collective-permute-start(bf16[512,1536]{1,0:T(8,128)(2,1)} %get-tuple-element.1632), channel_id=1, source_target_pairs={{1,0},{2,1},{3,2},{4,3},{5,4},{6,5},{7,6}} | collective-permute-start | bytes 4718600 | tf_op jit(solution)/shard_map/while/body/eval_jaxpr/ppermute | solution.py:687
  758.3 33.8 collective-permute-start
  795.6 82.9 %collective-permute-start.2 = (bf16[512,1536]{1,0:T(8,128)(2,1)}, bf16[512,1536]{1,0:T(8,128)(2,1)}, u32[]{:S(2)}, u32[]{:S(2)}) collective-permute-start(bf16[512,1536]{1,0:T(8,128)(2,1)} %get-tuple-element.1632), channel_id=1, source_target_pairs={{1,0},{2,1},{3,2},{4,3},{5,4},{6,5},{7,6}} | collective-permute-start | bytes 4718600 | tf_op jit(solution)/shard_map/while/body/eval_jaxpr/ppermute | solution.py:687
  882.5 71.9 %collective-permute-start.2 = (bf16[512,1536]{1,0:T(8,128)(2,1)}, bf16[512,1536]{1,0:T(8,128)(2,1)}, u32[]{:S(2)}, u32[]{:S(2)}) collective-permute-start(bf16[512,1536]{1,0:T(8,128)(2,1)} %get-tuple-element.1632), channel_id=1, source_target_pairs={{1,0},{2,1},{3,2},{4,3},{5,4},{6,5},{7,6}} | collective-permute-start | bytes 4718600 | tf_op jit(solution)/shard_map/while/body/eval_jaxpr/ppermute | solution.py:687
  966.9 162.9 %collective-permute-start.2 = (bf16[512,1536]{1,0:T(8,128)(2,1)}, bf16[512,1536]{1,0:T(8,128)(2,1)}, u32[]{:S(2)}, u32[]{:S(2)}) collective-permute-start(bf16[512,1536]{1,0:T(8,128)(2,1)} %get-tuple-element.1632), channel_id=1, source_target_pairs={{1,0},{2,1},{3,2},{4,3},{5,4},{6,5},{7,6}} | collective-permute-start | bytes 4718600 | tf_op jit(solution)/shard_map/while/body/eval_jaxpr/ppermute | solution.py:687
  1016.7 113.6 %collective-permute-start = (bf16[512,1536]{1,0:T(8,128)(2,1)}, bf16[512,1536]{1,0:T(8,128)(2,1)}, u32[]{:S(2)}, u32[]{:S(2)}) collective-permute-start(bf16[512,1536]{1,0:T(8,128)(2,1)} %get-tuple-element.1677), channel_id=1, source_target_pairs={{0,1},{1,2},{2,3},{3,4},{4,5},{5,6},{6,7}} | collective-permute-start | bytes 4718600 | tf_op jit(solution)/shard_map/while/body/eval_jaxpr/ppermute | solution.py:689
  1145.4 147.7 %collective-permute-start.2 = (bf16[512,1536]{1,0:T(8,128)(2,1)}, bf16[512,1536]{1,0:T(8,128)(2,1)}, u32[]{:S(2)}, u32[]{:S(2)}) collective-permute-start(bf16[512,1536]{1,0:T(8,128)(2,1)} %get-tuple-element.1632), channel_id=1, source_target_pairs={{1,0},{2,1},{3,2},{4,3},{5,4},{6,5},{7,6}} | collective-permute-start | bytes 4718600 | tf_op jit(solution)/shard_map/while/body/eval_jaxpr/ppermute | solution.py:687
  1195.2 98.3 %collective-permute-start = (bf16[512,1536]{1,0:T(8,128)(2,1)}, bf16[512,1536]{1,0:T(8,128)(2,1)}, u32[]{:S(2)}, u32[]{:S(2)}) collective-permute-start(bf16[512,1536]{1,0:T(8,128)(2,1)} %get-tuple-element.1677), channel_id=1, source_target_pairs={{0,1},{1,2},{2,3},{3,4},{4,5},{5,6},{6,7}} | collective-permute-start | bytes 4718600 | tf_op jit(solution)/shard_map/while/body/eval_jaxpr/ppermute | solution.py:689
  1323.9 115.6 %collective-permute-start.2 = (bf16[512,1536]{1,0:T(8,128)(2,1)}, bf16[512,1536]{1,0:T(8,128)(2,1)}, u32[]{:S(2)}, u32[]{:S(2)}) collective-permute-start(bf16[512,1536]{1,0:T(8,128)(2,1)} %get-tuple-element.1632), channel_id=1, source_target_pairs={{1,0},{2,1},{3,2},{4,3},{5,4},{6,5},{7,6}} | collective-permute-start | bytes 4718600 | tf_op jit(solution)/shard_map/while/body/eval_jaxpr/ppermute | solution.py:687
  1373.6 128.8 %collective-permute-start = (bf16[512,1536]{1,0:T(8,128)(2,1)}, bf16[512,1536]{1,0:T(8,128)(2,1)}, u32[]{:S(2)}, u32[]{:S(2)}) collective-permute-start(bf16[512,1536]{1,0:T(8,128)(2,1)} %get-tuple-element.1677), channel_id=1, source_target_pairs={{0,1},{1,2},{2,3},{3,4},{4,5},{5,6},{6,7}} | collective-permute-start | bytes 4718600 | tf_op jit(solution)/shard_map/while/body/eval_jaxpr/ppermute | solution.py:689
  1438.0 64.4 %collective-permute-start.1 = (bf16[512,1536]{1,0:T(8,128)(2,1)}, bf16[512,1536]{1,0:T(8,128)(2,1)}, u32[]{:S(2)}, u32[]{:S(2)}) collective-permute-start(bf16[512,1536]{1,0:T(8,128)(2,1)} %get-tuple-element.1679), channel_id=1, source_target_pairs={{1,0},{2,1},{3,2},{4,3},{5,4},{6,5},{7,6}} | collective-permute-start | bytes 4718600 | tf_op jit(solution)/shard_map/while/body/eval_jaxpr/ppermute | solution.py:690
  1503.4 56.5 %collective-permute-start.2 = (bf16[512,1536]{1,0:T(8,128)(2,1)}, bf16[512,1536]{1,0:T(8,128)(2,1)}, u32[]{:S(2)}, u32[]{:S(2)}) collective-permute-start(bf16[512,1536]{1,0:T(8,128)(2,1)} %get-tuple-element.1632), channel_id=1, source_target_pairs={{1,0},{2,1},{3,2},{4,3},{5,4},{6,5},{7,6}} | collective-permute-start | bytes 4718600 | tf_op jit(solution)/shard_map/while/body/eval_jaxpr/ppermute | solution.py:687
  1553.1 69.7 %collective-permute-start = (bf16[512,1536]{1,0:T(8,128)(2,1)}, bf16[512,1536]{1,0:T(8,128)(2,1)}, u32[]{:S(2)}, u32[]{:S(2)}) collective-permute-start(bf16[512,1536]{1,0:T(8,128)(2,1)} %get-tuple-element.1677), channel_id=1, source_target_pairs={{0,1},{1,2},{2,3},{3,4},{4,5},{5,6},{6,7}} | collective-permute-start | bytes 4718600 | tf_op jit(solution)/shard_map/while/body/eval_jaxpr/ppermute | solution.py:689
  1558.5 64.4 %collective-permute-start.1 = (bf16[512,1536]{1,0:T(8,128)(2,1)}, bf16[512,1536]{1,0:T(8,128)(2,1)}, u32[]{:S(2)}, u32[]{:S(2)}) collective-permute-start(bf16[512,1536]{1,0:T(8,128)(2,1)} %get-tuple-element.1679), channel_id=1, source_target_pairs={{1,0},{2,1},{3,2},{4,3},{5,4},{6,5},{7,6}} | collective-permute-start | bytes 4718600 | tf_op jit(solution)/shard_map/while/body/eval_jaxpr/ppermute | solution.py:690
  1623.8 56.5 %collective-permute-start.2 = (bf16[512,1536]{1,0:T(8,128)(2,1)}, bf16[512,1536]{1,0:T(8,128)(2,1)}, u32[]{:S(2)}, u32[]{:S(2)}) collective-permute-start(bf16[512,1536]{1,0:T(8,128)(2,1)} %get-tuple-element.1632), channel_id=1, source_target_pairs={{1,0},{2,1},{3,2},{4,3},{5,4},{6,5},{7,6}} | collective-permute-start | bytes 4718600 | tf_op jit(solution)/shard_map/while/body/eval_jaxpr/ppermute | solution.py:687
  1627.8 115.5 %collective-permute-start = (bf16[512,1536]{1,0:T(8,128)(2,1)}, bf16[512,1536]{1,0:T(8,128)(2,1)}, u32[]{:S(2)}, u32[]{:S(2)}) collective-permute-start(bf16[512,1536]{1,0:T(8,128)(2,1)} %get-tuple-element.1677), channel_id=1, source_target_pairs={{0,1},{1,2},{2,3},{3,4},{4,5},{5,6},{6,7}} | collective-permute-start | bytes 4718600 | tf_op jit(solution)/shard_map/while/body/eval_jaxpr/ppermute | solution.py:689
  1678.9 64.4 %collective-permute-start.1 = (bf16[512,1536]{1,0:T(8,128)(2,1)}, bf16[512,1536]{1,0:T(8,128)(2,1)}, u32[]{:S(2)}, u32[]{:S(2)}) collective-permute-start(bf16[512,1536]{1,0:T(8,128)(2,1)} %get-tuple-element.1679), channel_id=1, source_target_pairs={{1,0},{2,1},{3,2},{4,3},{5,4},{6,5},{7,6}} | collective-permute-start | bytes 4718600 | tf_op jit(solution)/shard_map/while/body/eval_jaxpr/ppermute | solution.py:690
  1748.3 69.8 %collective-permute-start = (bf16[512,1536]{1,0:T(8,128)(2,1)}, bf16[512,1536]{1,0:T(8,128)(2,1)}, u32[]{:S(2)}, u32[]{:S(2)}) collective-permute-start(bf16[512,1536]{1,0:T(8,128)(2,1)} %get-tuple-element.1677), channel_id=1, source_target_pairs={{0,1},{1,2},{2,3},{3,4},{4,5},{5,6},{6,7}} | collective-permute-start | bytes 4718600 | tf_op jit(solution)/shard_map/while/body/eval_jaxpr/ppermute | solution.py:689
  1753.6 64.4 %collective-permute-start.1 = (bf16[512,1536]{1,0:T(8,128)(2,1)}, bf16[512,1536]{1,0:T(8,128)(2,1)}, u32[]{:S(2)}, u32[]{:S(2)}) collective-permute-start(bf16[512,1536]{1,0:T(8,128)(2,1)} %get-tuple-element.1679), channel_id=1, source_target_pairs={{1,0},{2,1},{3,2},{4,3},{5,4},{6,5},{7,6}} | collective-permute-start | bytes 4718600 | tf_op jit(solution)/shard_map/while/body/eval_jaxpr/ppermute | solution.py:690
  1818.9 56.5 %collective-permute-start.2 = (bf16[512,1536]{1,0:T(8,128)(2,1)}, bf16[512,1536]{1,0:T(8,128)(2,1)}, u32[]{:S(2)}, u32[]{:S(2)}) collective-permute-start(bf16[512,1536]{1,0:T(8,128)(2,1)} %get-tuple-element.1632), channel_id=1, source_target_pairs={{1,0},{2,1},{3,2},{4,3},{5,4},{6,5},{7,6}} | collective-permute-start | bytes 4718600 | tf_op jit(solution)/shard_map/while/body/eval_jaxpr/ppermute | solution.py:687
  1823.0 115.5 %collective-permute-start = (bf16[512,1536]{1,0:T(8,128)(2,1)}, bf16[512,1536]{1,0:T(8,128)(2,1)}, u32[]{:S(2)}, u32[]{:S(2)}) collective-permute-start(bf16[512,1536]{1,0:T(8,128)(2,1)} %get-tuple-element.1677), channel_id=1, source_target_pairs={{0,1},{1,2},{2,3},{3,4},{4,5},{5,6},{6,7}} | collective-permute-start | bytes 4718600 | tf_op jit(solution)/shard_map/while/body/eval_jaxpr/ppermute | solution.py:689
  1874.0 64.4 %collective-permute-start.1 = (bf16[512,1536]{1,0:T(8,128)(2,1)}, bf16[512,1536]{1,0:T(8,128)(2,1)}, u32[]{:S(2)}, u32[]{:S(2)}) collective-permute-start(bf16[512,1536]{1,0:T(8,128)(2,1)} %get-tuple-element.1679), channel_id=1, source_target_pairs={{1,0},{2,1},{3,2},{4,3},{5,4},{6,5},{7,6}} | collective-permute-start | bytes 4718600 | tf_op jit(solution)/shard_map/while/body/eval_jaxpr/ppermute | solution.py:690
  1943.4 89.5 %collective-permute-start = (bf16[512,1536]{1,0:T(8,128)(2,1)}, bf16[512,1536]{1,0:T(8,128)(2,1)}, u32[]{:S(2)}, u32[]{:S(2)}) collective-permute-start(bf16[512,1536]{1,0:T(8,128)(2,1)} %get-tuple-element.1677), channel_id=1, source_target_pairs={{0,1},{1,2},{2,3},{3,4},{4,5},{5,6},{6,7}} | collective-permute-start | bytes 4718600 | tf_op jit(solution)/shard_map/while/body/eval_jaxpr/ppermute | solution.py:689
  1968.5 64.4 %collective-permute-start.1 = (bf16[512,1536]{1,0:T(8,128)(2,1)}, bf16[512,1536]{1,0:T(8,128)(2,1)}, u32[]{:S(2)}, u32[]{:S(2)}) collective-permute-start(bf16[512,1536]{1,0:T(8,128)(2,1)} %get-tuple-element.1679), channel_id=1, source_target_pairs={{1,0},{2,1},{3,2},{4,3},{5,4},{6,5},{7,6}} | collective-permute-start | bytes 4718600 | tf_op jit(solution)/shard_map/while/body/eval_jaxpr/ppermute | solution.py:690
  2033.8 48.0 %collective-permute-start.2 = (bf16[512,1536]{1,0:T(8,128)(2,1)}, bf16[512,1536]{1,0:T(8,128)(2,1)}, u32[]{:S(2)}, u32[]{:S(2)}) collective-permute-start(bf16[512,1536]{1,0:T(8,128)(2,1)} %get-tuple-element.1632), channel_id=1, source_target_pairs={{1,0},{2,1},{3,2},{4,3},{5,4},{6,5},{7,6}} | collective-permute-start | bytes 4718600 | tf_op jit(solution)/shard_map/while/body/eval_jaxpr/ppermute | solution.py:687
  2037.8 107.0 %collective-permute-start = (bf16[512,1536]{1,0:T(8,128)(2,1)}, bf16[512,1536]{1,0:T(8,128)(2,1)}, u32[]{:S(2)}, u32[]{:S(2)}) collective-permute-start(bf16[512,1536]{1,0:T(8,128)(2,1)} %get-tuple-element.1677), channel_id=1, source_target_pairs={{0,1},{1,2},{2,3},{3,4},{4,5},{5,6},{6,7}} | collective-permute-start | bytes 4718600 | tf_op jit(solution)/shard_map/while/body/eval_jaxpr/ppermute | solution.py:689
  2080.4 64.4 %collective-permute-start.1 = (bf16[512,1536]{1,0:T(8,128)(2,1)}, bf16[512,1536]{1,0:T(8,128)(2,1)}, u32[]{:S(2)}, u32[]{:S(2)}) collective-permute-start(bf16[512,1536]{1,0:T(8,128)(2,1)} %get-tuple-element.1679), channel_id=1, source_target_pairs={{1,0},{2,1},{3,2},{4,3},{5,4},{6,5},{7,6}} | collective-permute-start | bytes 4718600 | tf_op jit(solution)/shard_map/while/body/eval_jaxpr/ppermute | solution.py:690
  2149.8 80.1 %collective-permute-start = (bf16[512,1536]{1,0:T(8,128)(2,1)}, bf16[512,1536]{1,0:T(8,128)(2,1)}, u32[]{:S(2)}, u32[]{:S(2)}) collective-permute-start(bf16[512,1536]{1,0:T(8,128)(2,1)} %get-tuple-element.1677), channel_id=1, source_target_pairs={{0,1},{1,2},{2,3},{3,4},{4,5},{5,6},{6,7}} | collective-permute-start | bytes 4718600 | tf_op jit(solution)/shard_map/while/body/eval_jaxpr/ppermute | solution.py:689
  2165.5 64.4 %collective-permute-start.1 = (bf16[512,1536]{1,0:T(8,128)(2,1)}, bf16[512,1536]{1,0:T(8,128)(2,1)}, u32[]{:S(2)}, u32[]{:S(2)}) collective-permute-start(bf16[512,1536]{1,0:T(8,128)(2,1)} %get-tuple-element.1679), channel_id=1, source_target_pairs={{1,0},{2,1},{3,2},{4,3},{5,4},{6,5},{7,6}} | collective-permute-start | bytes 4718600 | tf_op jit(solution)/shard_map/while/body/eval_jaxpr/ppermute | solution.py:690
  2230.8 46.1 %collective-permute-start.2 = (bf16[512,1536]{1,0:T(8,128)(2,1)}, bf16[512,1536]{1,0:T(8,128)(2,1)}, u32[]{:S(2)}, u32[]{:S(2)}) collective-permute-start(bf16[512,1536]{1,0:T(8,128)(2,1)} %get-tuple-element.1632), channel_id=1, source_target_pairs={{1,0},{2,1},{3,2},{4,3},{5,4},{6,5},{7,6}} | collective-permute-start | bytes 4718600 | tf_op jit(solution)/shard_map/while/body/eval_jaxpr/ppermute | solution.py:687
  2234.9 105.1 %collective-permute-start = (bf16[512,1536]{1,0:T(8,128)(2,1)}, bf16[512,1536]{1,0:T(8,128)(2,1)}, u32[]{:S(2)}, u32[]{:S(2)}) collective-permute-start(bf16[512,1536]{1,0:T(8,128)(2,1)} %get-tuple-element.1677), channel_id=1, source_target_pairs={{0,1},{1,2},{2,3},{3,4},{4,5},{5,6},{6,7}} | collective-permute-start | bytes 4718600 | tf_op jit(solution)/shard_map/while/body/eval_jaxpr/ppermute | solution.py:689
  2275.6 64.4 %collective-permute-start.1 = (bf16[512,1536]{1,0:T(8,128)(2,1)}, bf16[512,1536]{1,0:T(8,128)(2,1)}, u32[]{:S(2)}, u32[]{:S(2)}) collective-permute-start(bf16[512,1536]{1,0:T(8,128)(2,1)} %get-tuple-element.1679), channel_id=1, source_target_pairs={{1,0},{2,1},{3,2},{4,3},{5,4},{6,5},{7,6}} | collective-permute-start | bytes 4718600 | tf_op jit(solution)/shard_map/while/body/eval_jaxpr/ppermute | solution.py:690
  2344.9 89.0 %collective-permute-start = (bf16[512,1536]{1,0:T(8,128)(2,1)}, bf16[512,1536]{1,0:T(8,128)(2,1)}, u32[]{:S(2)}, u32[]{:S(2)}) collective-permute-start(bf16[512,1536]{1,0:T(8,128)(2,1)} %get-tuple-element.1677), channel_id=1, source_target_pairs={{0,1},{1,2},{2,3},{3,4},{4,5},{5,6},{6,7}} | collective-permute-start | bytes 4718600 | tf_op jit(solution)/shard_map/while/body/eval_jaxpr/ppermute | solution.py:689
  2369.5 64.4 %collective-permute-start.1 = (bf16[512,1536]{1,0:T(8,128)(2,1)}, bf16[512,1536]{1,0:T(8,128)(2,1)}, u32[]{:S(2)}, u32[]{:S(2)}) collective-permute-start(bf16[512,1536]{1,0:T(8,128)(2,1)} %get-tuple-element.1679), channel_id=1, source_target_pairs={{1,0},{2,1},{3,2},{4,3},{5,4},{6,5},{7,6}} | collective-permute-start | bytes 4718600 | tf_op jit(solution)/shard_map/while/body/eval_jaxpr/ppermute | solution.py:690
  2434.8 48.0 %collective-permute-start.2 = (bf16[512,1536]{1,0:T(8,128)(2,1)}, bf16[512,1536]{1,0:T(8,128)(2,1)}, u32[]{:S(2)}, u32[]{:S(2)}) collective-permute-start(bf16[512,1536]{1,0:T(8,128)(2,1)} %get-tuple-element.1632), channel_id=1, source_target_pairs={{1,0},{2,1},{3,2},{4,3},{5,4},{6,5},{7,6}} | collective-permute-start | bytes 4718600 | tf_op jit(solution)/shard_map/while/body/eval_jaxpr/ppermute | solution.py:687
  2438.9 107.0 %collective-permute-start = (bf16[512,1536]{1,0:T(8,128)(2,1)}, bf16[512,1536]{1,0:T(8,128)(2,1)}, u32[]{:S(2)}, u32[]{:S(2)}) collective-permute-start(bf16[512,1536]{1,0:T(8,128)(2,1)} %get-tuple-element.1677), channel_id=1, source_target_pairs={{0,1},{1,2},{2,3},{3,4},{4,5},{5,6},{6,7}} | collective-permute-start | bytes 4718600 | tf_op jit(solution)/shard_map/while/body/eval_jaxpr/ppermute | solution.py:689
  2481.5 64.4 %collective-permute-start.1 = (bf16[512,1536]{1,0:T(8,128)(2,1)}, bf16[512,1536]{1,0:T(8,128)(2,1)}, u32[]{:S(2)}, u32[]{:S(2)}) collective-permute-start(bf16[512,1536]{1,0:T(8,128)(2,1)} %get-tuple-element.1679), channel_id=1, source_target_pairs={{1,0},{2,1},{3,2},{4,3},{5,4},{6,5},{7,6}} | collective-permute-start | bytes 4718600 | tf_op jit(solution)/shard_map/while/body/eval_jaxpr/ppermute | solution.py:690
  2550.8 81.0 %collective-permute-start = (bf16[512,1536]{1,0:T(8,128)(2,1)}, bf16[512,1536]{1,0:T(8,128)(2,1)}, u32[]{:S(2)}, u32[]{:S(2)}) collective-permute-start(bf16[512,1536]{1,0:T(8,128)(2,1)} %get-tuple-element.1677), channel_id=1, source_target_pairs={{0,1},{1,2},{2,3},{3,4},{4,5},{5,6},{6,7}} | collective-permute-start | bytes 4718600 | tf_op jit(solution)/shard_map/while/body/eval_jaxpr/ppermute | solution.py:689
  2567.5 64.4 %collective-permute-start.1 = (bf16[512,1536]{1,0:T(8,128)(2,1)}, bf16[512,1536]{1,0:T(8,128)(2,1)}, u32[]{:S(2)}, u32[]{:S(2)}) collective-permute-start(bf16[512,1536]{1,0:T(8,128)(2,1)} %get-tuple-element.1679), channel_id=1, source_target_pairs={{1,0},{2,1},{3,2},{4,3},{5,4},{6,5},{7,6}} | collective-permute-start | bytes 4718600 | tf_op jit(solution)/shard_map/while/body/eval_jaxpr/ppermute | solution.py:690
  2632.8 45.1 %collective-permute-start.2 = (bf16[512,1536]{1,0:T(8,128)(2,1)}, bf16[512,1536]{1,0:T(8,128)(2,1)}, u32[]{:S(2)}, u32[]{:S(2)}) collective-permute-start(bf16[512,1536]{1,0:T(8,128)(2,1)} %get-tuple-element.1632), channel_id=1, source_target_pairs={{1,0},{2,1},{3,2},{4,3},{5,4},{6,5},{7,6}} | collective-permute-start | bytes 4718600 | tf_op jit(solution)/shard_map/while/body/eval_jaxpr/ppermute | solution.py:687
  2636.8 104.1 %collective-permute-start = (bf16[512,1536]{1,0:T(8,128)(2,1)}, bf16[512,1536]{1,0:T(8,128)(2,1)}, u32[]{:S(2)}, u32[]{:S(2)}) collective-permute-start(bf16[512,1536]{1,0:T(8,128)(2,1)} %get-tuple-element.1677), channel_id=1, source_target_pairs={{0,1},{1,2},{2,3},{3,4},{4,5},{5,6},{6,7}} | collective-permute-start | bytes 4718600 | tf_op jit(solution)/shard_map/while/body/eval_jaxpr/ppermute | solution.py:689
  2676.5 64.4 %collective-permute-start.1 = (bf16[512,1536]{1,0:T(8,128)(2,1)}, bf16[512,1536]{1,0:T(8,128)(2,1)}, u32[]{:S(2)}, u32[]{:S(2)}) collective-permute-start(bf16[512,1536]{1,0:T(8,128)(2,1)} %get-tuple-element.1679), channel_id=1, source_target_pairs={{1,0},{2,1},{3,2},{4,3},{5,4},{6,5},{7,6}} | collective-permute-start | bytes 4718600 | tf_op jit(solution)/shard_map/while/body/eval_jaxpr/ppermute | solution.py:690
  2745.9 89.4 %collective-permute-start = (bf16[512,1536]{1,0:T(8,128)(2,1)}, bf16[512,1536]{1,0:T(8,128)(2,1)}, u32[]{:S(2)}, u32[]{:S(2)}) collective-permute-start(bf16[512,1536]{1,0:T(8,128)(2,1)} %get-tuple-element.1677), channel_id=1, source_target_pairs={{0,1},{1,2},{2,3},{3,4},{4,5},{5,6},{6,7}} | collective-permute-start | bytes 4718600 | tf_op jit(solution)/shard_map/while/body/eval_jaxpr/ppermute | solution.py:689
  2770.8 64.4 %collective-permute-start.1 = (bf16[512,1536]{1,0:T(8,128)(2,1)}, bf16[512,1536]{1,0:T(8,128)(2,1)}, u32[]{:S(2)}, u32[]{:S(2)}) collective-permute-start(bf16[512,1536]{1,0:T(8,128)(2,1)} %get-tuple-element.1679), channel_id=1, source_target_pairs={{1,0},{2,1},{3,2},{4,3},{5,4},{6,5},{7,6}} | collective-permute-start | bytes 4718600 | tf_op jit(solution)/shard_map/while/body/eval_jaxpr/ppermute | solution.py:690
  2836.2 48.0 %collective-permute-start.2 = (bf16[512,1536]{1,0:T(8,128)(2,1)}, bf16[512,1536]{1,0:T(8,128)(2,1)}, u32[]{:S(2)}, u32[]{:S(2)}) collective-permute-start(bf16[512,1536]{1,0:T(8,128)(2,1)} %get-tuple-element.1632), channel_id=1, source_target_pairs={{1,0},{2,1},{3,2},{4,3},{5,4},{6,5},{7,6}} | collective-permute-start | bytes 4718600 | tf_op jit(solution)/shard_map/while/body/eval_jaxpr/ppermute | solution.py:687
  2840.2 107.0 %collective-permute-start = (bf16[512,1536]{1,0:T(8,128)(2,1)}, bf16[512,1536]{1,0:T(8,128)(2,1)}, u32[]{:S(2)}, u32[]{:S(2)}) collective-permute-start(bf16[512,1536]{1,0:T(8,128)(2,1)} %get-tuple-element.1677), channel_id=1, source_target_pairs={{0,1},{1,2},{2,3},{3,4},{4,5},{5,6},{6,7}} | collective-permute-start | bytes 4718600 | tf_op jit(solution)/shard_map/while/body/eval_jaxpr/ppermute | solution.py:689
  2882.8 64.4 %collective-permute-start.1 = (bf16[512,1536]{1,0:T(8,128)(2,1)}, bf16[512,1536]{1,0:T(8,128)(2,1)}, u32[]{:S(2)}, u32[]{:S(2)}) collective-permute-start(bf16[512,1536]{1,0:T(8,128)(2,1)} %get-tuple-element.1679), channel_id=1, source_target_pairs={{1,0},{2,1},{3,2},{4,3},{5,4},{6,5},{7,6}} | collective-permute-start | bytes 4718600 | tf_op jit(solution)/shard_map/while/body/eval_jaxpr/ppermute | solution.py:690
  2948.1 47.6 %collective-permute-start.2 = (bf16[512,1536]{1,0:T(8,128)(2,1)}, bf16[512,1536]{1,0:T(8,128)(2,1)}, u32[]{:S(2)}, u32[]{:S(2)}) collective-permute-start(bf16[512,1536]{1,0:T(8,128)(2,1)} %get-tuple-element.1632), channel_id=1, source_target_pairs={{1,0},{2,1},{3,2},{4,3},{5,4},{6,5},{7,6}} | collective-permute-start | bytes 4718600 | tf_op jit(solution)/shard_map/while/body/eval_jaxpr/ppermute | solution.py:687
  2952.2 106.6 %collective-permute-start = (bf16[512,1536]{1,0:T(8,128)(2,1)}, bf16[512,1536]{1,0:T(8,128)(2,1)}, u32[]{:S(2)}, u32[]{:S(2)}) collective-permute-start(bf16[512,1536]{1,0:T(8,128)(2,1)} %get-tuple-element.1677), channel_id=1, source_target_pairs={{0,1},{1,2},{2,3},{3,4},{4,5},{5,6},{6,7}} | collective-permute-start | bytes 4718600 | tf_op jit(solution)/shard_map/while/body/eval_jaxpr/ppermute | solution.py:689
  2994.4 64.4 %collective-permute-start.1 = (bf16[512,1536]{1,0:T(8,128)(2,1)}, bf16[512,1536]{1,0:T(8,128)(2,1)}, u32[]{:S(2)}, u32[]{:S(2)}) collective-permute-start(bf16[512,1536]{1,0:T(8,128)(2,1)} %get-tuple-element.1679), channel_id=1, source_target_pairs={{1,0},{2,1},{3,2},{4,3},{5,4},{6,5},{7,6}} | collective-permute-start | bytes 4718600 | tf_op jit(solution)/shard_map/while/body/eval_jaxpr/ppermute | solution.py:690
  (90 other events, 2811.6 us)
Sparse Core Ops, SparseCore 0:
  3080.7 293.8 all-reduce.1

commit v3 on v2

--- a/solution.py
+++ b/solution.py
@@ -71,10 +71,10 @@
     return jnp.sum(t.reshape(t.shape[0] // 8, 8, t.shape[1]), axis=0)
 
 
-def fwd_kernel(idx, x_in, x_all, conv_in, g1, s1, bqkv, bproj, g2, s2, bup, bdown, wqkv, wproj, wup, wdown, *rest):
+def fwd_kernel(idx, x_in, x_all, g1, s1, bqkv, bproj, g2, s2, bup, bdown, wqkv, wproj, wup, wdown, *rest):
     n_alias = 11
-    (y_o, conv_o, xs_o, h1_o, qkv_o, mix_o, x1_o, h2_o, pre_o, lse_o, act_o,
-     x_s, h1_s, qkv_s, mix_s, x1_s, h2_s, act_s, stage_s, pre_s, acc_s, y_s, lse_s, vt_s, ot_s, conv_s, wq_s, wp_s, wu_s, wd_s,
+    (y_o, ys_o, xs_o, h1_o, qkv_o, mix_o, x1_o, h2_o, pre_o, lse_o, act_o,
+     x_s, h1_s, qkv_s, mix_s, x1_s, h2_s, act_s, stage_s, pre_s, acc_s, y_s, lse_s, vt_s, ot_s, zero_s, wq_s, wp_s, wu_s, wd_s,
      sem_in, sem_q, sem_u, sem_d, sem_pre, sem_act, sem_out) = rest[n_alias:]
     c, first, last = idx[0], idx[1], idx[2]
     n_seq, d = x_s.shape
@@ -88,7 +88,7 @@
     wd = lambda j: copy(wdown.at[pl.ds(pl.multiple_of(j * TF, TF), TF), :], wd_s.at[four(j)], sem_d.at[four(j)])
     pre_out = lambda j: copy(pre_s.at[four(j)], pre_o.at[c, :, lanes(j * TF, TF)], sem_pre.at[four(j)])
     x_copy = copy(x_in, x_s, sem_in.at[0])
-    wp_copy = copy(wproj, wp_s, sem_in.at[1])
+    wp_copy = copy(wproj, wp_s, sem_in.at[2])
 
     @pl.when(first == 1)
     def _():
@@ -108,12 +108,12 @@
         h1_s[rows] = (xhat * g1[...].astype(F32) + s1[...].astype(F32)).astype(BF)
 
     row_blocks(n_seq, ln_first)
-    conv_load = copy(conv_in, conv_s, sem_in.at[2])
-    conv_put = copy(conv_s, conv_o, sem_in.at[3])
+    zero_put = copy(zero_s, ys_o.at[c], sem_in.at[1])
 
     @pl.when(last == 0)
     def _():
-        conv_load.start()
+        zero_s[...] = jnp.zeros_like(zero_s)
+        zero_put.start()
 
     outs = [copy(x_s, xs_o.at[c], sem_out.at[0]), copy(h1_s, h1_o.at[c], sem_out.at[1])]
     for o in outs:
@@ -193,12 +193,6 @@
         return carry
 
     lax.fori_loop(0, 4, attend, 0)
-
-    @pl.when(last == 0)
-    def _():
-        conv_load.wait()
-        conv_put.start()
-
     outs.append(copy(mix_s, mix_o.at[c], sem_out.at[3]))
     outs[-1].start()
     outs.append(copy(lse_s, lse_o.at[c], sem_out.at[4]))
@@ -291,7 +285,7 @@
 
     @pl.when(last == 1)
     def _():
-        copy(y_s, conv_o, sem_in.at[3]).start()
+        copy(y_s, ys_o.at[c], sem_in.at[1]).start()
 
     for o in outs:
         o.wait()
@@ -299,23 +293,23 @@
         put_done(j - 3 + i)
     y_copy.wait()
 
-    conv_put.wait()
-
-
-def fwd_call(idx, x_in, x_all, conv_in, weights, y, conv, saved):
+    zero_put.wait()
+
+
+def fwd_call(idx, x_in, x_all, weights, y, y_all, saved):
     g1, s1, wqkv, bqkv, wproj, bproj, g2, s2, wup, bup, wdown, bdown = weights
     n_seq, d = x_in.shape
     e, f = wqkv.shape[1], wup.shape[1]
     r2 = lambda t: t.reshape(1, -1)
     vm = pl.BlockSpec(memory_space=pltpu.VMEM)
-    args = [idx, x_in, x_all, conv_in, r2(g1), r2(s1), r2(bqkv), r2(bproj), r2(g2), r2(s2), r2(bup), r2(bdown),
+    args = [idx, x_in, x_all, r2(g1), r2(s1), r2(bqkv), r2(bproj), r2(g2), r2(s2), r2(bup), r2(bdown),
             wqkv, wproj.reshape(d, d), wup, wdown]
-    alias = [y, conv] + list(saved)
+    alias = [y, y_all] + list(saved)
     dma = pltpu.SemaphoreType.DMA
     vmem = lambda *s: pltpu.VMEM(s[:-1], s[-1])
     outs = pl.pallas_call(
         fwd_kernel,
-        in_specs=[pl.BlockSpec(memory_space=pltpu.SMEM), ANY, ANY, ANY] + [vm] * 8 + [ANY] * (4 + len(alias)),
+        in_specs=[pl.BlockSpec(memory_space=pltpu.SMEM), ANY, ANY] + [vm] * 8 + [ANY] * (4 + len(alias)),
         out_specs=[ANY] * len(alias),
         out_shape=[jax.ShapeDtypeStruct(t.shape, t.dtype) for t in alias],
         input_output_aliases={len(args) + i: i for i in range(len(alias))},
@@ -324,7 +318,7 @@
             vmem(2, n_seq, TF, BF), vmem(4, n_seq, TF, BF), vmem(4, n_seq, TF, F32), vmem(n_seq, d, F32), vmem(n_seq, d, BF),
             vmem(4, 8, n_seq, F32), vmem(384, n_seq, BF), vmem(384, n_seq, BF), vmem(n_seq, d, BF),
             vmem(6, d, TQ, BF), vmem(d, d, BF), vmem(4, d, TF, BF), vmem(4, TF, d, BF),
-            dma((4,)), dma((6,)), dma((4,)), dma((4,)), dma((4,)), dma((4,)), dma((7,)),
+            dma((3,)), dma((6,)), dma((4,)), dma((4,)), dma((4,)), dma((4,)), dma((7,)),
         ],
         compiler_params=pltpu.CompilerParams(vmem_limit_bytes=VMEM_LIMIT),
         cost_estimate=pl.CostEstimate(flops=int(31e9), bytes_accessed=int(9e7), transcendentals=0),
@@ -333,10 +327,10 @@
     return outs[0], outs[1], tuple(outs[2:])
 
 
-def bwd_kernel(idx, dy_in, ct_all, conv, xs, qkv, mix, x1, pre, lse, g1, g2, wqkv, wproj, wup, wdown, *rest):
-    n_alias = 10
-    (dx_o, dxs_o, ys_o, dpre_o, dmid_o, dqkv_o, dys_o, sup_o, sqkv_o, sd_o,
-     dy_s, acc_s, dp_s, p_s, stage_s, x1_s, dm_s, do_s, qkv_s, mix_s, x_s, conv_s, lse_s, rd_s, kt_s, dqt_s, sup_s, sqkv_s, sd_s, fold_s, pre_s,
+def bwd_kernel(idx, dy_in, ct_all, xs, qkv, mix, x1, pre, lse, g1, g2, wqkv, wproj, wup, wdown, *rest):
+    n_alias = 9
+    (dx_o, dxs_o, dpre_o, dmid_o, dqkv_o, dys_o, sup_o, sqkv_o, sd_o,
+     dy_s, acc_s, dp_s, p_s, stage_s, x1_s, dm_s, do_s, qkv_s, mix_s, x_s, zero_s, lse_s, rd_s, kt_s, dqt_s, sup_s, sqkv_s, sd_s, fold_s, pre_s,
      wq_s, wp_s, wu_s, wd_s,
      sem_in, sem_q, sem_u, sem_d, sem_pre, sem_dp, sem_out) = rest[n_alias:]
     c, first, last = idx[0], idx[1], idx[2]
@@ -353,8 +347,8 @@
     dp_out = lambda j: copy(stage_s.at[four(j)], dpre_o.at[c, :, lanes(j * TF, TF)], sem_dp.at[four(j)])
     dy_copy = copy(dy_in, dy_s, sem_in.at[0])
     ins = [copy(x1.at[c], x1_s, sem_in.at[1]), copy(wproj, wp_s, sem_in.at[2]), copy(qkv.at[c], qkv_s, sem_in.at[3]),
-           copy(mix.at[c], mix_s, sem_in.at[4]), copy(lse.at[c], lse_s, sem_in.at[5]), copy(xs.at[c], x_s, sem_in.at[6]),
-           copy(conv, conv_s, sem_in.at[7])]
+           copy(mix.at[c], mix_s, sem_in.at[4]), copy(lse.at[c], lse_s, sem_in.at[5]), copy(xs.at[c], x_s, sem_in.at[6])]
+    zero_put = copy(zero_s, dxs_o.at[c], sem_in.at[7])
     colsum = lambda t: jnp.sum(t, axis=0, keepdims=True)
 
     @pl.when(last == 1)
@@ -445,9 +439,12 @@
     for t in ins[2:]:
         t.start()
     up_back(j, 1)
-    ins[6].wait()
-    outs.append(copy(conv_s, ys_o.at[c], sem_out.at[1]))
-    outs[-1].start()
+
+    @pl.when(first == 0)
+    def _():
+        zero_s[...] = jnp.zeros_like(zero_s)
+        zero_put.start()
+
     ins[0].wait()
 
     def ln_bwd(src, base, base2, gain, dst, rows_at):
@@ -562,7 +559,7 @@
 
     @pl.when(first == 1)
     def _():
-        copy(x1_s, dxs_o.at[c], sem_in.at[1]).start()
+        copy(x1_s, dxs_o.at[c], sem_in.at[7]).start()
 
     sd_s[6:8, :] = jnp.zeros((2, d), F32)
     for i, (src, dst) in enumerate(((sup_s, sup_o), (sqkv_s, sqkv_o), (sd_s, sd_o))):
@@ -572,25 +569,23 @@
         o.wait()
     dx_copy.wait()
 
-    @pl.when(first == 1)
-    def _():
-        copy(x1_s, dxs_o.at[c], sem_in.at[1]).wait()
-
-
-def bwd_call(idx, dy_in, ct_all, conv, weights, saved, dx, dx_all, y_all, store):
+    zero_put.wait()
+
+
+def bwd_call(idx, dy_in, ct_all, weights, saved, dx, dx_all, store):
     g1, s1, wqkv, bqkv, wproj, bproj, g2, s2, wup, bup, wdown, bdown = weights
     xs, h1, qkv, mix, x1, h2, pre, lse, act = saved
     n_seq, d = dy_in.shape
     e, f = wqkv.shape[1], wup.shape[1]
     r2 = lambda t: t.reshape(1, -1)
     vm = pl.BlockSpec(memory_space=pltpu.VMEM)
-    args = [idx, dy_in, ct_all, conv, xs, qkv, mix, x1, pre, lse, r2(g1), r2(g2), wqkv, wproj.reshape(d, d), wup, wdown]
-    alias = [dx, dx_all, y_all] + list(store)
+    args = [idx, dy_in, ct_all, xs, qkv, mix, x1, pre, lse, r2(g1), r2(g2), wqkv, wproj.reshape(d, d), wup, wdown]
+    alias = [dx, dx_all] + list(store)
     dma = pltpu.SemaphoreType.DMA
     vmem = lambda *s: pltpu.VMEM(s[:-1], s[-1])
     outs = pl.pallas_call(
         bwd_kernel,
-        in_specs=[pl.BlockSpec(memory_space=pltpu.SMEM)] + [ANY] * 9 + [vm] * 2 + [ANY] * (4 + len(alias)),
+        in_specs=[pl.BlockSpec(memory_space=pltpu.SMEM)] + [ANY] * 8 + [vm] * 2 + [ANY] * (4 + len(alias)),
         out_specs=[ANY] * len(alias),
         out_shape=[jax.ShapeDtypeStruct(t.shape, t.dtype) for t in alias],
         input_output_aliases={len(args) + i: i for i in range(len(alias))},
@@ -605,7 +600,148 @@
         cost_estimate=pl.CostEstimate(flops=int(36e9), bytes_accessed=int(1.1e8), transcendentals=0),
         name="layer_bwd",
     )(*args, *alias)
-    return outs[0], outs[1], outs[2], tuple(outs[3:])
+    return outs[0], outs[1], tuple(outs[2:])
+
+
+N_TILE, N_ACC, WT = 12, 3, 1536
+
+
+def wgrad_kernel(tab, h1, mix, h2, act, dqkv, dmid, dpre, dys, *rest):
+    gq, gp, gu, gd, x_s, y_s, xt_s, acc_s, sem_x, sem_y, sem_load, sem_put = rest[4:]
+    n = tab[0, 0]
+    copy = pltpu.make_async_copy
+    two = lambda s: lax.rem(s, 2)
+    kinds = ((0, 3, h1, dqkv, gq, False, True, False), (3, 1, mix, dmid, gp, False, False, False),
+             (4, 4, h2, dpre, gu, False, True, False), (8, 4, act, dys, gd, True, False, True))
+
+    def by_kind(tile, act_on):
+        for base, count, x, y, g, xcol, ycol, grow in kinds:
+            @pl.when((tile >= base) & (tile < base + count))
+            def _(base=base, x=x, y=y, g=g, xcol=xcol, ycol=ycol, grow=grow):
+                at = pl.multiple_of((tile - base) * WT, WT)
+                cols = lambda on: pl.ds(at, WT) if on else pl.ds(0, WT)
+                act_on(x, y, g.at[cols(grow), cols(ycol)], cols(xcol), cols(ycol))
+
+    def load_xy(s):
+        rows = pl.ds(2 * tab[2, s], 2)
+
+        def go(x, y, g, xc, yc):
+            copy(x.at[rows, :, xc], x_s.at[two(s)], sem_x.at[two(s)]).start()
+            copy(y.at[rows, :, yc], y_s.at[two(s)], sem_y.at[two(s)]).start()
+
+        by_kind(tab[1, s], go)
+
+    slot_of = lambda s: lax.rem(tab[5, s], N_ACC)
+    put_done = lambda slot: copy(acc_s.at[slot], gp, sem_put.at[slot]).wait()
+
+    def open_tile(s):
+        slot = slot_of(s)
+
+        @pl.when(tab[5, s] >= N_ACC)
+        def _():
+            put_done(slot)
+
+        @pl.when(tab[3, s] == 1)
+        def _():
+            by_kind(tab[1, s], lambda x, y, g, xc, yc: copy(g, acc_s.at[slot], sem_load.at[slot]).start())
+
+        @pl.when(tab[3, s] == 0)
+        def _():
+            acc_s[slot] = jnp.zeros((WT, WT), F32)
+
+    @pl.when(n > 0)
+    def _():
+        load_xy(0)
+        open_tile(0)
+
+    def step(s, carry):
+        slot = slot_of(s)
+
+        @pl.when(s + 1 < n)
+        def _():
+            load_xy(s + 1)
+
+            @pl.when(tab[3, s + 1] < 2)
+            def _():
+                open_tile(s + 1)
+
+        @pl.when(tab[3, s] == 1)
+        def _():
+            copy(gp, acc_s.at[slot], sem_load.at[slot]).wait()
+
+        copy(h1.at[pl.ds(0, 2)], x_s.at[two(s)], sem_x.at[two(s)]).wait()
+        copy(h1.at[pl.ds(0, 2)], y_s.at[two(s)], sem_y.at[two(s)]).wait()
+        x, y = x_s.at[two(s)], y_s.at[two(s)]
+        depth = x.shape[0] * x.shape[1]
+        for m in range(0, WT, NC):
+            xt_s[m // NC] = x[:, :, m:m + NC].reshape(depth, NC).T
+        for m in range(0, WT, NC):
+            for c in range(0, WT, NC):
+                acc_s[slot, m:m + NC, c:c + NC] += mm(xt_s[m // NC], y[:, :, c:c + NC].reshape(depth, NC))
+
+        @pl.when(tab[4, s] == 1)
+        def _():
+            by_kind(tab[1, s], lambda x, y, g, xc, yc: copy(acc_s.at[slot], g, sem_put.at[slot]).start())
+
+        return carry
+
+    lax.fori_loop(0, n, step, 0)
+    for i in range(N_ACC):
+        @pl.when(tab[0, 1] > i)
+        def _(i=i):
+            put_done(lax.rem(tab[0, 1] - 1 - i, N_ACC))
+
+
+def wgrad_call(tab, saved, store, grads):
+    xs, h1, qkv, mix, x1, h2, pre, lse, act = saved
+    dpre, dmid, dqkv, dys = store[:4]
+    n_seq, d = h1.shape[1:]
+    args = [tab, h1, mix, h2, act, dqkv, dmid, dpre, dys]
+    dma = pltpu.SemaphoreType.DMA
+    return tuple(pl.pallas_call(
+        wgrad_kernel,
+        in_specs=[pl.BlockSpec(memory_space=pltpu.SMEM)] + [ANY] * (8 + len(grads)),
+        out_specs=[ANY] * len(grads),
+        out_shape=[jax.ShapeDtypeStruct(g.shape, g.dtype) for g in grads],
+        input_output_aliases={len(args) + i: i for i in range(len(grads))},
+        scratch_shapes=[
+            pltpu.VMEM((2, 2, n_seq, WT), BF), pltpu.VMEM((2, 2, n_seq, WT), BF), pltpu.VMEM((WT // NC, NC, 2 * n_seq), BF),
+            pltpu.VMEM((N_ACC, WT, WT), F32), dma((2,)), dma((2,)), dma((N_ACC,)), dma((N_ACC,)),
+        ],
+        compiler_params=pltpu.CompilerParams(vmem_limit_bytes=VMEM_LIMIT),
+        cost_estimate=pl.CostEstimate(flops=int(2e10), bytes_accessed=int(1e8), transcendentals=0),
+        name="weight_grad",
+    )(*args, *grads))
+
+
+def fill_table(done, n):
+    s = jnp.arange(16, dtype=jnp.int32)
+    v = done + s
+    pair = v // N_TILE
+    head = jnp.where(s < 2, n, 0)
+    return jnp.stack([head, v % N_TILE, pair, jnp.where(pair > 0, 1, 0), jnp.ones_like(s), s]).astype(jnp.int32)
+
+
+def rest_table(done, n_pair):
+    total = N_TILE * n_pair
+    q, r = done // N_TILE, done % N_TILE
+    s = jnp.arange(total + 8, dtype=jnp.int32)
+    short, full = jnp.maximum(n_pair - q - 1, 1), jnp.maximum(n_pair - q, 1)
+    split = r * (n_pair - q - 1)
+    early = s < split
+    s2 = s - split
+    tile = jnp.where(early, s // short, r + s2 // full)
+    within = jnp.where(early, s % short, s2 % full)
+    base = jnp.where(early, q + 1, q)
+    count = jnp.where(early, short, full)
+    mode = jnp.where(within > 0, 2, jnp.where(base > 0, 1, 0))
+    start = jnp.where(n_pair - q - 1 > 0, 0, r)
+    n = total - done
+    head = jnp.where(s == 0, n, jnp.where(s == 1, jnp.where(n > 0, N_TILE - start, 0), 0))
+    return jnp.stack([head, tile, base + within, mode, jnp.where(within == count - 1, 1, 0), tile - start]).astype(jnp.int32)
+
+
+FILL_F, FILL_B = 5, 7
 
 
 def fresh(shapes):
@@ -615,27 +751,6 @@
         out_specs=[ANY] * len(shapes),
         name="fresh",
     )()
-
-
-def relay_kernel(src, _alias, dst, buf, sems):
-    load = pltpu.make_async_copy(src, buf, sems.at[0])
-    load.start()
-    load.wait()
-    put = pltpu.make_async_copy(buf, dst, sems.at[1])
-    put.start()
-    put.wait()
-
-
-def relay(src, dst):
-    return pl.pallas_call(
-        relay_kernel,
-        in_specs=[ANY, ANY],
-        out_specs=ANY,
-        out_shape=jax.ShapeDtypeStruct(dst.shape, dst.dtype),
-        input_output_aliases={1: 0},
-        scratch_shapes=[pltpu.VMEM(src.shape, src.dtype), pltpu.SemaphoreType.DMA((2,))],
-        name="relay",
-    )(src, dst)
 
 
 def solution(mesh):
@@ -661,48 +776,83 @@
         one = sds((n_seq, d), BF)
         shapes = [many(d), many(d), many(3 * d), many(d), many(d), many(d), many(f, F32), sds((n_chunk, 4, 8, n_seq), F32), many(f),
                   many(f), many(d), many(3 * d), many(d), tall(1, f), tall(1, 3 * d), tall(8, d),
-                  many(d), many(d), one, one, one, one, one]
+                  many(d), many(d), one, one, one,
+                  sds((d, 3 * d), F32), sds((d, d), F32), sds((d, f), F32), sds((f, d), F32)]
         bufs = fresh(shapes)
         saved, store = tuple(bufs[:9]), tuple(bufs[9:16])
-        dx_all, y_all, x_in, conv_in, y, dx, conv = bufs[16:]
-
-        def forward(t, x_in, conv_in, y, conv, saved):
+        dx_all, y_all, x_in, y, dx = bufs[16:21]
+        mats = tuple(bufs[21:])
+        n_pair = n_chunk // 2
+
+        def idx_of(c):
+            return jnp.stack([jnp.clip(c, 0, n_chunk - 1), stage == 0, stage == last_stage]).astype(jnp.int32)
+
+        def forward(t, x_in, y, y_all, saved):
             c = t - stage
-            ok = (c >= 0) & (c < n_chunk)
-            idx = jnp.stack([jnp.clip(c, 0, n_chunk - 1), stage == 0, stage == last_stage]).astype(jnp.int32)
-            run = lambda x_in, conv_in, y, conv, saved: fwd_call(idx, x_in, x_all, conv_in, weights, y, conv, saved)
-            skip = lambda x_in, conv_in, y, conv, saved: (y, relay(conv_in, conv), saved)
-            return lax.cond(ok, run, skip, x_in, conv_in, y, conv, saved)
-
-        def backward(t, dy_in, conv, saved, dx, dx_all, y_all, store):
+            run = lambda x_in, y, y_all, saved: fwd_call(idx_of(c), x_in, x_all, weights, y, y_all, saved)
+            skip = lambda x_in, y, y_all, saved: (y, y_all, saved)
+            return lax.cond((c >= 0) & (c < n_chunk), run, skip, x_in, y, y_all, saved)
+
+        def backward(t, dy_in, saved, dx, dx_all, store):
             c = t - (2 * last_stage - stage)
-            ok = (c >= 0) & (c < n_chunk)
-            idx = jnp.stack([jnp.clip(c, 0, n_chunk - 1), stage == 0, stage == last_stage]).astype(jnp.int32)
-            run = lambda dy_in, conv, saved, dx, dx_all, y_all, store: bwd_call(idx, dy_in, ct_all, conv, weights, saved, dx, dx_all, y_all, store)
-            skip = lambda dy_in, conv, saved, dx, dx_all, y_all, store: (dx, dx_all, y_all, store)
-            return lax.cond(ok, run, skip, dy_in, conv, saved, dx, dx_all, y_all, store)
-
-        def step(t, state):
-            x_in, conv_in, y, dx, conv, saved, store, dx_all, y_all = state
+            run = lambda dy_in, saved, dx, dx_all, store: bwd_call(idx_of(c), dy_in, ct_all, weights, saved, dx, dx_all, store)
+            skip = lambda dy_in, saved, dx, dx_all, store: (dx, dx_all, store)
+            return lax.cond((c >= 0) & (c < n_chunk), run, skip, dy_in, saved, dx, dx_all, store)
+
+        def weight_part(done, ready, limit, saved, store, mats):
+            n = jnp.clip(ready - done, 0, limit)
+            return done + n, wgrad_call(fill_table(done, n), saved, store, mats)
+
+        def fill(t, state):
+            x_in, y, y_all, saved = state
+            y, y_all, saved = forward(t, x_in, y, y_all, saved)
+            return lax.ppermute(y, 'pp', fwd_pairs), y, y_all, saved
+
+        def steady(t, state):
+            x_in, y, y_all, saved, dx, dx_all, store, done, mats = state
             dy_in = lax.ppermute(dx, 'pp', bwd_pairs)
-            y, conv, saved = forward(t, x_in, conv_in, y, conv, saved)
+            c = t - stage
+
+            def run(x_in, y, y_all, saved, store, done, mats):
+                return fwd_call(idx_of(c), x_in, x_all, weights, y, y_all, saved) + (done, mats)
+
+            def idle(x_in, y, y_all, saved, store, done, mats):
+                ready = (t + stage - 2 * last_stage) // 2 * N_TILE
+                return (y, y_all, saved) + weight_part(done, ready, FILL_F, saved, store, mats)
+
+            y, y_all, saved, done, mats = lax.cond(c < n_chunk, run, idle, x_in, y, y_all, saved, store, done, mats)
             x_in = lax.ppermute(y, 'pp', fwd_pairs)
-            conv_in = lax.ppermute(conv, 'pp', bwd_pairs)
-            dx, dx_all, y_all, store = backward(t, dy_in, conv, saved, dx, dx_all, y_all, store)
-            return x_in, conv_in, y, dx, conv, saved, store, dx_all, y_all
-
-        state = (x_in, conv_in, y, dx, conv, saved, store, dx_all, y_all)
-        x_in, conv_in, y, dx, conv, saved, store, dx_all, y_all = lax.fori_loop(0, n_chunk + 2 * last_stage, step, state)
-
-        grad_in = lax.psum(jnp.where(stage == 0, dx_all, jnp.zeros_like(dx_all)), 'pp')
-        xs, h1, qkv, mix, x1, h2, pre, lse, act = saved
-        dpre, dmid, dqkv, dys, sum_up, sum_qkv, sum_d = store
-        wgrad = lambda a, b: jnp.einsum('cka,ckb->ab', a, b, preferred_element_type=F32)
+            dx, dx_all, store = backward(t, dy_in, saved, dx, dx_all, store)
+            return x_in, y, y_all, saved, dx, dx_all, store, done, mats
+
+        def drain(t, state):
+            dx, dx_all, store, done, mats = state
+            dy_in = lax.ppermute(dx, 'pp', bwd_pairs)
+            c = t - (2 * last_stage - stage)
+
+            def run(dy_in, dx, dx_all, store, done, mats):
+                return bwd_call(idx_of(c), dy_in, ct_all, weights, saved, dx, dx_all, store) + (done, mats)
+
+            def idle(dy_in, dx, dx_all, store, done, mats):
+                return (dx, dx_all, store) + weight_part(done, n_pair * N_TILE, FILL_B, saved, store, mats)
+
+            return lax.cond(c < n_chunk, run, idle, dy_in, dx, dx_all, store, done, mats)
+
+        x_in, y, y_all, saved = lax.fori_loop(0, last_stage, fill, (x_in, y, y_all, saved))
+        done = jnp.int32(0)
+        x_in, y, y_all, saved, dx, dx_all, store, done, mats = lax.fori_loop(
+            last_stage, last_stage + n_chunk, steady, (x_in, y, y_all, saved, dx, dx_all, store, done, mats))
+        acts_out = lax.psum(y_all, 'pp')
+        dx, dx_all, store, done, mats = lax.fori_loop(
+            last_stage + n_chunk, 2 * last_stage + n_chunk, drain, (dx, dx_all, store, done, mats))
+        dx_all, acts_out = lax.optimization_barrier((dx_all, acts_out))
+        grad_in = lax.psum(dx_all, 'pp')
+        g_qkv, g_proj, g_up, g_down = wgrad_call(rest_table(done, n_pair), saved, store, mats)
+        sum_up, sum_qkv, sum_d = store[4:]
         vec = jnp.sum(sum_d, axis=0)
-        grads = (vec[0], vec[1], wgrad(h1, dqkv), jnp.sum(sum_qkv, axis=(0, 1)),
-                 wgrad(mix, dmid).reshape(stacked_w[4].shape[1:]), vec[4], vec[2], vec[3],
-                 wgrad(h2, dpre), jnp.sum(sum_up, axis=(0, 1)), wgrad(act, dys), vec[5])
+        grads = (vec[0], vec[1], g_qkv, jnp.sum(sum_qkv, axis=(0, 1)), g_proj.reshape(stacked_w[4].shape[1:]), vec[4],
+                 vec[2], vec[3], g_up, jnp.sum(sum_up, axis=(0, 1)), g_down, vec[5])
         shape4 = acts_in.shape
-        return (y_all.reshape(shape4), grad_in.reshape(shape4)) + tuple(g[None] for g in grads)
+        return (acts_out.reshape(shape4), grad_in.reshape(shape4)) + tuple(g[None] for g in grads)
 
     return jax.shard_map(stage_body, mesh=mesh, in_specs=(act_spec, act_spec) + param_specs, out_specs=(act_spec, act_spec) + grad_specs, check_vma=False)

time: 3660 us -> 3400 us (0.929)
  Pallas kernels: 1820 us -> 2400 us
  matrix products: 525 us -> 0 us
  starting transfers between devices: 1110 us -> 612 us
  waiting for transfers between devices: 102 us -> 244 us
    pallas_call x14 -> x8, Pallas kernels: 37 us -> 655 us  [wgrad_call(): pl.pallas_call(wgrad_kernel, in_specs=[pl.BlockSpec(memory_space=pltpu.SM...]
    dot_general x4 -> x0, matrix products: 525 us -> none  [stage_body(): jnp.einsum('cka,ckb->ab', a, b, preferred_element_type=F32)]
    ppermute x90 -> x46, starting transfers between devices: 1110 us -> 612 us  [the longest x16 479 us: steady(): x_in = lax.ppermute(y, 'pp', fwd_pairs)]
    ppermute x90 -> x46, waiting for transfers between devices: 102 us -> 236 us  [the longest x7 211 us: drain(): dy_in = lax.ppermute(dx, 'pp', bwd_pairs)]
    pallas_call x16, Pallas kernels: 1010 us -> 966 us  [bwd_call(): pl.pallas_call(bwd_kernel, in_specs=[pl.BlockSpec(memory_space=pltpu.SMEM...]
  transfers between devices with their start and end apart: 91 -> 48, of which waited for: 28 -> 22; matrix products, arithmetic and copies ran while one was open for 15% -> 1% of each run, Pallas kernels for 50% -> 61%
where the time goes in v3:
time: 3400 us; the launch traced here: 3380 us
  Pallas kernels  2400 us (71%)
  starting transfers between devices  612 us (18%)
  waiting for transfers between devices  244 us (7%)
  local copies, waits for them, and re-layouts  49.9 us (1%)
  loops' own time  34.4 us (1%)
    pallas_call x16, Pallas kernels, bwd_call(): pl.pallas_call(bwd_kernel, in_specs=[pl.BlockSpec(memory_space=pltpu.SMEM...  966 us
    pallas_call x16, Pallas kernels, fwd_call(): pl.pallas_call(fwd_kernel, in_specs=[pl.BlockSpec(memory_space=pltpu.SMEM...  781 us
    pallas_call x8, Pallas kernels, wgrad_call(): pl.pallas_call(wgrad_kernel, in_specs=[pl.BlockSpec(memory_space=pltpu.SM...  655 us
    ppermute x16, starting transfers between devices, steady(): x_in = lax.ppermute(y, 'pp', fwd_pairs)  479 us
    ppermute x7, waiting for transfers between devices, drain(): dy_in = lax.ppermute(dx, 'pp', bwd_pairs)  211 us
    ppermute x7, starting transfers between devices, fill(): return (lax.ppermute(y, 'pp', fwd_pairs), y, y_all, saved)  103 us
  transfers between devices with their start and end apart: 48, of which 22 were waited for; matrix products, arithmetic and copies ran while one was open for 1% of the time, Pallas kernels for 61%

profile of v3, /device:TPU:0, one launch (start us, length us, event | category | flops | bytes accessed | tf_op | source)
XLA Modules:
  0.0 3377.8 jit_solution(9060448413932549914)
XLA Ops:
  7.2 461.5 %while.139 = (s32[]{:T(128)}, bf16[512,1536]{1,0:T(8,128)(2,1)}, bf16[512,1536]{1,0:T(8,128)(2,1)}, bf16[16,512,1536]{2,1,0:T(8,128)(2,1)}, bf16[16,512,1536]{2,...) while((s32[]{:T(128)}, bf16[512,1536]{1,0:T(8,128)(2,1)}, ...), condition=%wide.region_3.4_spmd, body=%wide.region_0.3_spmd.sunk | while | flops 31000000512 | bytes 96292184 | solution.py:841
  7.3 49.4 %conditional.8 = ((bf16[512,1536]{1,0:T(8,128)(2,1)}, bf16[16,512,1536]{2,1,0:T(8,128)(2,1)}, bf16[16,512,1536]{2,1,0:T(8,128)(2,1)}, bf16[16,512,1536]{2,1,0:T(...) conditional(s32[]{:T(128)} %convert_element_type.43, ...), branch_computations={%region_1.0_spmd, %region_2.2_spmd} | conditional | flops 31000000512 | bytes 90000088 | solution.py:794
  61.0 49.4 %conditional.8 = ((bf16[512,1536]{1,0:T(8,128)(2,1)}, bf16[16,512,1536]{2,1,0:T(8,128)(2,1)}, bf16[16,512,1536]{2,1,0:T(8,128)(2,1)}, bf16[16,512,1536]{2,1,0:T(...) conditional(s32[]{:T(128)} %convert_element_type.43, ...), branch_computations={%region_1.0_spmd, %region_2.2_spmd} | conditional | flops 31000000512 | bytes 90000088 | solution.py:794
  115.6 49.4 %conditional.8 = ((bf16[512,1536]{1,0:T(8,128)(2,1)}, bf16[16,512,1536]{2,1,0:T(8,128)(2,1)}, bf16[16,512,1536]{2,1,0:T(8,128)(2,1)}, bf16[16,512,1536]{2,1,0:T(...) conditional(s32[]{:T(128)} %convert_element_type.43, ...), branch_computations={%region_1.0_spmd, %region_2.2_spmd} | conditional | flops 31000000512 | bytes 90000088 | solution.py:794
  184.3 49.4 %conditional.8 = ((bf16[512,1536]{1,0:T(8,128)(2,1)}, bf16[16,512,1536]{2,1,0:T(8,128)(2,1)}, bf16[16,512,1536]{2,1,0:T(8,128)(2,1)}, bf16[16,512,1536]{2,1,0:T(...) conditional(s32[]{:T(128)} %convert_element_type.43, ...), branch_computations={%region_1.0_spmd, %region_2.2_spmd} | conditional | flops 31000000512 | bytes 90000088 | solution.py:794
  255.4 49.4 %conditional.8 = ((bf16[512,1536]{1,0:T(8,128)(2,1)}, bf16[16,512,1536]{2,1,0:T(8,128)(2,1)}, bf16[16,512,1536]{2,1,0:T(8,128)(2,1)}, bf16[16,512,1536]{2,1,0:T(...) conditional(s32[]{:T(128)} %convert_element_type.43, ...), branch_computations={%region_1.0_spmd, %region_2.2_spmd} | conditional | flops 31000000512 | bytes 90000088 | solution.py:794
  256.0 48.8 %layer_fwd.2 = (bf16[512,1536]{1,0:T(8,128)(2,1)}, bf16[16,512,1536]{2,1,0:T(8,128)(2,1)}, bf16[16,512,1536]{2,1,0:T(8,128)(2,1)}, bf16[16,512,1536]{2,1,0:T(8,1...) custom-call(s32[3]{0:T(128)} %pad_add_fusion.idx, ...), custom_call_target="tpu_custom_call", output_to_operand_aliasing={{0}: (15, {}), {1}: (16, {}), {2}: (17, {}), {3}: (18, {}),... | custom-call | flops 31000000512 | bytes 90000000 | tf_op jit(solution)/shard_map/while/body/eval_jaxpr/cond/branch_1_fun/layer_fwd/pallas_call | solution.py:310
  326.5 49.4 %conditional.8 = ((bf16[512,1536]{1,0:T(8,128)(2,1)}, bf16[16,512,1536]{2,1,0:T(8,128)(2,1)}, bf16[16,512,1536]{2,1,0:T(8,128)(2,1)}, bf16[16,512,1536]{2,1,0:T(...) conditional(s32[]{:T(128)} %convert_element_type.43, ...), branch_computations={%region_1.0_spmd, %region_2.2_spmd} | conditional | flops 31000000512 | bytes 90000088 | solution.py:794
  397.6 49.4 %conditional.8 = ((bf16[512,1536]{1,0:T(8,128)(2,1)}, bf16[16,512,1536]{2,1,0:T(8,128)(2,1)}, bf16[16,512,1536]{2,1,0:T(8,128)(2,1)}, bf16[16,512,1536]{2,1,0:T(...) conditional(s32[]{:T(128)} %convert_element_type.43, ...), branch_computations={%region_1.0_spmd, %region_2.2_spmd} | conditional | flops 31000000512 | bytes 90000088 | solution.py:794
  468.8 1871.3 %while.140 = (s32[]{:T(128)}, bf16[512,1536]{1,0:T(8,128)(2,1)}, bf16[512,1536]{1,0:T(8,128)(2,1)}, bf16[16,512,1536]{2,1,0:T(8,128)(2,1)}, bf16[16,512,1536]{2,...) while((s32[]{:T(128)}, bf16[512,1536]{1,0:T(8,128)(2,1)}, ...), condition=%wide.region_9.10_spmd, body=%wide.region_4.9_spmd.sunk | while | flops 67000000512 | bytes 228877328 | solution.py:843
  488.7 49.4 %conditional.9 = (bf16[512,1536]{1,0:T(8,128)(2,1)}, bf16[16,512,1536]{2,1,0:T(8,128)(2,1)}, bf16[16,512,1536]{2,1,0:T(8,128)(2,1)}, bf16[16,512,1536]{2,1,0:T(8...) conditional(s32[]{:T(128)} %convert_element_type.44, ...), branch_computations={%region_5.5_spmd, %region_6.6_spmd} | conditional | flops 31000000512 | bytes 100001528 | solution.py:823
  561.8 49.4 %conditional.9 = (bf16[512,1536]{1,0:T(8,128)(2,1)}, bf16[16,512,1536]{2,1,0:T(8,128)(2,1)}, bf16[16,512,1536]{2,1,0:T(8,128)(2,1)}, bf16[16,512,1536]{2,1,0:T(8...) conditional(s32[]{:T(128)} %convert_element_type.44, ...), branch_computations={%region_5.5_spmd, %region_6.6_spmd} | conditional | flops 31000000512 | bytes 100001528 | solution.py:823
  634.9 49.4 %conditional.9 = (bf16[512,1536]{1,0:T(8,128)(2,1)}, bf16[16,512,1536]{2,1,0:T(8,128)(2,1)}, bf16[16,512,1536]{2,1,0:T(8,128)(2,1)}, bf16[16,512,1536]{2,1,0:T(8...) conditional(s32[]{:T(128)} %convert_element_type.44, ...), branch_computations={%region_5.5_spmd, %region_6.6_spmd} | conditional | flops 31000000512 | bytes 100001528 | solution.py:823
  708.0 49.4 %conditional.9 = (bf16[512,1536]{1,0:T(8,128)(2,1)}, bf16[16,512,1536]{2,1,0:T(8,128)(2,1)}, bf16[16,512,1536]{2,1,0:T(8,128)(2,1)}, bf16[16,512,1536]{2,1,0:T(8...) conditional(s32[]{:T(128)} %convert_element_type.44, ...), branch_computations={%region_5.5_spmd, %region_6.6_spmd} | conditional | flops 31000000512 | bytes 100001528 | solution.py:823
  781.1 49.4 %conditional.9 = (bf16[512,1536]{1,0:T(8,128)(2,1)}, bf16[16,512,1536]{2,1,0:T(8,128)(2,1)}, bf16[16,512,1536]{2,1,0:T(8,128)(2,1)}, bf16[16,512,1536]{2,1,0:T(8...) conditional(s32[]{:T(128)} %convert_element_type.44, ...), branch_computations={%region_5.5_spmd, %region_6.6_spmd} | conditional | flops 31000000512 | bytes 100001528 | solution.py:823
  854.3 49.4 %conditional.9 = (bf16[512,1536]{1,0:T(8,128)(2,1)}, bf16[16,512,1536]{2,1,0:T(8,128)(2,1)}, bf16[16,512,1536]{2,1,0:T(8,128)(2,1)}, bf16[16,512,1536]{2,1,0:T(8...) conditional(s32[]{:T(128)} %convert_element_type.44, ...), branch_computations={%region_5.5_spmd, %region_6.6_spmd} | conditional | flops 31000000512 | bytes 100001528 | solution.py:823
  927.4 49.4 %conditional.9 = (bf16[512,1536]{1,0:T(8,128)(2,1)}, bf16[16,512,1536]{2,1,0:T(8,128)(2,1)}, bf16[16,512,1536]{2,1,0:T(8,128)(2,1)}, bf16[16,512,1536]{2,1,0:T(8...) conditional(s32[]{:T(128)} %convert_element_type.44, ...), branch_computations={%region_5.5_spmd, %region_6.6_spmd} | conditional | flops 31000000512 | bytes 100001528 | solution.py:823
  1000.5 49.4 %conditional.9 = (bf16[512,1536]{1,0:T(8,128)(2,1)}, bf16[16,512,1536]{2,1,0:T(8,128)(2,1)}, bf16[16,512,1536]{2,1,0:T(8,128)(2,1)}, bf16[16,512,1536]{2,1,0:T(8...) conditional(s32[]{:T(128)} %convert_element_type.44, ...), branch_computations={%region_5.5_spmd, %region_6.6_spmd} | conditional | flops 31000000512 | bytes 100001528 | solution.py:823
  1049.9 285.4 %collective-permute-start.1 = (bf16[512,1536]{1,0:T(8,128)(2,1)}, bf16[512,1536]{1,0:T(8,128)(2,1)}, u32[]{:S(2)}, u32[]{:S(2)}) collective-permute-start(bf16[512,1536]{1,0:T(8,128)(2,1)} %get-tuple-element.4000), channel_id=1, source_target_pairs={{0,1},{1,2},{2,3},{3,4},{4,5},{5,6},{6,7}} | collective-permute-start | bytes 4718600 | tf_op jit(solution)/shard_map/while/body/eval_jaxpr/ppermute | solution.py:824
  1335.4 61.1 %conditional.10 = ((bf16[512,1536]{1,0:T(8,128)(2,1)}, bf16[16,512,1536]{2,1,0:T(8,128)(2,1)}, bf16[16,512,6144]{2,1,0:T(8,128)(2,1)}, bf16[16,512,1536]{2,1,0:T...) conditional(s32[]{:T(128)} %convert_element_type.45, ...), branch_computations={%region_7.7_spmd, %region_8.8_spmd} | conditional | flops 35999997952 | bytes 110000088 | solution.py:800
  1336.0 60.5 %layer_bwd.2 = (bf16[512,1536]{1,0:T(8,128)(2,1)}, bf16[16,512,1536]{2,1,0:T(8,128)(2,1)}, bf16[16,512,6144]{2,1,0:T(8,128)(2,1)}, bf16[16,512,1536]{2,1,0:T(8,1...) custom-call(s32[3]{0:T(128)} %pad_add_fusion.2.idx, ...), custom_call_target="tpu_custom_call", output_to_operand_aliasing={{0}: (15, {}), {1}: (16, {}), {2}: (17, {}), {3}: (18, {}),... | custom-call | flops 35999997952 | bytes 110000000 | tf_op jit(solution)/shard_map/while/body/eval_jaxpr/cond/branch_1_fun/layer_bwd/pallas_call | solution.py:586
  1398.7 49.4 %conditional.9 = (bf16[512,1536]{1,0:T(8,128)(2,1)}, bf16[16,512,1536]{2,1,0:T(8,128)(2,1)}, bf16[16,512,1536]{2,1,0:T(8,128)(2,1)}, bf16[16,512,1536]{2,1,0:T(8...) conditional(s32[]{:T(128)} %convert_element_type.44, ...), branch_computations={%region_5.5_spmd, %region_6.6_spmd} | conditional | flops 31000000512 | bytes 100001528 | solution.py:823
  1399.3 48.8 %layer_fwd.3 = (bf16[512,1536]{1,0:T(8,128)(2,1)}, bf16[16,512,1536]{2,1,0:T(8,128)(2,1)}, bf16[16,512,1536]{2,1,0:T(8,128)(2,1)}, bf16[16,512,1536]{2,1,0:T(8,1...) custom-call(s32[3]{0:T(128)} %pad_add_fusion.1.idx, ...), custom_call_target="tpu_custom_call", output_to_operand_aliasing={{0}: (15, {}), {1}: (16, {}), {2}: (17, {}), {3}: (18, {}),... | custom-call | flops 31000000512 | bytes 90000000 | tf_op jit(solution)/shard_map/while/body/eval_jaxpr/cond/branch_1_fun/layer_fwd/pallas_call | solution.py:310
  1452.9 61.0 %conditional.10 = ((bf16[512,1536]{1,0:T(8,128)(2,1)}, bf16[16,512,1536]{2,1,0:T(8,128)(2,1)}, bf16[16,512,6144]{2,1,0:T(8,128)(2,1)}, bf16[16,512,1536]{2,1,0:T...) conditional(s32[]{:T(128)} %convert_element_type.45, ...), branch_computations={%region_7.7_spmd, %region_8.8_spmd} | conditional | flops 35999997952 | bytes 110000088 | solution.py:800
  1453.5 60.4 %layer_bwd.2 = (bf16[512,1536]{1,0:T(8,128)(2,1)}, bf16[16,512,1536]{2,1,0:T(8,128)(2,1)}, bf16[16,512,6144]{2,1,0:T(8,128)(2,1)}, bf16[16,512,1536]{2,1,0:T(8,1...) custom-call(s32[3]{0:T(128)} %pad_add_fusion.2.idx, ...), custom_call_target="tpu_custom_call", output_to_operand_aliasing={{0}: (15, {}), {1}: (16, {}), {2}: (17, {}), {3}: (18, {}),... | custom-call | flops 35999997952 | bytes 110000000 | tf_op jit(solution)/shard_map/while/body/eval_jaxpr/cond/branch_1_fun/layer_bwd/pallas_call | solution.py:586
  1570.4 61.1 %conditional.10 = ((bf16[512,1536]{1,0:T(8,128)(2,1)}, bf16[16,512,1536]{2,1,0:T(8,128)(2,1)}, bf16[16,512,6144]{2,1,0:T(8,128)(2,1)}, bf16[16,512,1536]{2,1,0:T...) conditional(s32[]{:T(128)} %convert_element_type.45, ...), branch_computations={%region_7.7_spmd, %region_8.8_spmd} | conditional | flops 35999997952 | bytes 110000088 | solution.py:800
  1571.0 60.4 %layer_bwd.2 = (bf16[512,1536]{1,0:T(8,128)(2,1)}, bf16[16,512,1536]{2,1,0:T(8,128)(2,1)}, bf16[16,512,6144]{2,1,0:T(8,128)(2,1)}, bf16[16,512,1536]{2,1,0:T(8,1...) custom-call(s32[3]{0:T(128)} %pad_add_fusion.2.idx, ...), custom_call_target="tpu_custom_call", output_to_operand_aliasing={{0}: (15, {}), {1}: (16, {}), {2}: (17, {}), {3}: (18, {}),... | custom-call | flops 35999997952 | bytes 110000000 | tf_op jit(solution)/shard_map/while/body/eval_jaxpr/cond/branch_1_fun/layer_bwd/pallas_call | solution.py:586
  1674.7 61.0 %conditional.10 = ((bf16[512,1536]{1,0:T(8,128)(2,1)}, bf16[16,512,1536]{2,1,0:T(8,128)(2,1)}, bf16[16,512,6144]{2,1,0:T(8,128)(2,1)}, bf16[16,512,1536]{2,1,0:T...) conditional(s32[]{:T(128)} %convert_element_type.45, ...), branch_computations={%region_7.7_spmd, %region_8.8_spmd} | conditional | flops 35999997952 | bytes 110000088 | solution.py:800
  1675.3 60.4 %layer_bwd.2 = (bf16[512,1536]{1,0:T(8,128)(2,1)}, bf16[16,512,1536]{2,1,0:T(8,128)(2,1)}, bf16[16,512,6144]{2,1,0:T(8,128)(2,1)}, bf16[16,512,1536]{2,1,0:T(8,1...) custom-call(s32[3]{0:T(128)} %pad_add_fusion.2.idx, ...), custom_call_target="tpu_custom_call", output_to_operand_aliasing={{0}: (15, {}), {1}: (16, {}), {2}: (17, {}), {3}: (18, {}),... | custom-call | flops 35999997952 | bytes 110000000 | tf_op jit(solution)/shard_map/while/body/eval_jaxpr/cond/branch_1_fun/layer_bwd/pallas_call | solution.py:586
  1792.3 61.0 %conditional.10 = ((bf16[512,1536]{1,0:T(8,128)(2,1)}, bf16[16,512,1536]{2,1,0:T(8,128)(2,1)}, bf16[16,512,6144]{2,1,0:T(8,128)(2,1)}, bf16[16,512,1536]{2,1,0:T...) conditional(s32[]{:T(128)} %convert_element_type.45, ...), branch_computations={%region_7.7_spmd, %region_8.8_spmd} | conditional | flops 35999997952 | bytes 110000088 | solution.py:800
  1792.9 60.4 %layer_bwd.2 = (bf16[512,1536]{1,0:T(8,128)(2,1)}, bf16[16,512,1536]{2,1,0:T(8,128)(2,1)}, bf16[16,512,6144]{2,1,0:T(8,128)(2,1)}, bf16[16,512,1536]{2,1,0:T(8,1...) custom-call(s32[3]{0:T(128)} %pad_add_fusion.2.idx, ...), custom_call_target="tpu_custom_call", output_to_operand_aliasing={{0}: (15, {}), {1}: (16, {}), {2}: (17, {}), {3}: (18, {}),... | custom-call | flops 35999997952 | bytes 110000000 | tf_op jit(solution)/shard_map/while/body/eval_jaxpr/cond/branch_1_fun/layer_bwd/pallas_call | solution.py:586
  1855.5 50.9 %conditional.9 = (bf16[512,1536]{1,0:T(8,128)(2,1)}, bf16[16,512,1536]{2,1,0:T(8,128)(2,1)}, bf16[16,512,1536]{2,1,0:T(8,128)(2,1)}, bf16[16,512,1536]{2,1,0:T(8...) conditional(s32[]{:T(128)} %convert_element_type.44, ...), branch_computations={%region_5.5_spmd, %region_6.6_spmd} | conditional | flops 31000000512 | bytes 100001528 | solution.py:823
  1856.2 50.1 %weight_grad.3 = (f32[1536,4608]{1,0:T(8,128)}, f32[1536,1536]{1,0:T(8,128)}, f32[1536,6144]{1,0:T(8,128)}, f32[6144,1536]{1,0:T(8,128)}) custom-call(s32[6,16]{1,0:T(8,128)} %stack.76.tab, bf16[16,512,1536]{2,1,0:T(8,128)(2,1)} %get-tuple-element.3739.h1, ...), custom_call_target="tpu_custom_call", output_to_operand_aliasing={{0}: (9, {}), {1}: (10, {}), {2}: (11, {}), {3}: (12, {})} | custom-call | flops 20000000000 | bytes 100000000 | tf_op jit(solution)/shard_map/while/body/eval_jaxpr/cond/branch_0_fun/weight_grad/pallas_call | solution.py:701
  1908.8 61.1 %conditional.10 = ((bf16[512,1536]{1,0:T(8,128)(2,1)}, bf16[16,512,1536]{2,1,0:T(8,128)(2,1)}, bf16[16,512,6144]{2,1,0:T(8,128)(2,1)}, bf16[16,512,1536]{2,1,0:T...) conditional(s32[]{:T(128)} %convert_element_type.45, ...), branch_computations={%region_7.7_spmd, %region_8.8_spmd} | conditional | flops 35999997952 | bytes 110000088 | solution.py:800
  1909.5 60.4 %layer_bwd.2 = (bf16[512,1536]{1,0:T(8,128)(2,1)}, bf16[16,512,1536]{2,1,0:T(8,128)(2,1)}, bf16[16,512,6144]{2,1,0:T(8,128)(2,1)}, bf16[16,512,1536]{2,1,0:T(8,1...) custom-call(s32[3]{0:T(128)} %pad_add_fusion.2.idx, ...), custom_call_target="tpu_custom_call", output_to_operand_aliasing={{0}: (15, {}), {1}: (16, {}), {2}: (17, {}), {3}: (18, {}),... | custom-call | flops 35999997952 | bytes 110000000 | tf_op jit(solution)/shard_map/while/body/eval_jaxpr/cond/branch_1_fun/layer_bwd/pallas_call | solution.py:586
  1972.1 50.9 %conditional.9 = (bf16[512,1536]{1,0:T(8,128)(2,1)}, bf16[16,512,1536]{2,1,0:T(8,128)(2,1)}, bf16[16,512,1536]{2,1,0:T(8,128)(2,1)}, bf16[16,512,1536]{2,1,0:T(8...) conditional(s32[]{:T(128)} %convert_element_type.44, ...), branch_computations={%region_5.5_spmd, %region_6.6_spmd} | conditional | flops 31000000512 | bytes 100001528 | solution.py:823
  1972.8 50.2 %weight_grad.3 = (f32[1536,4608]{1,0:T(8,128)}, f32[1536,1536]{1,0:T(8,128)}, f32[1536,6144]{1,0:T(8,128)}, f32[6144,1536]{1,0:T(8,128)}) custom-call(s32[6,16]{1,0:T(8,128)} %stack.76.tab, bf16[16,512,1536]{2,1,0:T(8,128)(2,1)} %get-tuple-element.3739.h1, ...), custom_call_target="tpu_custom_call", output_to_operand_aliasing={{0}: (9, {}), {1}: (10, {}), {2}: (11, {}), {3}: (12, {})} | custom-call | flops 20000000000 | bytes 100000000 | tf_op jit(solution)/shard_map/while/body/eval_jaxpr/cond/branch_0_fun/weight_grad/pallas_call | solution.py:701
  2028.7 61.0 %conditional.10 = ((bf16[512,1536]{1,0:T(8,128)(2,1)}, bf16[16,512,1536]{2,1,0:T(8,128)(2,1)}, bf16[16,512,6144]{2,1,0:T(8,128)(2,1)}, bf16[16,512,1536]{2,1,0:T...) conditional(s32[]{:T(128)} %convert_element_type.45, ...), branch_computations={%region_7.7_spmd, %region_8.8_spmd} | conditional | flops 35999997952 | bytes 110000088 | solution.py:800
  2029.4 60.4 %layer_bwd.2 = (bf16[512,1536]{1,0:T(8,128)(2,1)}, bf16[16,512,1536]{2,1,0:T(8,128)(2,1)}, bf16[16,512,6144]{2,1,0:T(8,128)(2,1)}, bf16[16,512,1536]{2,1,0:T(8,1...) custom-call(s32[3]{0:T(128)} %pad_add_fusion.2.idx, ...), custom_call_target="tpu_custom_call", output_to_operand_aliasing={{0}: (15, {}), {1}: (16, {}), {2}: (17, {}), {3}: (18, {}),... | custom-call | flops 35999997952 | bytes 110000000 | tf_op jit(solution)/shard_map/while/body/eval_jaxpr/cond/branch_1_fun/layer_bwd/pallas_call | solution.py:586
  2092.0 50.9 %conditional.9 = (bf16[512,1536]{1,0:T(8,128)(2,1)}, bf16[16,512,1536]{2,1,0:T(8,128)(2,1)}, bf16[16,512,1536]{2,1,0:T(8,128)(2,1)}, bf16[16,512,1536]{2,1,0:T(8...) conditional(s32[]{:T(128)} %convert_element_type.44, ...), branch_computations={%region_5.5_spmd, %region_6.6_spmd} | conditional | flops 31000000512 | bytes 100001528 | solution.py:823
  2092.7 50.1 %weight_grad.3 = (f32[1536,4608]{1,0:T(8,128)}, f32[1536,1536]{1,0:T(8,128)}, f32[1536,6144]{1,0:T(8,128)}, f32[6144,1536]{1,0:T(8,128)}) custom-call(s32[6,16]{1,0:T(8,128)} %stack.76.tab, bf16[16,512,1536]{2,1,0:T(8,128)(2,1)} %get-tuple-element.3739.h1, ...), custom_call_target="tpu_custom_call", output_to_operand_aliasing={{0}: (9, {}), {1}: (10, {}), {2}: (11, {}), {3}: (12, {})} | custom-call | flops 20000000000 | bytes 100000000 | tf_op jit(solution)/shard_map/while/body/eval_jaxpr/cond/branch_0_fun/weight_grad/pallas_call | solution.py:701
  2147.2 61.1 %conditional.10 = ((bf16[512,1536]{1,0:T(8,128)(2,1)}, bf16[16,512,1536]{2,1,0:T(8,128)(2,1)}, bf16[16,512,6144]{2,1,0:T(8,128)(2,1)}, bf16[16,512,1536]{2,1,0:T...) conditional(s32[]{:T(128)} %convert_element_type.45, ...), branch_computations={%region_7.7_spmd, %region_8.8_spmd} | conditional | flops 35999997952 | bytes 110000088 | solution.py:800
  2147.8 60.5 %layer_bwd.2 = (bf16[512,1536]{1,0:T(8,128)(2,1)}, bf16[16,512,1536]{2,1,0:T(8,128)(2,1)}, bf16[16,512,6144]{2,1,0:T(8,128)(2,1)}, bf16[16,512,1536]{2,1,0:T(8,1...) custom-call(s32[3]{0:T(128)} %pad_add_fusion.2.idx, ...), custom_call_target="tpu_custom_call", output_to_operand_aliasing={{0}: (15, {}), {1}: (16, {}), {2}: (17, {}), {3}: (18, {}),... | custom-call | flops 35999997952 | bytes 110000000 | tf_op jit(solution)/shard_map/while/body/eval_jaxpr/cond/branch_1_fun/layer_bwd/pallas_call | solution.py:586
  2210.5 50.9 %conditional.9 = (bf16[512,1536]{1,0:T(8,128)(2,1)}, bf16[16,512,1536]{2,1,0:T(8,128)(2,1)}, bf16[16,512,1536]{2,1,0:T(8,128)(2,1)}, bf16[16,512,1536]{2,1,0:T(8...) conditional(s32[]{:T(128)} %convert_element_type.44, ...), branch_computations={%region_5.5_spmd, %region_6.6_spmd} | conditional | flops 31000000512 | bytes 100001528 | solution.py:823
  2211.2 50.1 %weight_grad.3 = (f32[1536,4608]{1,0:T(8,128)}, f32[1536,1536]{1,0:T(8,128)}, f32[1536,6144]{1,0:T(8,128)}, f32[6144,1536]{1,0:T(8,128)}) custom-call(s32[6,16]{1,0:T(8,128)} %stack.76.tab, bf16[16,512,1536]{2,1,0:T(8,128)(2,1)} %get-tuple-element.3739.h1, ...), custom_call_target="tpu_custom_call", output_to_operand_aliasing={{0}: (9, {}), {1}: (10, {}), {2}: (11, {}), {3}: (12, {})} | custom-call | flops 20000000000 | bytes 100000000 | tf_op jit(solution)/shard_map/while/body/eval_jaxpr/cond/branch_0_fun/weight_grad/pallas_call | solution.py:701
  2265.6 61.1 %conditional.10 = ((bf16[512,1536]{1,0:T(8,128)(2,1)}, bf16[16,512,1536]{2,1,0:T(8,128)(2,1)}, bf16[16,512,6144]{2,1,0:T(8,128)(2,1)}, bf16[16,512,1536]{2,1,0:T...) conditional(s32[]{:T(128)} %convert_element_type.45, ...), branch_computations={%region_7.7_spmd, %region_8.8_spmd} | conditional | flops 35999997952 | bytes 110000088 | solution.py:800
  2266.2 60.5 %layer_bwd.2 = (bf16[512,1536]{1,0:T(8,128)(2,1)}, bf16[16,512,1536]{2,1,0:T(8,128)(2,1)}, bf16[16,512,6144]{2,1,0:T(8,128)(2,1)}, bf16[16,512,1536]{2,1,0:T(8,1...) custom-call(s32[3]{0:T(128)} %pad_add_fusion.2.idx, ...), custom_call_target="tpu_custom_call", output_to_operand_aliasing={{0}: (15, {}), {1}: (16, {}), {2}: (17, {}), {3}: (18, {}),... | custom-call | flops 35999997952 | bytes 110000000 | tf_op jit(solution)/shard_map/while/body/eval_jaxpr/cond/branch_1_fun/layer_bwd/pallas_call | solution.py:586
  2341.2 647.7 %while.141 = (s32[]{:T(128)}, bf16[512,1536]{1,0:T(8,128)(2,1)}, bf16[16,512,1536]{2,1,0:T(8,128)(2,1)}, bf16[16,512,6144]{2,1,0:T(8,128)(2,1)}, bf16[16,512,153...) while((s32[]{:T(128)}, bf16[512,1536]{1,0:T(8,128)(2,1)}, ...), condition=%wide.region_13.14_spmd, body=%wide.region_10.13_spmd.sunk | while | flops 35999997952 | bytes 116292416 | solution.py:846
  2346.5 61.0 %conditional.11 = (bf16[512,1536]{1,0:T(8,128)(2,1)}, bf16[16,512,1536]{2,1,0:T(8,128)(2,1)}, bf16[16,512,6144]{2,1,0:T(8,128)(2,1)}, bf16[16,512,1536]{2,1,0:T(...) conditional(s32[]{:T(128)} %convert_element_type.46, ...), branch_computations={%region_11.11_spmd, %region_12.12_spmd} | conditional | flops 35999997952 | bytes 110000192 | solution.py:839
  2347.2 60.4 %layer_bwd.3 = (bf16[512,1536]{1,0:T(8,128)(2,1)}, bf16[16,512,1536]{2,1,0:T(8,128)(2,1)}, bf16[16,512,6144]{2,1,0:T(8,128)(2,1)}, bf16[16,512,1536]{2,1,0:T(8,1...) custom-call(s32[3]{0:T(128)} %pad_add_fusion.3.idx, ...), custom_call_target="tpu_custom_call", output_to_operand_aliasing={{0}: (15, {}), {1}: (16, {}), {2}: (17, {}), {3}: (18, {}),... | custom-call | flops 35999997952 | bytes 110000000 | tf_op jit(solution)/shard_map/while/body/eval_jaxpr/cond/branch_1_fun/layer_bwd/pallas_call | solution.py:586
  2448.4 61.1 %conditional.11 = (bf16[512,1536]{1,0:T(8,128)(2,1)}, bf16[16,512,1536]{2,1,0:T(8,128)(2,1)}, bf16[16,512,6144]{2,1,0:T(8,128)(2,1)}, bf16[16,512,1536]{2,1,0:T(...) conditional(s32[]{:T(128)} %convert_element_type.46, ...), branch_computations={%region_11.11_spmd, %region_12.12_spmd} | conditional | flops 35999997952 | bytes 110000192 | solution.py:839
  2449.1 60.4 %layer_bwd.3 = (bf16[512,1536]{1,0:T(8,128)(2,1)}, bf16[16,512,1536]{2,1,0:T(8,128)(2,1)}, bf16[16,512,6144]{2,1,0:T(8,128)(2,1)}, bf16[16,512,1536]{2,1,0:T(8,1...) custom-call(s32[3]{0:T(128)} %pad_add_fusion.3.idx, ...), custom_call_target="tpu_custom_call", output_to_operand_aliasing={{0}: (15, {}), {1}: (16, {}), {2}: (17, {}), {3}: (18, {}),... | custom-call | flops 35999997952 | bytes 110000000 | tf_op jit(solution)/shard_map/while/body/eval_jaxpr/cond/branch_1_fun/layer_bwd/pallas_call | solution.py:586
  2546.3 61.1 %conditional.11 = (bf16[512,1536]{1,0:T(8,128)(2,1)}, bf16[16,512,1536]{2,1,0:T(8,128)(2,1)}, bf16[16,512,6144]{2,1,0:T(8,128)(2,1)}, bf16[16,512,1536]{2,1,0:T(...) conditional(s32[]{:T(128)} %convert_element_type.46, ...), branch_computations={%region_11.11_spmd, %region_12.12_spmd} | conditional | flops 35999997952 | bytes 110000192 | solution.py:839
  2547.0 60.5 %layer_bwd.3 = (bf16[512,1536]{1,0:T(8,128)(2,1)}, bf16[16,512,1536]{2,1,0:T(8,128)(2,1)}, bf16[16,512,6144]{2,1,0:T(8,128)(2,1)}, bf16[16,512,1536]{2,1,0:T(8,1...) custom-call(s32[3]{0:T(128)} %pad_add_fusion.3.idx, ...), custom_call_target="tpu_custom_call", output_to_operand_aliasing={{0}: (15, {}), {1}: (16, {}), {2}: (17, {}), {3}: (18, {}),... | custom-call | flops 35999997952 | bytes 110000000 | tf_op jit(solution)/shard_map/while/body/eval_jaxpr/cond/branch_1_fun/layer_bwd/pallas_call | solution.py:586
  2646.8 61.0 %conditional.11 = (bf16[512,1536]{1,0:T(8,128)(2,1)}, bf16[16,512,1536]{2,1,0:T(8,128)(2,1)}, bf16[16,512,6144]{2,1,0:T(8,128)(2,1)}, bf16[16,512,1536]{2,1,0:T(...) conditional(s32[]{:T(128)} %convert_element_type.46, ...), branch_computations={%region_11.11_spmd, %region_12.12_spmd} | conditional | flops 35999997952 | bytes 110000192 | solution.py:839
  2647.4 60.3 %layer_bwd.3 = (bf16[512,1536]{1,0:T(8,128)(2,1)}, bf16[16,512,1536]{2,1,0:T(8,128)(2,1)}, bf16[16,512,6144]{2,1,0:T(8,128)(2,1)}, bf16[16,512,1536]{2,1,0:T(8,1...) custom-call(s32[3]{0:T(128)} %pad_add_fusion.3.idx, ...), custom_call_target="tpu_custom_call", output_to_operand_aliasing={{0}: (15, {}), {1}: (16, {}), {2}: (17, {}), {3}: (18, {}),... | custom-call | flops 35999997952 | bytes 110000000 | tf_op jit(solution)/shard_map/while/body/eval_jaxpr/cond/branch_1_fun/layer_bwd/pallas_call | solution.py:586
  2709.1 53.6 %collective-permute-done.3 = bf16[512,1536]{1,0:T(8,128)(2,1)} collective-permute-done((bf16[512,1536]{1,0:T(8,128)(2,1)}, bf16[512,1536]{1,0:T(8,128)(2,1)}, u32[]{:S(2)}, u32[]{:S(2)}) %collective-permute-start.3) | collective-permute-done | bytes 1572896 | tf_op jit(solution)/shard_map/while/body/eval_jaxpr/ppermute | solution.py:830
  2762.7 61.0 %conditional.11 = (bf16[512,1536]{1,0:T(8,128)(2,1)}, bf16[16,512,1536]{2,1,0:T(8,128)(2,1)}, bf16[16,512,6144]{2,1,0:T(8,128)(2,1)}, bf16[16,512,1536]{2,1,0:T(...) conditional(s32[]{:T(128)} %convert_element_type.46, ...), branch_computations={%region_11.11_spmd, %region_12.12_spmd} | conditional | flops 35999997952 | bytes 110000192 | solution.py:839
  2763.4 60.3 %layer_bwd.3 = (bf16[512,1536]{1,0:T(8,128)(2,1)}, bf16[16,512,1536]{2,1,0:T(8,128)(2,1)}, bf16[16,512,6144]{2,1,0:T(8,128)(2,1)}, bf16[16,512,1536]{2,1,0:T(8,1...) custom-call(s32[3]{0:T(128)} %pad_add_fusion.3.idx, ...), custom_call_target="tpu_custom_call", output_to_operand_aliasing={{0}: (15, {}), {1}: (16, {}), {2}: (17, {}), {3}: (18, {}),... | custom-call | flops 35999997952 | bytes 110000000 | tf_op jit(solution)/shard_map/while/body/eval_jaxpr/cond/branch_1_fun/layer_bwd/pallas_call | solution.py:586
  2845.2 61.1 %conditional.11 = (bf16[512,1536]{1,0:T(8,128)(2,1)}, bf16[16,512,1536]{2,1,0:T(8,128)(2,1)}, bf16[16,512,6144]{2,1,0:T(8,128)(2,1)}, bf16[16,512,1536]{2,1,0:T(...) conditional(s32[]{:T(128)} %convert_element_type.46, ...), branch_computations={%region_11.11_spmd, %region_12.12_spmd} | conditional | flops 35999997952 | bytes 110000192 | solution.py:839
  2845.9 60.4 %layer_bwd.3 = (bf16[512,1536]{1,0:T(8,128)(2,1)}, bf16[16,512,1536]{2,1,0:T(8,128)(2,1)}, bf16[16,512,6144]{2,1,0:T(8,128)(2,1)}, bf16[16,512,1536]{2,1,0:T(8,1...) custom-call(s32[3]{0:T(128)} %pad_add_fusion.3.idx, ...), custom_call_target="tpu_custom_call", output_to_operand_aliasing={{0}: (15, {}), {1}: (16, {}), {2}: (17, {}), {3}: (18, {}),... | custom-call | flops 35999997952 | bytes 110000000 | tf_op jit(solution)/shard_map/while/body/eval_jaxpr/cond/branch_1_fun/layer_bwd/pallas_call | solution.py:586
  2927.6 61.1 %conditional.11 = (bf16[512,1536]{1,0:T(8,128)(2,1)}, bf16[16,512,1536]{2,1,0:T(8,128)(2,1)}, bf16[16,512,6144]{2,1,0:T(8,128)(2,1)}, bf16[16,512,1536]{2,1,0:T(...) conditional(s32[]{:T(128)} %convert_element_type.46, ...), branch_computations={%region_11.11_spmd, %region_12.12_spmd} | conditional | flops 35999997952 | bytes 110000192 | solution.py:839
  2928.3 60.4 %layer_bwd.3 = (bf16[512,1536]{1,0:T(8,128)(2,1)}, bf16[16,512,1536]{2,1,0:T(8,128)(2,1)}, bf16[16,512,6144]{2,1,0:T(8,128)(2,1)}, bf16[16,512,1536]{2,1,0:T(8,1...) custom-call(s32[3]{0:T(128)} %pad_add_fusion.3.idx, ...), custom_call_target="tpu_custom_call", output_to_operand_aliasing={{0}: (15, {}), {1}: (16, {}), {2}: (17, {}), {3}: (18, {}),... | custom-call | flops 35999997952 | bytes 110000000 | tf_op jit(solution)/shard_map/while/body/eval_jaxpr/cond/branch_1_fun/layer_bwd/pallas_call | solution.py:586
  2993.3 335.8 %weight_grad.5 = (f32[1536,4608]{1,0:T(8,128)}, f32[1536,1536]{1,0:T(8,128)}, f32[1536,6144]{1,0:T(8,128)}, f32[6144,1536]{1,0:T(8,128)}) custom-call(s32[6,104]{1,0:T(8,128)} %stack.97.tab, bf16[16,512,1536]{2,1,0:T(8,128)(2,1)} %get-tuple-element.4180, ...), custom_call_target="tpu_custom_call", output_to_operand_aliasing={{0}: (9, {}), {1}: (10, {}), {2}: (11, {}), {3}: (12, {})} | custom-call | flops 20000000000 | bytes 100000000 | tf_op jit(solution)/shard_map/weight_grad/pallas_call | solution.py:701
  (278 shorter events, 1510.1 us)
Async XLA Ops:
  7.2 2981.8 %all-reduce.3.cloned.1.call-start = ((), (), s32[]{:S(2)}) async-start(), calls=%async_computation | async-start | bytes 50331648 | tf_op jit(solution)/shard_map/psum | solution.py:845
  56.7 4.3 collective-permute-start
  110.4 5.3 collective-permute-start
  165.0 19.3 collective-permute-start
  233.7 21.7 collective-permute-start
  304.8 21.7 collective-permute-start
  375.9 21.7 collective-permute-start
  447.0 21.7 collective-permute-start
  487.4 71.3 %collective-permute-start.2 = (bf16[512,1536]{1,0:T(8,128)(2,1)}, bf16[512,1536]{1,0:T(8,128)(2,1)}, u32[]{:S(2)}, u32[]{:S(2)}) collective-permute-start(bf16[512,1536]{1,0:T(8,128)(2,1)} %get-tuple-element.3964), channel_id=1, source_target_pairs={{1,0},{2,1},{3,2},{4,3},{5,4},{6,5},{7,6}} | collective-permute-start | bytes 4718600 | tf_op jit(solution)/shard_map/while/body/eval_jaxpr/ppermute | solution.py:813
  488.7 70.0 %copy-start = (f32[16,8,1536]{2,1,0:T(8,128)S(1)}, f32[16,8,1536]{2,1,0:T(8,128)}, u32[]{:S(2)}) copy-start(f32[16,8,1536]{2,1,0:T(8,128)} %get-tuple-element.3972) | copy-start | bytes 2359300 | tf_op jit(solution)/shard_map/while
  538.1 22.4 collective-permute-start.1
  560.5 71.3 %collective-permute-start.2 = (bf16[512,1536]{1,0:T(8,128)(2,1)}, bf16[512,1536]{1,0:T(8,128)(2,1)}, u32[]{:S(2)}, u32[]{:S(2)}) collective-permute-start(bf16[512,1536]{1,0:T(8,128)(2,1)} %get-tuple-element.3964), channel_id=1, source_target_pairs={{1,0},{2,1},{3,2},{4,3},{5,4},{6,5},{7,6}} | collective-permute-start | bytes 4718600 | tf_op jit(solution)/shard_map/while/body/eval_jaxpr/ppermute | solution.py:813
  561.8 70.0 %copy-start = (f32[16,8,1536]{2,1,0:T(8,128)S(1)}, f32[16,8,1536]{2,1,0:T(8,128)}, u32[]{:S(2)}) copy-start(f32[16,8,1536]{2,1,0:T(8,128)} %get-tuple-element.3972) | copy-start | bytes 2359300 | tf_op jit(solution)/shard_map/while
  611.2 22.4 collective-permute-start.1
  633.6 71.3 %collective-permute-start.2 = (bf16[512,1536]{1,0:T(8,128)(2,1)}, bf16[512,1536]{1,0:T(8,128)(2,1)}, u32[]{:S(2)}, u32[]{:S(2)}) collective-permute-start(bf16[512,1536]{1,0:T(8,128)(2,1)} %get-tuple-element.3964), channel_id=1, source_target_pairs={{1,0},{2,1},{3,2},{4,3},{5,4},{6,5},{7,6}} | collective-permute-start | bytes 4718600 | tf_op jit(solution)/shard_map/while/body/eval_jaxpr/ppermute | solution.py:813
  634.9 70.0 %copy-start = (f32[16,8,1536]{2,1,0:T(8,128)S(1)}, f32[16,8,1536]{2,1,0:T(8,128)}, u32[]{:S(2)}) copy-start(f32[16,8,1536]{2,1,0:T(8,128)} %get-tuple-element.3972) | copy-start | bytes 2359300 | tf_op jit(solution)/shard_map/while
  684.3 22.4 collective-permute-start.1
  706.7 71.3 %collective-permute-start.2 = (bf16[512,1536]{1,0:T(8,128)(2,1)}, bf16[512,1536]{1,0:T(8,128)(2,1)}, u32[]{:S(2)}, u32[]{:S(2)}) collective-permute-start(bf16[512,1536]{1,0:T(8,128)(2,1)} %get-tuple-element.3964), channel_id=1, source_target_pairs={{1,0},{2,1},{3,2},{4,3},{5,4},{6,5},{7,6}} | collective-permute-start | bytes 4718600 | tf_op jit(solution)/shard_map/while/body/eval_jaxpr/ppermute | solution.py:813
  708.0 70.0 %copy-start = (f32[16,8,1536]{2,1,0:T(8,128)S(1)}, f32[16,8,1536]{2,1,0:T(8,128)}, u32[]{:S(2)}) copy-start(f32[16,8,1536]{2,1,0:T(8,128)} %get-tuple-element.3972) | copy-start | bytes 2359300 | tf_op jit(solution)/shard_map/while
  757.5 22.4 collective-permute-start.1
  779.8 71.3 %collective-permute-start.2 = (bf16[512,1536]{1,0:T(8,128)(2,1)}, bf16[512,1536]{1,0:T(8,128)(2,1)}, u32[]{:S(2)}, u32[]{:S(2)}) collective-permute-start(bf16[512,1536]{1,0:T(8,128)(2,1)} %get-tuple-element.3964), channel_id=1, source_target_pairs={{1,0},{2,1},{3,2},{4,3},{5,4},{6,5},{7,6}} | collective-permute-start | bytes 4718600 | tf_op jit(solution)/shard_map/while/body/eval_jaxpr/ppermute | solution.py:813
  781.1 70.0 %copy-start = (f32[16,8,1536]{2,1,0:T(8,128)S(1)}, f32[16,8,1536]{2,1,0:T(8,128)}, u32[]{:S(2)}) copy-start(f32[16,8,1536]{2,1,0:T(8,128)} %get-tuple-element.3972) | copy-start | bytes 2359300 | tf_op jit(solution)/shard_map/while
  830.6 22.4 collective-permute-start.1
  853.0 71.3 %collective-permute-start.2 = (bf16[512,1536]{1,0:T(8,128)(2,1)}, bf16[512,1536]{1,0:T(8,128)(2,1)}, u32[]{:S(2)}, u32[]{:S(2)}) collective-permute-start(bf16[512,1536]{1,0:T(8,128)(2,1)} %get-tuple-element.3964), channel_id=1, source_target_pairs={{1,0},{2,1},{3,2},{4,3},{5,4},{6,5},{7,6}} | collective-permute-start | bytes 4718600 | tf_op jit(solution)/shard_map/while/body/eval_jaxpr/ppermute | solution.py:813
  854.3 70.0 %copy-start = (f32[16,8,1536]{2,1,0:T(8,128)S(1)}, f32[16,8,1536]{2,1,0:T(8,128)}, u32[]{:S(2)}) copy-start(f32[16,8,1536]{2,1,0:T(8,128)} %get-tuple-element.3972) | copy-start | bytes 2359300 | tf_op jit(solution)/shard_map/while
  903.7 22.4 collective-permute-start.1
  926.1 71.3 %collective-permute-start.2 = (bf16[512,1536]{1,0:T(8,128)(2,1)}, bf16[512,1536]{1,0:T(8,128)(2,1)}, u32[]{:S(2)}, u32[]{:S(2)}) collective-permute-start(bf16[512,1536]{1,0:T(8,128)(2,1)} %get-tuple-element.3964), channel_id=1, source_target_pairs={{1,0},{2,1},{3,2},{4,3},{5,4},{6,5},{7,6}} | collective-permute-start | bytes 4718600 | tf_op jit(solution)/shard_map/while/body/eval_jaxpr/ppermute | solution.py:813
  927.4 70.0 %copy-start = (f32[16,8,1536]{2,1,0:T(8,128)S(1)}, f32[16,8,1536]{2,1,0:T(8,128)}, u32[]{:S(2)}) copy-start(f32[16,8,1536]{2,1,0:T(8,128)} %get-tuple-element.3972) | copy-start | bytes 2359300 | tf_op jit(solution)/shard_map/while
  976.8 22.4 collective-permute-start.1
  999.2 336.2 %collective-permute-start.2 = (bf16[512,1536]{1,0:T(8,128)(2,1)}, bf16[512,1536]{1,0:T(8,128)(2,1)}, u32[]{:S(2)}, u32[]{:S(2)}) collective-permute-start(bf16[512,1536]{1,0:T(8,128)(2,1)} %get-tuple-element.3964), channel_id=1, source_target_pairs={{1,0},{2,1},{3,2},{4,3},{5,4},{6,5},{7,6}} | collective-permute-start | bytes 4718600 | tf_op jit(solution)/shard_map/while/body/eval_jaxpr/ppermute | solution.py:813
  1000.5 334.9 %copy-start = (f32[16,8,1536]{2,1,0:T(8,128)S(1)}, f32[16,8,1536]{2,1,0:T(8,128)}, u32[]{:S(2)}) copy-start(f32[16,8,1536]{2,1,0:T(8,128)} %get-tuple-element.3972) | copy-start | bytes 2359300 | tf_op jit(solution)/shard_map/while
  1049.9 346.5 %collective-permute-start.1 = (bf16[512,1536]{1,0:T(8,128)(2,1)}, bf16[512,1536]{1,0:T(8,128)(2,1)}, u32[]{:S(2)}, u32[]{:S(2)}) collective-permute-start(bf16[512,1536]{1,0:T(8,128)(2,1)} %get-tuple-element.4000), channel_id=1, source_target_pairs={{0,1},{1,2},{2,3},{3,4},{4,5},{5,6},{6,7}} | collective-permute-start | bytes 4718600 | tf_op jit(solution)/shard_map/while/body/eval_jaxpr/ppermute | solution.py:824
  1397.4 55.5 %collective-permute-start.2 = (bf16[512,1536]{1,0:T(8,128)(2,1)}, bf16[512,1536]{1,0:T(8,128)(2,1)}, u32[]{:S(2)}, u32[]{:S(2)}) collective-permute-start(bf16[512,1536]{1,0:T(8,128)(2,1)} %get-tuple-element.3964), channel_id=1, source_target_pairs={{1,0},{2,1},{3,2},{4,3},{5,4},{6,5},{7,6}} | collective-permute-start | bytes 4718600 | tf_op jit(solution)/shard_map/while/body/eval_jaxpr/ppermute | solution.py:813
  1398.7 54.2 %copy-start = (f32[16,8,1536]{2,1,0:T(8,128)S(1)}, f32[16,8,1536]{2,1,0:T(8,128)}, u32[]{:S(2)}) copy-start(f32[16,8,1536]{2,1,0:T(8,128)} %get-tuple-element.3972) | copy-start | bytes 2359300 | tf_op jit(solution)/shard_map/while
  1448.1 65.8 %collective-permute-start.1 = (bf16[512,1536]{1,0:T(8,128)(2,1)}, bf16[512,1536]{1,0:T(8,128)(2,1)}, u32[]{:S(2)}, u32[]{:S(2)}) collective-permute-start(bf16[512,1536]{1,0:T(8,128)(2,1)} %get-tuple-element.4000), channel_id=1, source_target_pairs={{0,1},{1,2},{2,3},{3,4},{4,5},{5,6},{6,7}} | collective-permute-start | bytes 4718600 | tf_op jit(solution)/shard_map/while/body/eval_jaxpr/ppermute | solution.py:824
  1514.8 55.6 %collective-permute-start.2 = (bf16[512,1536]{1,0:T(8,128)(2,1)}, bf16[512,1536]{1,0:T(8,128)(2,1)}, u32[]{:S(2)}, u32[]{:S(2)}) collective-permute-start(bf16[512,1536]{1,0:T(8,128)(2,1)} %get-tuple-element.3964), channel_id=1, source_target_pairs={{1,0},{2,1},{3,2},{4,3},{5,4},{6,5},{7,6}} | collective-permute-start | bytes 4718600 | tf_op jit(solution)/shard_map/while/body/eval_jaxpr/ppermute | solution.py:813
  1516.1 54.3 %copy-start = (f32[16,8,1536]{2,1,0:T(8,128)S(1)}, f32[16,8,1536]{2,1,0:T(8,128)}, u32[]{:S(2)}) copy-start(f32[16,8,1536]{2,1,0:T(8,128)} %get-tuple-element.3972) | copy-start | bytes 2359300 | tf_op jit(solution)/shard_map/while
  1552.3 79.1 %collective-permute-start.1 = (bf16[512,1536]{1,0:T(8,128)(2,1)}, bf16[512,1536]{1,0:T(8,128)(2,1)}, u32[]{:S(2)}, u32[]{:S(2)}) collective-permute-start(bf16[512,1536]{1,0:T(8,128)(2,1)} %get-tuple-element.4000), channel_id=1, source_target_pairs={{0,1},{1,2},{2,3},{3,4},{4,5},{5,6},{6,7}} | collective-permute-start | bytes 4718600 | tf_op jit(solution)/shard_map/while/body/eval_jaxpr/ppermute | solution.py:824
  1632.4 42.3 %collective-permute-start.2 = (bf16[512,1536]{1,0:T(8,128)(2,1)}, bf16[512,1536]{1,0:T(8,128)(2,1)}, u32[]{:S(2)}, u32[]{:S(2)}) collective-permute-start(bf16[512,1536]{1,0:T(8,128)(2,1)} %get-tuple-element.3964), channel_id=1, source_target_pairs={{1,0},{2,1},{3,2},{4,3},{5,4},{6,5},{7,6}} | collective-permute-start | bytes 4718600 | tf_op jit(solution)/shard_map/while/body/eval_jaxpr/ppermute | solution.py:813
  1633.7 41.1 %copy-start = (f32[16,8,1536]{2,1,0:T(8,128)S(1)}, f32[16,8,1536]{2,1,0:T(8,128)}, u32[]{:S(2)}) copy-start(f32[16,8,1536]{2,1,0:T(8,128)} %get-tuple-element.3972) | copy-start | bytes 2359300 | tf_op jit(solution)/shard_map/while
  1669.9 65.8 %collective-permute-start.1 = (bf16[512,1536]{1,0:T(8,128)(2,1)}, bf16[512,1536]{1,0:T(8,128)(2,1)}, u32[]{:S(2)}, u32[]{:S(2)}) collective-permute-start(bf16[512,1536]{1,0:T(8,128)(2,1)} %get-tuple-element.4000), channel_id=1, source_target_pairs={{0,1},{1,2},{2,3},{3,4},{4,5},{5,6},{6,7}} | collective-permute-start | bytes 4718600 | tf_op jit(solution)/shard_map/while/body/eval_jaxpr/ppermute | solution.py:824
  1736.6 55.6 %collective-permute-start.2 = (bf16[512,1536]{1,0:T(8,128)(2,1)}, bf16[512,1536]{1,0:T(8,128)(2,1)}, u32[]{:S(2)}, u32[]{:S(2)}) collective-permute-start(bf16[512,1536]{1,0:T(8,128)(2,1)} %get-tuple-element.3964), channel_id=1, source_target_pairs={{1,0},{2,1},{3,2},{4,3},{5,4},{6,5},{7,6}} | collective-permute-start | bytes 4718600 | tf_op jit(solution)/shard_map/while/body/eval_jaxpr/ppermute | solution.py:813
  1737.9 54.3 %copy-start = (f32[16,8,1536]{2,1,0:T(8,128)S(1)}, f32[16,8,1536]{2,1,0:T(8,128)}, u32[]{:S(2)}) copy-start(f32[16,8,1536]{2,1,0:T(8,128)} %get-tuple-element.3972) | copy-start | bytes 2359300 | tf_op jit(solution)/shard_map/while
  1786.1 67.2 %collective-permute-start.1 = (bf16[512,1536]{1,0:T(8,128)(2,1)}, bf16[512,1536]{1,0:T(8,128)(2,1)}, u32[]{:S(2)}, u32[]{:S(2)}) collective-permute-start(bf16[512,1536]{1,0:T(8,128)(2,1)} %get-tuple-element.4000), channel_id=1, source_target_pairs={{0,1},{1,2},{2,3},{3,4},{4,5},{5,6},{6,7}} | collective-permute-start | bytes 4718600 | tf_op jit(solution)/shard_map/while/body/eval_jaxpr/ppermute | solution.py:824
  1854.2 54.7 %collective-permute-start.2 = (bf16[512,1536]{1,0:T(8,128)(2,1)}, bf16[512,1536]{1,0:T(8,128)(2,1)}, u32[]{:S(2)}, u32[]{:S(2)}) collective-permute-start(bf16[512,1536]{1,0:T(8,128)(2,1)} %get-tuple-element.3964), channel_id=1, source_target_pairs={{1,0},{2,1},{3,2},{4,3},{5,4},{6,5},{7,6}} | collective-permute-start | bytes 4718600 | tf_op jit(solution)/shard_map/while/body/eval_jaxpr/ppermute | solution.py:813
  1855.5 53.4 %copy-start = (f32[16,8,1536]{2,1,0:T(8,128)S(1)}, f32[16,8,1536]{2,1,0:T(8,128)}, u32[]{:S(2)}) copy-start(f32[16,8,1536]{2,1,0:T(8,128)} %get-tuple-element.3972) | copy-start | bytes 2359300 | tf_op jit(solution)/shard_map/while
  1906.3 63.6 %collective-permute-start.1 = (bf16[512,1536]{1,0:T(8,128)(2,1)}, bf16[512,1536]{1,0:T(8,128)(2,1)}, u32[]{:S(2)}, u32[]{:S(2)}) collective-permute-start(bf16[512,1536]{1,0:T(8,128)(2,1)} %get-tuple-element.4000), channel_id=1, source_target_pairs={{0,1},{1,2},{2,3},{3,4},{4,5},{5,6},{6,7}} | collective-permute-start | bytes 4718600 | tf_op jit(solution)/shard_map/while/body/eval_jaxpr/ppermute | solution.py:824
  1970.8 58.0 %collective-permute-start.2 = (bf16[512,1536]{1,0:T(8,128)(2,1)}, bf16[512,1536]{1,0:T(8,128)(2,1)}, u32[]{:S(2)}, u32[]{:S(2)}) collective-permute-start(bf16[512,1536]{1,0:T(8,128)(2,1)} %get-tuple-element.3964), channel_id=1, source_target_pairs={{1,0},{2,1},{3,2},{4,3},{5,4},{6,5},{7,6}} | collective-permute-start | bytes 4718600 | tf_op jit(solution)/shard_map/while/body/eval_jaxpr/ppermute | solution.py:813
  1972.1 56.7 %copy-start = (f32[16,8,1536]{2,1,0:T(8,128)S(1)}, f32[16,8,1536]{2,1,0:T(8,128)}, u32[]{:S(2)}) copy-start(f32[16,8,1536]{2,1,0:T(8,128)} %get-tuple-element.3972) | copy-start | bytes 2359300 | tf_op jit(solution)/shard_map/while
  2023.0 66.8 %collective-permute-start.1 = (bf16[512,1536]{1,0:T(8,128)(2,1)}, bf16[512,1536]{1,0:T(8,128)(2,1)}, u32[]{:S(2)}, u32[]{:S(2)}) collective-permute-start(bf16[512,1536]{1,0:T(8,128)(2,1)} %get-tuple-element.4000), channel_id=1, source_target_pairs={{0,1},{1,2},{2,3},{3,4},{4,5},{5,6},{6,7}} | collective-permute-start | bytes 4718600 | tf_op jit(solution)/shard_map/while/body/eval_jaxpr/ppermute | solution.py:824
  2090.7 56.5 %collective-permute-start.2 = (bf16[512,1536]{1,0:T(8,128)(2,1)}, bf16[512,1536]{1,0:T(8,128)(2,1)}, u32[]{:S(2)}, u32[]{:S(2)}) collective-permute-start(bf16[512,1536]{1,0:T(8,128)(2,1)} %get-tuple-element.3964), channel_id=1, source_target_pairs={{1,0},{2,1},{3,2},{4,3},{5,4},{6,5},{7,6}} | collective-permute-start | bytes 4718600 | tf_op jit(solution)/shard_map/while/body/eval_jaxpr/ppermute | solution.py:813
  2092.0 55.2 %copy-start = (f32[16,8,1536]{2,1,0:T(8,128)S(1)}, f32[16,8,1536]{2,1,0:T(8,128)}, u32[]{:S(2)}) copy-start(f32[16,8,1536]{2,1,0:T(8,128)} %get-tuple-element.3972) | copy-start | bytes 2359300 | tf_op jit(solution)/shard_map/while
  2142.9 65.4 %collective-permute-start.1 = (bf16[512,1536]{1,0:T(8,128)(2,1)}, bf16[512,1536]{1,0:T(8,128)(2,1)}, u32[]{:S(2)}, u32[]{:S(2)}) collective-permute-start(bf16[512,1536]{1,0:T(8,128)(2,1)} %get-tuple-element.4000), channel_id=1, source_target_pairs={{0,1},{1,2},{2,3},{3,4},{4,5},{5,6},{6,7}} | collective-permute-start | bytes 4718600 | tf_op jit(solution)/shard_map/while/body/eval_jaxpr/ppermute | solution.py:824
  2209.2 56.4 %collective-permute-start.2 = (bf16[512,1536]{1,0:T(8,128)(2,1)}, bf16[512,1536]{1,0:T(8,128)(2,1)}, u32[]{:S(2)}, u32[]{:S(2)}) collective-permute-start(bf16[512,1536]{1,0:T(8,128)(2,1)} %get-tuple-element.3964), channel_id=1, source_target_pairs={{1,0},{2,1},{3,2},{4,3},{5,4},{6,5},{7,6}} | collective-permute-start | bytes 4718600 | tf_op jit(solution)/shard_map/while/body/eval_jaxpr/ppermute | solution.py:813
  2210.5 55.1 %copy-start = (f32[16,8,1536]{2,1,0:T(8,128)S(1)}, f32[16,8,1536]{2,1,0:T(8,128)}, u32[]{:S(2)}) copy-start(f32[16,8,1536]{2,1,0:T(8,128)} %get-tuple-element.3972) | copy-start | bytes 2359300 | tf_op jit(solution)/shard_map/while
  2261.4 65.3 %collective-permute-start.1 = (bf16[512,1536]{1,0:T(8,128)(2,1)}, bf16[512,1536]{1,0:T(8,128)(2,1)}, u32[]{:S(2)}, u32[]{:S(2)}) collective-permute-start(bf16[512,1536]{1,0:T(8,128)(2,1)} %get-tuple-element.4000), channel_id=1, source_target_pairs={{0,1},{1,2},{2,3},{3,4},{4,5},{5,6},{6,7}} | collective-permute-start | bytes 4718600 | tf_op jit(solution)/shard_map/while/body/eval_jaxpr/ppermute | solution.py:824
  2340.2 996.6 %all-reduce.5.cloned.1.call-start = ((), (), s32[]{:S(2)}) async-start(), calls=%async_computation.1 | async-start | bytes 50331648 | tf_op jit(solution)/shard_map/psum | solution.py:849
  2341.2 5.2 collective-permute-start.3
  2407.6 40.8 %collective-permute-start.3 = (bf16[512,1536]{1,0:T(8,128)(2,1)}, bf16[512,1536]{1,0:T(8,128)(2,1)}, u32[]{:S(2)}, u32[]{:S(2)}) collective-permute-start(bf16[512,1536]{1,0:T(8,128)(2,1)} %get-tuple-element.4082), channel_id=1, source_target_pairs={{1,0},{2,1},{3,2},{4,3},{5,4},{6,5},{7,6}} | collective-permute-start | bytes 4718600 | tf_op jit(solution)/shard_map/while/body/eval_jaxpr/ppermute | solution.py:830
  2509.5 36.7 %collective-permute-start.3 = (bf16[512,1536]{1,0:T(8,128)(2,1)}, bf16[512,1536]{1,0:T(8,128)(2,1)}, u32[]{:S(2)}, u32[]{:S(2)}) collective-permute-start(bf16[512,1536]{1,0:T(8,128)(2,1)} %get-tuple-element.4082), channel_id=1, source_target_pairs={{1,0},{2,1},{3,2},{4,3},{5,4},{6,5},{7,6}} | collective-permute-start | bytes 4718600 | tf_op jit(solution)/shard_map/while/body/eval_jaxpr/ppermute | solution.py:830
  2607.5 39.3 %collective-permute-start.3 = (bf16[512,1536]{1,0:T(8,128)(2,1)}, bf16[512,1536]{1,0:T(8,128)(2,1)}, u32[]{:S(2)}, u32[]{:S(2)}) collective-permute-start(bf16[512,1536]{1,0:T(8,128)(2,1)} %get-tuple-element.4082), channel_id=1, source_target_pairs={{1,0},{2,1},{3,2},{4,3},{5,4},{6,5},{7,6}} | collective-permute-start | bytes 4718600 | tf_op jit(solution)/shard_map/while/body/eval_jaxpr/ppermute | solution.py:830
  2707.8 54.9 %collective-permute-start.3 = (bf16[512,1536]{1,0:T(8,128)(2,1)}, bf16[512,1536]{1,0:T(8,128)(2,1)}, u32[]{:S(2)}, u32[]{:S(2)}) collective-permute-start(bf16[512,1536]{1,0:T(8,128)(2,1)} %get-tuple-element.4082), channel_id=1, source_target_pairs={{1,0},{2,1},{3,2},{4,3},{5,4},{6,5},{7,6}} | collective-permute-start | bytes 4718600 | tf_op jit(solution)/shard_map/while/body/eval_jaxpr/ppermute | solution.py:830
  2823.8 21.4 collective-permute-start.3
  2906.3 21.3 collective-permute-start.3
  (22 other events, 52.0 us)
Sparse Core Ops, SparseCore 0:
  2340.3 364.8 all-reduce.2
  2989.2 347.5 all-reduce.4
